TPU v7x, 32 devices: a whole 2x2x4 slice. The times are simulated.
32 devices in a mesh: ta: 4 (over y, x), gz: 2 (over core), xy: 4 (over z).
Axes of the slice: x: 2, y: 2, z: 4, core: 2. Of those that a mesh axis runs over, the one named last changes fastest.
Arguments:
- source_field: float32 [2, 4, 3, 4, 2, 4, 128], P(None, None, None, 'ta', 'gz', 'xy'), may hold values from -6 to 6
- gauge_links: float32 [2, 8, 3, 3, 4, 2, 4, 128], P(None, None, None, None, 'ta', 'gz', 'xy'), may hold values from -2.5 to 2.5
- fine_vectors: bfloat16 [2, 24, 4, 3, 4, 2, 4, 128], P(None, None, None, None, 'ta', 'gz', 'xy'), may hold values from -1.75 to 1.75
- middle_blocks: float32 [2, 9, 24, 4, 2, 4, 768], P(None, None, None, 'ta', 'gz', 'xy'), may hold values from -0.3125 to 0.3125
- middle_vectors: float32 [2, 24, 4, 2, 4, 768], P(None, None, 'ta', 'gz', 'xy'), may hold values from -0.625 to 0.625
- bottom_blocks: float32 [2, 7, 4, 2, 2304], P(None, None, 'ta', 'gz'), may hold values from -4 to 4
Outputs:
- solution: float32 [2, 4, 3, 4, 2, 4, 128], P(None, None, None, 'ta', 'gz', 'xy')
- smoothed_residual: float32 [2, 4, 3, 4, 2, 4, 128], P(None, None, None, 'ta', 'gz', 'xy')
All inputs are finite; a program needn't handle non-finite values.
Results may differ from a plain program's by a relative error of at most 0.0034.
Values sent between devices are 32-bit elements; how exact they have to be, the bound alone decides.
No kernel may reach another device: no remote copies, remote signals or barrier semaphores. Data moves between devices by JAX's collectives and lax.ppermute only.
A program may use at most 64 MiB of HBM per device.

v0:
```python
import functools
import math

import jax
import jax.numpy as jnp
import numpy as np
from jax import lax
from jax.experimental import pallas as pl
from jax.experimental.pallas import tpu as pltpu
from jax.sharding import PartitionSpec as P

BY = 4
NVEC = 24
NVEC2 = 24
SPINOR = 24
HALF = 12
LANES = 128
SUB = 8

quark_mass = 0.1
twist_mass = 0.1
fine_damping = 0.8
middle_damping = 0.4
middle_shift = 2.0
bottom_shift = 2.0
gamma = np.array(
    [
        [[0, 0, 1, 0], [0, 0, 0, 1], [1, 0, 0, 0], [0, 1, 0, 0]],
        [[0, 0, 1j, 0], [0, 0, 0, -1j], [-1j, 0, 0, 0], [0, 1j, 0, 0]],
        [[0, 0, 0, 1j], [0, 0, 1j, 0], [0, -1j, 0, 0], [-1j, 0, 0, 0]],
        [[0, 0, 0, -1], [0, 0, 1, 0], [0, 1, 0, 0], [-1, 0, 0, 0]],
    ],
    np.complex64,
)
chirality = np.array([1.0, 1.0, -1.0, -1.0])
HIGHEST = lax.Precision.HIGHEST
F32 = jnp.float32
BF16 = jnp.bfloat16


def real_form(matrix):
    return np.block([[matrix.real, -matrix.imag], [matrix.imag, matrix.real]])


def fine_tables():
    color = np.eye(3)
    project = np.zeros((2, 2, 3, 8, 8, SPINOR))
    rebuild = np.zeros((SPINOR, 2, 2, 3, 8))
    for m in range(4):
        for back in range(2):
            sign = -1.0 if back else 1.0
            way = 2 * m + back
            upper = np.eye(4)[:2] - sign * gamma[m][:2]
            project[:, :, :, way, way] = real_form(np.kron(upper, color)).reshape(2, 2, 3, SPINOR)
            lower = np.concatenate([np.eye(2), -sign * gamma[m][2:, :2]])
            rebuild[..., way] = real_form(np.kron(lower, color)).reshape(SPINOR, 2, 2, 3)
    project = project.reshape(HALF * 8, 8 * SPINOR)
    rebuild = rebuild.reshape(SPINOR, HALF * 8)
    mass = 4.0 + quark_mass
    twist = np.kron(np.diag(mass + 1j * twist_mass * chirality), color)
    diagonal = real_form(twist)
    inverse = real_form(np.linalg.inv(twist))
    first = project @ np.kron(np.eye(8), fine_damping * inverse)
    second = np.concatenate(
        [
            0.5 * fine_damping * inverse @ rebuild,
            fine_damping * (2.0 - fine_damping) * inverse,
        ],
        axis=1,
    )
    third = np.concatenate([0.5 * rebuild, -diagonal, np.eye(SPINOR)], axis=1)
    return [np.asarray(t, np.float32) for t in (first, second, project, third)]


def pairings(n):
    if n % 2:
        return [[((i + 1) % n, i) for i in range(n)], [(i, (i + 1) % n) for i in range(n)]]
    near = [(i, i ^ 1) for i in range(n)]
    far = [(i, (i + 1) % n if i % 2 else (i - 1) % n) for i in range(n)]
    return [near] if n == 2 else [near, far]


def neighbours(array, axes):
    found = []
    for axis in axes:
        pairs = pairings(lax.axis_size(axis))
        found.append([lax.ppermute(array, axis, p) for p in pairs])
    return found


def side_step(axis, which):
    n = lax.axis_size(axis)
    ahead = 1 if which == 0 else -1
    if n % 2:
        return ahead
    return ahead * (1 - 2 * (lax.axis_index(axis) % 2))


def ahead_behind(pair, axis):
    if len(pair) == 1:
        return pair[0], pair[0]
    n = lax.axis_size(axis)
    if n % 2:
        return pair[0], pair[1]
    even = lax.axis_index(axis) % 2 == 0
    return jnp.where(even, pair[0], pair[1]), jnp.where(even, pair[1], pair[0])


def dot(a, b):
    return jnp.dot(a, b, precision=HIGHEST, preferred_element_type=F32)


def dot_nt(a, b, precision=HIGHEST):
    return lax.dot_general(
        a, b, (((1,), (1,)), ((), ())), precision=precision, preferred_element_type=F32
    )


def parts(x):
    high = x.astype(BF16)
    rest = x - high.astype(F32)
    middle = rest.astype(BF16)
    low = (rest - middle.astype(F32)).astype(BF16)
    return high, middle, low


def iota(shape, dim):
    return lax.broadcasted_iota(jnp.int32, shape, dim)


def one_hot(condition, dtype=F32):
    return jnp.where(condition, 1.0, 0.0).astype(dtype)


def hopping(spinor, halos, gauge, project, axes):
    seen = []
    for pair, axis in zip(halos, axes):
        seen.extend(ahead_behind(pair, axis))
    seen.append(pltpu.roll(spinor, LANES - 1, 1))
    seen.append(pltpu.roll(spinor, 1, 1))
    half = dot(project, jnp.concatenate(seen, axis=0))
    rows = [[[None] * 3 for _ in range(2)] for _ in range(2)]
    for a in range(3):
        for b in range(3):
            link = [gauge[pl.ds(p * 72 + a * 3 + b, 8, stride=9), :] for p in range(2)]
            for s in range(2):
                re = half[(s * 3 + b) * 8 : (s * 3 + b) * 8 + 8]
                im = half[(6 + s * 3 + b) * 8 : (6 + s * 3 + b) * 8 + 8]
                out_re = link[0] * re - link[1] * im
                out_im = link[0] * im + link[1] * re
                for p, value in ((0, out_re), (1, out_im)):
                    old = rows[p][s][a]
                    rows[p][s][a] = value if old is None else old + value
    return [rows[p][s][a] for p in range(2) for s in range(2) for a in range(3)]


def first_kernel(counts, axes, *refs):
    source, refs = refs[0], refs[1:]
    halos, at = [], 0
    for count in counts:
        halos.append([r[...] for r in refs[at : at + count]])
        at += count
    gauge, vectors, project, table, out = refs[at:]
    value = source[...]
    rows = hopping(value, halos, gauge, project[...], axes)
    out[:SPINOR] = dot(table[...], jnp.concatenate(rows + [value], axis=0))
    out[SPINOR:] = vectors[...]


def strided_vectors(fine, i):
    row = (i % 3) * 4 + i // 3
    return [fine[pl.ds(p * NVEC * HALF + row, NVEC, stride=HALF), :] for p in range(2)]


def second_kernel(counts, axes, blocks, place, dests, *refs):
    source, own, refs = refs[0], refs[1], refs[2:]
    halos, at = [], 0
    for count in counts:
        halos.append([r[...] for r in refs[at : at + count]])
        at += count
    gauge, fine, vectors, project, table, out, middle, sent, wide = refs[at:]
    spinor = own[...]
    rows = hopping(spinor, halos, gauge, project[...], axes)
    residual = dot(table[...], jnp.concatenate(rows + [spinor, source[...]], axis=0))
    out[...] = residual
    low = residual.astype(BF16).astype(F32)
    wide[...] = fine[...].astype(F32)
    sum_re = jnp.zeros((NVEC, LANES), F32)
    sum_im = jnp.zeros((NVEC, LANES), F32)
    for i in range(HALF):
        re, im = strided_vectors(wide, i)
        low_re, low_im = low[i : i + 1], low[HALF + i : HALF + i + 1]
        sum_re = sum_re + re * low_re + im * low_im
        sum_im = sum_im + re * low_im - im * low_re
    group = iota((LANES, LANES), 1) % blocks == iota((LANES, LANES), 0) // BY
    right = dot(jnp.concatenate([sum_re, sum_im], axis=0), one_hot(group))
    middle[...] = right
    per = LANES // blocks
    count = NVEC // per
    keep = iota((NVEC, LANES), 1) // blocks == iota((NVEC, LANES), 0) % per
    pick = one_hot(iota((NVEC, NVEC), 1) // per == iota((NVEC, NVEC), 0) % count)
    kept = [jnp.where(keep, right[p * NVEC : (p + 1) * NVEC], 0.0) for p in range(2)]
    pattern = dot(pick, jnp.concatenate(kept, axis=1))
    pat_re, pat_im = pattern[:, :LANES], pattern[:, LANES:]
    size = NVEC2 * count
    made_re, made_im = [], []
    for block in range(size // NVEC):
        re = vectors[pl.ds(block * NVEC, NVEC), :]
        im = vectors[pl.ds(size + block * NVEC, NVEC), :]
        made_re.append(re * pat_re + im * pat_im)
        made_im.append(re * pat_im - im * pat_re)
    ones = jnp.ones((SUB, LANES), F32)
    shift = lax.axis_index("xy") * NVEC2 if place else 0
    scatter = one_hot(iota((size, LANES), 1) == iota((size, LANES), 0) // count + shift)
    line = [
        dot(dot_nt(ones, jnp.concatenate(made, axis=0)), scatter) for made in (made_re, made_im)
    ]
    both = jnp.where(iota((SUB, LANES), 0) % 2 == 0, line[0], line[1])
    for i in range(2 * dests // SUB):
        sent[i * SUB : (i + 1) * SUB] = both


def swap_pairs(x):
    return jnp.where(iota(x.shape, 0) % 2 == 0, pltpu.roll(x, SUB - 1, 0), pltpu.roll(x, 1, 0))


def bottom_apply(v, near, image, spread, gather, held, stride, nz, width):
    lane = iota(v.shape, 1)
    edge = width - NVEC2
    up = jnp.where(lane < edge, pltpu.roll(v, LANES - NVEC2, 1), pltpu.roll(v, edge, 1))
    down = jnp.where(lane >= NVEC2, pltpu.roll(v, NVEC2, 1), pltpu.roll(v, LANES - edge, 1))
    rows = jnp.concatenate([v, jnp.where(lane < width, up, 0.0), down], axis=0)
    total = None
    for part in parts(rows):
        term = jnp.dot(part, spread[...], preferred_element_type=F32)
        total = term if total is None else total + term
    near[...] = total
    chunks = near.shape[1] // LANES
    for c in range(chunks):
        here = pl.ds(c * LANES, LANES)
        own = [near[q * SUB : (q + 1) * SUB, here] for q in range(2)]
        side = [
            [near[(2 * d + q) * SUB : (2 * d + q + 1) * SUB, here] for q in range(2)]
            for d in (1, 2)
        ]
        stack = [
            (0, own),
            (1, [pltpu.roll(x, SUB - nz, 0) for x in own]),
            (2, [pltpu.roll(x, nz, 0) for x in own]),
            (3, [swap_pairs(x) for x in own]),
            (5, side[0]),
            (6, side[1]),
        ]
        acc_re = acc_im = None
        for d, (re, im) in stack:
            block = [held[pl.ds((p * 7 + d) * chunks + c, SUB, stride=stride), :] for p in range(2)]
            if d == 3:
                block = [
                    block[p] + held[pl.ds((p * 7 + 4) * chunks + c, SUB, stride=stride), :]
                    for p in range(2)
                ]
            got_re = block[0] * re - block[1] * im
            got_im = block[0] * im + block[1] * re
            acc_re = got_re if acc_re is None else acc_re + got_re
            acc_im = got_im if acc_im is None else acc_im + got_im
        image[:SUB, here] = acc_re
        image[SUB:, here] = acc_im
    total = bottom_shift * v
    for part in parts(image[...]):
        total = total + dot_nt(part, gather[...], None)
    return total


def whole_sum(x):
    return jnp.sum(jnp.sum(x, axis=1, keepdims=True), axis=0, keepdims=True)


def minimal_residual(r, f, s):
    r_re, r_im, f_re, f_im, s_re, s_im = r[:SUB], r[SUB:], f[:SUB], f[SUB:], s[:SUB], s[SUB:]
    ff = whole_sum(f_re * f_re + f_im * f_im)
    ss = whole_sum(s_re * s_re + s_im * s_im)
    cross_re = whole_sum(f_re * s_re + f_im * s_im)
    cross_im = whole_sum(f_re * s_im - f_im * s_re)
    one_re = whole_sum(f_re * r_re + f_im * r_im)
    one_im = whole_sum(f_re * r_im - f_im * r_re)
    two_re = whole_sum(s_re * r_re + s_im * r_im)
    two_im = whole_sum(s_re * r_im - s_im * r_re)
    determinant = ff * ss - cross_re * cross_re - cross_im * cross_im
    a_re = (ss * one_re - (cross_re * two_re - cross_im * two_im)) / determinant
    a_im = (ss * one_im - (cross_re * two_im + cross_im * two_re)) / determinant
    b_re = (ff * two_re - (cross_re * one_re + cross_im * one_im)) / determinant
    b_im = (ff * two_im - (cross_re * one_im - cross_im * one_re)) / determinant
    return jnp.concatenate(
        [
            a_re * r_re - a_im * r_im + b_re * f_re - b_im * f_im,
            a_re * r_im + a_im * r_re + b_re * f_im + b_im * f_re,
        ],
        axis=0,
    )


def bottom_rows(sites, shape, solution):
    nt, nz, nx = shape
    here = [lax.axis_index(a) for a in ("ta", "gz", "xy")]
    row, col = iota((2 * SUB, 2 * SUB), 0), iota((2 * SUB, 2 * SUB), 1)
    site = row // 2
    lines = jnp.full((2 * SUB, 2 * SUB), here[0] * nz + here[1], jnp.int32)
    turns = {0: [], 1: [], -1: []}
    at = 1
    side_rows = []
    for number, (axis, count) in enumerate(zip(("ta", "gz", "xy"), sites)):
        for which in range(count):
            step = side_step(axis, which)
            if number == 0:
                line = lax.rem(here[0] + step + nt, nt) * nz + here[1]
                lines = jnp.where(site == at, line, lines)
            elif number == 1:
                line = here[0] * nz + lax.rem(here[1] + step + nz, nz)
                lines = jnp.where(site == at, line, lines)
            else:
                side_rows.append((at, lax.rem(here[2] + step + nx, nx)))
            at += 1
    pick = one_hot((col % SUB == lines) & (col // SUB == row % 2))
    rows = dot(pick, solution)

    def turned(x):
        return pltpu.roll(rows, lax.rem(LANES - NVEC2 * x, LANES), 1)

    result = turned(here[2])
    for n, x in side_rows:
        result = jnp.where(iota(result.shape, 0) // 2 == n, turned(x), result)
    return jnp.where(iota(result.shape, 1) < NVEC2, result, 0.0)


def middle_step(counts, axes, blocks, rows, vectors, middle, read_block, fine, spinor, out, wide):
    per = LANES // blocks
    count = NVEC // per
    size = NVEC2 * count
    spread = one_hot(
        (iota((LANES, 2 * LANES), 0) == iota((LANES, 2 * LANES), 1) // count)
        & (iota((LANES, 2 * LANES), 1) < size),
        BF16,
    )
    coefs = None
    for part in parts(rows):
        term = jnp.dot(part, spread, preferred_element_type=F32)
        coefs = term if coefs is None else coefs + term
    same = iota((NVEC, size), 1) % count == iota((NVEC, size), 0) % count
    guesses = []
    for n, ref in enumerate(vectors):
        skip = ref.shape[0] - 2 * size
        wide_vectors = jnp.concatenate(
            [ref[skip : skip + size], ref[skip + size : skip + 2 * size]], axis=1
        )
        left = jnp.concatenate(
            [jnp.where(same, coefs[2 * n + q : 2 * n + q + 1, :size], 0.0) for q in range(2)],
            axis=0,
        )
        made = dot(left, wide_vectors)
        guesses.append(
            jnp.concatenate(
                [
                    made[:NVEC, :LANES] - made[NVEC:, LANES:],
                    made[:NVEC, LANES:] + made[NVEC:, :LANES],
                ],
                axis=0,
            )
        )
    own = guesses[0]
    near = [own]
    at = 1
    for c, axis in zip(counts, axes):
        near.extend(ahead_behind(guesses[at : at + c], axis))
        at += c
    aggregate = iota(own.shape, 1) % blocks
    near.append(
        jnp.where(
            aggregate == blocks - 1, pltpu.roll(own, blocks - 1, 1), pltpu.roll(own, LANES - 1, 1)
        )
    )
    near.append(
        jnp.where(aggregate == 0, pltpu.roll(own, LANES - blocks + 1, 1), pltpu.roll(own, 1, 1))
    )
    made_re, made_im = [], []
    for block in range(size // NVEC):
        acc_re = acc_im = None
        for d, value in enumerate(near):
            re, im = value[:NVEC], value[NVEC:]
            m_re, m_im = [read_block(p, d, block) for p in range(2)]
            got_re = m_re * re - m_im * im
            got_im = m_re * im + m_im * re
            acc_re = got_re if acc_re is None else acc_re + got_re
            acc_im = got_im if acc_im is None else acc_im + got_im
        row = iota((NVEC, LANES), 0) + block * NVEC
        at_home = (row % count) * per + iota((NVEC, LANES), 1) // blocks == row // count
        keep = 1.0 - middle_damping * middle_shift
        made_re.append(jnp.where(at_home, keep * own[:NVEC], 0.0) - middle_damping * acc_re)
        made_im.append(jnp.where(at_home, keep * own[NVEC:], 0.0) - middle_damping * acc_im)
    made = jnp.concatenate(
        [jnp.concatenate(made_re, axis=0), jnp.concatenate(made_im, axis=0)], axis=1
    )
    row_sum = one_hot(iota((NVEC, size), 1) // count == iota((NVEC, size), 0))
    summed = dot(row_sum, made)
    summed = jnp.concatenate([summed[:, :LANES], summed[:, LANES:]], axis=0)
    lane_sum = one_hot(
        iota((LANES, LANES), 0) % blocks == iota((LANES, LANES), 1) % blocks
    )
    update = dot(summed, lane_sum) + middle_damping * middle[...]
    lift = one_hot(iota((LANES, LANES), 0) == iota((LANES, LANES), 1) // BY, BF16)
    lifted = jnp.dot(update.astype(BF16), lift, preferred_element_type=F32)
    u_re, u_im = lifted[:NVEC], lifted[NVEC:]
    wide[...] = fine[...].astype(F32)
    sum_re, sum_im = [], []
    for i in range(HALF):
        re, im = strided_vectors(wide, i)
        sum_re.append(jnp.sum(re * u_re - im * u_im, axis=0, keepdims=True))
        sum_im.append(jnp.sum(re * u_im + im * u_re, axis=0, keepdims=True))
    out[...] = spinor[...] + jnp.concatenate(sum_re + sum_im, axis=0)


def third_kernel(counts, axes, blocks, shape, received, *refs):
    n_sites = 1 + sum(counts)
    held_in, refs = refs[:4], refs[4:]
    spread_in, gather_in, matrix_in, refs = refs[0], refs[1], refs[2], refs[3:]
    vectors, refs = refs[:n_sites], refs[n_sites:]
    middle, fine, spinor, out = refs[:4]
    held, spread, gather, matrix, near, image, wide, sems = refs[4:]
    nt, nz, nx = shape
    stride = held.shape[0] // SUB
    depth = held_in[0].shape[0] // 2
    ta, gz = lax.axis_index("ta"), lax.axis_index("gz")
    copies = []
    for i, ref in enumerate(held_in):
        for h in range(2):
            line = (ta ^ (2 * (i % 2) + h)) * nz + (gz ^ (i // 2))
            target = held.at[pl.ds(pl.multiple_of(line * stride, SUB), depth)]
            copies.append(
                pltpu.make_async_copy(ref.at[pl.ds(h * depth, depth)], target, sems.at[2 * i + h])
            )
    copies.append(pltpu.make_async_copy(spread_in, spread, sems.at[8]))
    copies.append(pltpu.make_async_copy(gather_in, gather, sems.at[9]))
    matrix_copy = pltpu.make_async_copy(matrix_in, matrix, sems.at[10])
    for copy in copies:
        copy.start()
    matrix_copy.start()
    total = received.shape[0]
    row, col = iota((2 * SUB, total), 0), iota((2 * SUB, total), 1)
    fold = one_hot((col // (2 * nx) == row % SUB) & (col % 2 == row // SUB))
    r = dot(fold, received[...])
    for copy in copies:
        copy.wait()
    apply = functools.partial(
        bottom_apply,
        near=near,
        image=image,
        spread=spread,
        gather=gather,
        held=held,
        stride=stride,
        nz=nz,
        width=nx * NVEC2,
    )
    f = apply(r)
    s = apply(f)
    rows = bottom_rows(counts, shape, minimal_residual(r, f, s))
    matrix_copy.wait()
    size = NVEC * NVEC * blocks // LANES

    def read_block(p, d, block):
        return matrix[pl.ds((p * 9 + d) * size + block * NVEC, NVEC), :]

    middle_step(
        counts, axes, blocks, rows, vectors, middle, read_block, fine, spinor, out, wide
    )


def fourth_kernel(counts, axes, blocks, rows, *refs):
    n_sites = 1 + sum(counts)
    matrix, refs = refs[0], refs[1:]
    vectors, refs = refs[:n_sites], refs[n_sites:]
    middle, fine, spinor, out, wide = refs
    size = NVEC * NVEC * blocks // LANES

    def read_block(p, d, block):
        return matrix[pl.ds((p * 9 + d) * size + block * NVEC, NVEC), :]

    middle_step(
        counts, axes, blocks, rows[...], vectors, middle, read_block, fine, spinor, out, wide
    )


def vmem():
    return pl.BlockSpec(memory_space=pltpu.VMEM)


def anywhere():
    return pl.BlockSpec(memory_space=pl.ANY)


def top(rows):
    return pl.BlockSpec((rows, LANES), lambda i: (0, 0))


def shape_of(*dims):
    return jax.ShapeDtypeStruct(dims, F32)


def params(mib):
    return pltpu.CompilerParams(vmem_limit_bytes=mib * 2**20)


def line_solve(right, bottom_blocks):
    split = bottom_blocks.reshape((2, 7, -1, NVEC2, NVEC2))
    line = lax.all_gather(right, "xy", axis=1, tiled=False)

    def moved(v, axis, step):
        n = lax.axis_size(axis)
        return lax.ppermute(v, axis, [((i + step) % n, i) for i in range(n)])

    def product(blocks, v):
        return jnp.einsum("dxjk,dxk->xj", blocks, v, precision=HIGHEST)

    def apply(v):
        near = [v, moved(v, "ta", 1), moved(v, "ta", -1), moved(v, "gz", 1), moved(v, "gz", -1)]
        near = jnp.stack(near + [jnp.roll(v, -1, 1), jnp.roll(v, 1, 1)], axis=1)
        re = product(split[0], near[0]) - product(split[1], near[1])
        im = product(split[0], near[1]) + product(split[1], near[0])
        return bottom_shift * v + jnp.stack([re, im])

    first = apply(line)
    second = apply(first)

    def inner(u, w):
        return [jnp.sum(u[0] * w[0] + u[1] * w[1]), jnp.sum(u[0] * w[1] - u[1] * w[0])]

    sums = inner(first, first)[:1] + inner(second, second)[:1] + inner(first, second)
    sums = sums + inner(first, line) + inner(second, line)
    ff, ss, cr, ci, pr, pi, qr, qi = lax.psum(jnp.stack(sums), ("ta", "gz"))
    det = ff * ss - cr * cr - ci * ci
    a_re = (ss * pr - (cr * qr - ci * qi)) / det
    a_im = (ss * pi - (cr * qi + ci * qr)) / det
    b_re = (ff * qr - (cr * pr + ci * pi)) / det
    b_im = (ff * qi - (cr * pi - ci * pr)) / det

    def scaled(re, im, v):
        return jnp.stack([re * v[0] - im * v[1], re * v[1] + im * v[0]])

    solved = scaled(a_re, a_im, line) + scaled(b_re, b_im, first)
    return lax.dynamic_index_in_dim(solved, lax.axis_index("xy"), 1, keepdims=False)


def shards(source_field, gauge_links, fine_vectors, middle_blocks, middle_vectors, bottom_blocks):
    axes = ("ta", "gz", "xy")
    shape = tuple(lax.axis_size(a) for a in axes)
    nt, nz, nx = shape
    devices = nt * nz * nx
    blocks = source_field.shape[-1] // BY
    source = source_field.reshape(SPINOR, LANES)
    gauge = gauge_links.reshape(-1, LANES)
    fine = jnp.transpose(fine_vectors, (0, 1, 3, 4, 5, 6, 2, 7)).reshape(-1, LANES)
    matrix = middle_blocks.reshape(-1, LANES)
    vectors = middle_vectors.reshape(-1, LANES)
    size = vectors.shape[0]
    first, second, project, third = fine_tables()
    counts = [len(pairings(n)) for n in shape]
    gathered = nt == 4 and nz == 2 and nx * NVEC2 <= LANES

    halos = neighbours(source, axes)
    flat = [a for pair in halos for a in pair]
    if gathered:
        per_line = bottom_blocks.shape[-1] * 14 // LANES
        depth = -(-per_line // SUB) * SUB
        line = jnp.pad(bottom_blocks.reshape(per_line, LANES), ((0, depth - per_line), (0, 0)))
        pair = jnp.concatenate([line, lax.ppermute(line, "ta", [(i, i ^ 1) for i in range(nt)])])
    payload = pl.pallas_call(
        functools.partial(first_kernel, counts, axes),
        out_shape=shape_of(SPINOR + size, LANES),
        in_specs=[vmem()] * (len(flat) + 5),
        out_specs=vmem(),
        compiler_params=params(8),
    )(source, *flat, gauge, vectors, first, second)

    near = neighbours(payload, axes)
    flat_near = [a for pair in near for a in pair]
    if gathered:
        other = lax.ppermute(pair, "ta", [(i, i ^ 2) for i in range(nt)])
        swap = [(i, i ^ 1) for i in range(nz)]
        held = [pair, other, lax.ppermute(pair, "gz", swap), lax.ppermute(other, "gz", swap)]
    dests = devices if gathered else SUB
    residual, middle, sent = pl.pallas_call(
        functools.partial(second_kernel, counts, axes, blocks, gathered, dests),
        out_shape=(
            shape_of(SPINOR, LANES),
            shape_of(2 * NVEC, LANES),
            shape_of(2 * dests, LANES),
        ),
        grid=(1,),
        in_specs=[vmem()] + [top(SPINOR)] * (1 + len(flat_near)) + [vmem()] * 5,
        out_specs=(vmem(), vmem(), vmem()),
        scratch_shapes=[pltpu.VMEM(fine.shape, F32)],
        compiler_params=params(8),
    )(source, payload, *flat_near, gauge, fine, vectors, project, third)

    if gathered:
        received = lax.all_to_all(sent.reshape(devices, 2, LANES), axes, 0, 0)
        received = received.reshape(2 * devices, LANES)
        lane = np.arange(nx * NVEC2 * NVEC2)
        k_lane = np.arange(LANES)[:, None]
        spread = k_lane == (lane // (NVEC2 * NVEC2) * NVEC2 + lane % NVEC2)[None]
        gather = k_lane == (lane // NVEC2)[None]
        spread, gather = jnp.asarray(spread, BF16), jnp.asarray(gather, BF16)
        wide = lane.size
        stride = depth + SUB
        solution = pl.pallas_call(
            functools.partial(third_kernel, counts, axes, blocks, shape),
            out_shape=shape_of(SPINOR, LANES),
            grid=(1,),
            in_specs=[vmem()]
            + [anywhere()] * 7
            + [vmem()] * (1 + len(flat_near))
            + [vmem(), vmem(), top(SPINOR)],
            out_specs=vmem(),
            scratch_shapes=[
                pltpu.VMEM((SUB * stride, LANES), F32),
                pltpu.VMEM(spread.shape, BF16),
                pltpu.VMEM(gather.shape, BF16),
                pltpu.VMEM(matrix.shape, F32),
                pltpu.VMEM((6 * SUB, wide), F32),
                pltpu.VMEM((2 * SUB, wide), F32),
                pltpu.VMEM(fine.shape, F32),
                pltpu.SemaphoreType.DMA((11,)),
            ],
            compiler_params=params(20),
        )(received, *held, spread, gather, matrix, vectors, *flat_near, middle, fine, payload)
    else:
        solved = line_solve(sent[:2, :NVEC2], bottom_blocks)
        solved = jnp.pad(solved, ((0, 0), (0, LANES - NVEC2)))
        rows = [solved] + [a for pair in neighbours(solved, axes) for a in pair]
        rows = jnp.concatenate(rows)
        rows = jnp.pad(rows, ((0, 2 * SUB - rows.shape[0]), (0, 0)))
        solution = pl.pallas_call(
            functools.partial(fourth_kernel, counts, axes, blocks),
            out_shape=shape_of(SPINOR, LANES),
            grid=(1,),
            in_specs=[vmem()] * (3 + len(flat_near)) + [vmem(), vmem(), top(SPINOR)],
            out_specs=vmem(),
            scratch_shapes=[pltpu.VMEM(fine.shape, F32)],
            compiler_params=params(16),
        )(rows, matrix, vectors, *flat_near, middle, fine, payload)
    return solution.reshape(source_field.shape), residual.reshape(source_field.shape)


def solution(mesh):
    return jax.shard_map(
        shards,
        mesh=mesh,
        in_specs=(
            P(None, None, None, "ta", "gz", "xy", None),
            P(None, None, None, None, "ta", "gz", "xy", None),
            P(None, None, None, None, "ta", "gz", "xy", None),
            P(None, None, None, "ta", "gz", "xy", None),
            P(None, None, "ta", "gz", "xy", None),
            P(None, None, "ta", "gz", None),
        ),
        out_specs=(
            P(None, None, None, "ta", "gz", "xy", None),
            P(None, None, None, "ta", "gz", "xy", None),
        ),
        check_vma=False,
    )
```

profile of v0, /device:TPU:0, one launch (start us, length us, event | category | flops | bytes accessed | tf_op | source)
XLA Modules:
  0.0 58.2 jit_solution(8380173646004691793)
XLA Ops:
  0.6 0.0 copy-start.10
  0.7 1.4 %reduce = f32[2,7,2304]{2,1,0:T(8,128)S(1)} reduce(f32[2,7,1,1,2304]{4,3,2,1,0:T(1,128)} %param.17, f32[]{:T(128)} %constant.29), dimensions={2,3}, to_apply=%param.17.reduce_sub_computation | reduce | bytes 258052 | tf_op args[5]
  2.2 3.0 %collective-permute-start.10 = (f32[256,128]{1,0:T(8,128)S(1)}, f32[256,128]{1,0:T(8,128)S(1)}, u32[]{:S(2)}, u32[]{:S(2)}) collective-permute-start(f32[256,128]{1,0:T(8,128)S(1)} %pad.4), channel_id=1, source_target_pairs={{0,8},{8,0},{16,24},{24,16},{1,9},{9,1},{17,25},{25,17},{2,10},{10... | collective-permute-start | bytes 393224 | tf_op jit(solution)/shard_map/ppermute | solution.py:574
  5.2 3.5 %collective-permute-done.10 = f32[256,128]{1,0:T(8,128)S(1)} collective-permute-done((f32[256,128]{1,0:T(8,128)S(1)}, f32[256,128]{1,0:T(8,128)S(1)}, u32[]{:S(2)}, u32[]{:S(2)}) %collective-permute-start.10) | collective-permute-done | bytes 131104 | tf_op jit(solution)/shard_map/ppermute | solution.py:574
  8.7 1.8 %collective-permute-start.11 = (f32[512,128]{1,0:T(8,128)S(1)}, f32[512,128]{1,0:T(8,128)S(1)}, u32[]{:S(2)}, u32[]{:S(2)}) collective-permute-start(f32[512,128]{1,0:T(8,128)S(1)} %pad_maximum_fusion.refs_0_), channel_id=1, source_target_pairs={{0,16},{8,24},{16,0},{24,8},{1,17},{9,25},{17,1},{25,9},{2,18},{10... | collective-permute-start | bytes 786440 | tf_op jit(solution)/shard_map/ppermute | solution.py:586
  10.5 3.6 %collective-permute-start.4 = (f32[24,128]{1,0:T(8,128)S(1)}, f32[24,128]{1,0:T(8,128)S(1)}, u32[]{:S(2)}, u32[]{:S(2)}) collective-permute-start(f32[24,128]{1,0:T(8,128)S(1)} %bitcast.20), channel_id=1, source_target_pairs={{0,3},{1,2},{2,1},{3,0},{4,7},{5,6},{6,5},{7,4},{8,11},{9,10},{10,... | collective-permute-start | bytes 36872 | tf_op jit(solution)/shard_map/ppermute | solution.py:87
  14.2 1.4 %collective-permute-start.1 = (f32[24,128]{1,0:T(8,128)S(1)}, f32[24,128]{1,0:T(8,128)S(1)}, u32[]{:S(2)}, u32[]{:S(2)}) collective-permute-start(f32[24,128]{1,0:T(8,128)S(1)} %bitcast.23), channel_id=1, source_target_pairs={{0,24},{8,16},{16,8},{24,0},{1,25},{9,17},{17,9},{25,1},{2,26},{10... | collective-permute-start | bytes 36872 | tf_op jit(solution)/shard_map/ppermute | solution.py:87
  15.6 0.5 collective-permute-done.4.refs_5_
  16.0 1.5 %collective-permute-start = (f32[24,128]{1,0:T(8,128)S(1)}, f32[24,128]{1,0:T(8,128)S(1)}, u32[]{:S(2)}, u32[]{:S(2)}) collective-permute-start(f32[24,128]{1,0:T(8,128)S(1)} %bitcast.24), channel_id=1, source_target_pairs={{0,8},{8,0},{16,24},{24,16},{1,9},{9,1},{17,25},{25,17},{2,10},{10... | collective-permute-start | bytes 36872 | tf_op jit(solution)/shard_map/ppermute | solution.py:87
  17.5 0.3 collective-permute-done.3.refs_4_
  17.8 0.9 %collective-permute-done.1.refs_2_ = f32[24,128]{1,0:T(8,128)S(1)} collective-permute-done((f32[24,128]{1,0:T(8,128)S(1)}, f32[24,128]{1,0:T(8,128)S(1)}, u32[]{:S(2)}, u32[]{:S(2)}) %collective-permute-start.1) | collective-permute-done | bytes 12320 | tf_op jit(solution)/shard_map/ppermute | solution.py:87
  18.7 1.0 %collective-permute-done.refs_1_ = f32[24,128]{1,0:T(8,128)S(1)} collective-permute-done((f32[24,128]{1,0:T(8,128)S(1)}, f32[24,128]{1,0:T(8,128)S(1)}, u32[]{:S(2)}, u32[]{:S(2)}) %collective-permute-start) | collective-permute-done | bytes 12320 | tf_op jit(solution)/shard_map/ppermute | solution.py:87
  19.8 0.5 shard_map.131.refs_1_.refs_15_
  20.3 3.6 %collective-permute-start.9 = (f32[312,128]{1,0:T(8,128)S(1)}, f32[312,128]{1,0:T(8,128)S(1)}, u32[]{:S(2)}, u32[]{:S(2)}) collective-permute-start(f32[312,128]{1,0:T(8,128)S(1)} %shard_map.131.refs_1_.refs_15_), channel_id=1, source_target_pairs={{0,3},{1,2},{2,1},{3,0},{4,7},{5,6},{6,5},{7,4},{8,11},{9,10},{10,... | collective-permute-start | bytes 479240 | tf_op jit(solution)/shard_map/ppermute | solution.py:87
  23.9 0.5 collective-permute-start.13
  24.4 0.1 collective-permute-start.7
  24.5 4.3 %collective-permute-done.9.refs_6_.refs_12_ = f32[312,128]{1,0:T(8,128)S(1)} collective-permute-done((f32[312,128]{1,0:T(8,128)S(1)}, f32[312,128]{1,0:T(8,128)S(1)}, u32[]{:S(2)}, u32[]{:S(2)}) %collective-permute-start.9) | collective-permute-done | bytes 159776 | tf_op jit(solution)/shard_map/ppermute | solution.py:87
  28.8 1.5 %collective-permute-start.6 = (f32[312,128]{1,0:T(8,128)S(1)}, f32[312,128]{1,0:T(8,128)S(1)}, u32[]{:S(2)}, u32[]{:S(2)}) collective-permute-start(f32[312,128]{1,0:T(8,128)S(1)} %shard_map.131.refs_1_.refs_15_), channel_id=1, source_target_pairs={{0,24},{8,16},{16,8},{24,0},{1,25},{9,17},{17,9},{25,1},{2,26},{10... | collective-permute-start | bytes 479240 | tf_op jit(solution)/shard_map/ppermute | solution.py:87
  30.3 1.2 %collective-permute-start.5 = (f32[312,128]{1,0:T(8,128)S(1)}, f32[312,128]{1,0:T(8,128)S(1)}, u32[]{:S(2)}, u32[]{:S(2)}) collective-permute-start(f32[312,128]{1,0:T(8,128)S(1)} %shard_map.131.refs_1_.refs_15_), channel_id=1, source_target_pairs={{0,8},{8,0},{16,24},{24,16},{1,9},{9,1},{17,25},{25,17},{2,10},{10... | collective-permute-start | bytes 479240 | tf_op jit(solution)/shard_map/ppermute | solution.py:87
  31.5 3.5 %collective-permute-done.6.refs_3_.refs_9_ = f32[312,128]{1,0:T(8,128)S(1)} collective-permute-done((f32[312,128]{1,0:T(8,128)S(1)}, f32[312,128]{1,0:T(8,128)S(1)}, u32[]{:S(2)}, u32[]{:S(2)}) %collective-permute-start.6) | collective-permute-done | bytes 159776 | tf_op jit(solution)/shard_map/ppermute | solution.py:87
  35.0 1.5 %collective-permute-done.5.refs_2_.refs_8_ = f32[312,128]{1,0:T(8,128)S(1)} collective-permute-done((f32[312,128]{1,0:T(8,128)S(1)}, f32[312,128]{1,0:T(8,128)S(1)}, u32[]{:S(2)}, u32[]{:S(2)}) %collective-permute-start.5) | collective-permute-done | bytes 159776 | tf_op jit(solution)/shard_map/ppermute | solution.py:87
  36.5 2.0 %shard_map.132 = (f32[24,128]{1,0:T(8,128)}, f32[48,128]{1,0:T(8,128)S(1)}, f32[64,128]{1,0:T(8,128)S(1)}) custom-call(f32[24,128]{1,0:T(8,128)S(1)} %bitcast.26, f32[312,128]{1,0:T(8,128)S(1)} %shard_map.131.refs_1_.refs_15_, f32[312,128]{1,0:T(8,128)S(1)} %collective-permute-done.5.refs_2_.refs_8_, f32[312,128]{1,0:T(8,128)S(1)} %collective-permute-done.6.refs_3_.refs_9_, ...), custom_call_target="tpu_custom_call" | custom-call | tf_op jit(solution)/shard_map/pallas_call | solution.py:590
  38.4 12.1 %all_to_all.5 = f32[32,2,128]{2,1,0:T(2,128)S(1)} all-to-all(f32[32,2,128]{2,1,0:T(2,128)S(1)} %bitcast.27), channel_id=1, replica_groups=mesh['ta'=4,'gz'=2,'xy'=4] {'ta','gz','xy'}, dimensions={0} | all-to-all | bytes 65536 | tf_op jit(solution)/shard_map/all_to_all | solution.py:605
  50.6 7.6 %shard_map.133 = f32[24,128]{1,0:T(8,128)} custom-call(f32[64,128]{1,0:T(8,128)S(1)} %bitcast.19, f32[512,128]{1,0:T(8,128)S(1)} %pad_maximum_fusion.refs_0_, f32[512,128]{1,0:T(8,128)S(1)} %collective-permute-done.11.refs_1_, f32[512,128]{1,0:T(8,128)S(1)} %collective-permute-done.12.refs_2_, f32[512,128]{1,0:T(8,128)S(1)} %collective-permute-done.13.refs_3_, ...), custom_call_target="tpu_custom_call" | custom-call | tf_op jit(solution)/shard_map/pallas_call | solution.py:614
  (34 shorter events, 0.1 us)
Async XLA Ops:
  0.6 19.1 %copy-start.10 = (f32[24,120]{1,0:T(8,128)S(1)}, f32[24,120]{1,0:T(8,128)}, u32[]{:S(2)}) copy-start(f32[24,120]{1,0:T(8,128)} %constant.16.clone.refs_9_) | copy-start | bytes 34564
  0.6 19.1 %copy-start.7 = (f32[96,192]{1,0:T(8,128)S(1)}, f32[96,192]{1,0:T(8,128)}, u32[]{:S(2)}) copy-start(f32[96,192]{1,0:T(8,128)} %constant.15.clone.refs_8_) | copy-start | bytes 221188
  0.7 35.8 %copy-start.9 = (f32[24,144]{1,0:T(8,128)S(1)}, f32[24,144]{1,0:T(8,128)}, u32[]{:S(2)}) copy-start(f32[24,144]{1,0:T(8,128)} %constant.18.clone.refs_11_) | copy-start | bytes 41476
  0.7 35.8 %copy-start.6 = (f32[96,192]{1,0:T(8,128)S(1)}, f32[96,192]{1,0:T(8,128)}, u32[]{:S(2)}) copy-start(f32[96,192]{1,0:T(8,128)} %constant.17.clone.refs_10_) | copy-start | bytes 221188
  0.7 19.1 %copy-start = (f32[2,24,1,1,1,768]{5,4,3,2,1,0:T(1,128)S(1)}, f32[2,24,1,1,1,768]{5,4,3,2,1,0:T(1,128)}, u32[]{:S(2)}) copy-start(f32[2,24,1,1,1,768]{5,4,3,2,1,0:T(1,128)} %param.16) | copy-start | bytes 442372
  0.7 19.0 %copy-start.5 = (f32[2,8,3,3,1,1,1,128]{7,6,5,4,3,2,1,0:T(1,128)S(1)}, f32[2,8,3,3,1,1,1,128]{7,6,5,4,3,2,1,0:T(1,128)}, u32[]{:S(2)}) copy-start(f32[2,8,3,3,1,1,1,128]{7,6,5,4,3,2,1,0:T(1,128)} %param.13) | copy-start | bytes 221188
  0.7 35.7 %copy-start.2 = (bf16[2,24,4,3,1,1,1,128]{7,2,6,5,4,3,1,0:T(4,128)(2,1)S(1)}, bf16[2,24,4,3,1,1,1,128]{7,2,6,5,4,3,1,0:T(4,128)(2,1)}, u32[]{:S(2)}) copy-start(bf16[2,24,4,3,1,1,1,128]{7,2,6,5,4,3,1,0:T(4,128)(2,1)} %param.14) | copy-start | bytes 442372
  2.1 48.4 %copy-start.1 = (f32[2,9,24,1,1,1,768]{6,5,4,3,2,1,0:T(1,128)S(1)}, f32[2,9,24,1,1,1,768]{6,5,4,3,2,1,0:T(1,128)}, u32[]{:S(2)}) copy-start(f32[2,9,24,1,1,1,768]{6,5,4,3,2,1,0:T(1,128)} %param.15) | copy-start | bytes 3981316
  2.1 48.4 %copy-start.3 = (bf16[128,2304]{1,0:T(8,128)(2,1)S(1)}, bf16[128,2304]{1,0:T(8,128)(2,1)}, u32[]{:S(2)}) copy-start(bf16[128,2304]{1,0:T(8,128)(2,1)} %constant.20.clone.refs_5_) | copy-start | bytes 1769476
  2.1 48.4 %copy-start.4 = (bf16[128,2304]{1,0:T(8,128)(2,1)S(1)}, bf16[128,2304]{1,0:T(8,128)(2,1)}, u32[]{:S(2)}) copy-start(bf16[128,2304]{1,0:T(8,128)(2,1)} %constant.19.clone.refs_4_) | copy-start | bytes 1769476
  2.2 6.5 %collective-permute-start.10 = (f32[256,128]{1,0:T(8,128)S(1)}, f32[256,128]{1,0:T(8,128)S(1)}, u32[]{:S(2)}, u32[]{:S(2)}) collective-permute-start(f32[256,128]{1,0:T(8,128)S(1)} %pad.4), channel_id=1, source_target_pairs={{0,8},{8,0},{16,24},{24,16},{1,9},{9,1},{17,25},{25,17},{2,10},{10... | collective-permute-start | bytes 393224 | tf_op jit(solution)/shard_map/ppermute | solution.py:574
  8.7 15.2 %collective-permute-start.11 = (f32[512,128]{1,0:T(8,128)S(1)}, f32[512,128]{1,0:T(8,128)S(1)}, u32[]{:S(2)}, u32[]{:S(2)}) collective-permute-start(f32[512,128]{1,0:T(8,128)S(1)} %pad_maximum_fusion.refs_0_), channel_id=1, source_target_pairs={{0,16},{8,24},{16,0},{24,8},{1,17},{9,25},{17,1},{25,9},{2,18},{10... | collective-permute-start | bytes 786440 | tf_op jit(solution)/shard_map/ppermute | solution.py:586
  10.5 5.5 %collective-permute-start.4 = (f32[24,128]{1,0:T(8,128)S(1)}, f32[24,128]{1,0:T(8,128)S(1)}, u32[]{:S(2)}, u32[]{:S(2)}) collective-permute-start(f32[24,128]{1,0:T(8,128)S(1)} %bitcast.20), channel_id=1, source_target_pairs={{0,3},{1,2},{2,1},{3,0},{4,7},{5,6},{6,5},{7,4},{8,11},{9,10},{10,... | collective-permute-start | bytes 36872 | tf_op jit(solution)/shard_map/ppermute | solution.py:87
  14.1 3.7 %collective-permute-start.3 = (f32[24,128]{1,0:T(8,128)S(1)}, f32[24,128]{1,0:T(8,128)S(1)}, u32[]{:S(2)}, u32[]{:S(2)}) collective-permute-start(f32[24,128]{1,0:T(8,128)S(1)} %bitcast.21), channel_id=1, source_target_pairs={{0,1},{1,0},{2,3},{3,2},{4,5},{5,4},{6,7},{7,6},{8,9},{9,8},{10,11... | collective-permute-start | bytes 36872 | tf_op jit(solution)/shard_map/ppermute | solution.py:87
  14.2 3.7 %collective-permute-start.2 = (f32[24,128]{1,0:T(8,128)S(1)}, f32[24,128]{1,0:T(8,128)S(1)}, u32[]{:S(2)}, u32[]{:S(2)}) collective-permute-start(f32[24,128]{1,0:T(8,128)S(1)} %bitcast.22), channel_id=1, source_target_pairs={{0,4},{4,0},{1,5},{5,1},{2,6},{6,2},{3,7},{7,3},{8,12},{12,8},{9,1... | collective-permute-start | bytes 36872 | tf_op jit(solution)/shard_map/ppermute | solution.py:87
  14.2 4.6 %collective-permute-start.1 = (f32[24,128]{1,0:T(8,128)S(1)}, f32[24,128]{1,0:T(8,128)S(1)}, u32[]{:S(2)}, u32[]{:S(2)}) collective-permute-start(f32[24,128]{1,0:T(8,128)S(1)} %bitcast.23), channel_id=1, source_target_pairs={{0,24},{8,16},{16,8},{24,0},{1,25},{9,17},{17,9},{25,1},{2,26},{10... | collective-permute-start | bytes 36872 | tf_op jit(solution)/shard_map/ppermute | solution.py:87
  16.0 3.7 %collective-permute-start = (f32[24,128]{1,0:T(8,128)S(1)}, f32[24,128]{1,0:T(8,128)S(1)}, u32[]{:S(2)}, u32[]{:S(2)}) collective-permute-start(f32[24,128]{1,0:T(8,128)S(1)} %bitcast.24), channel_id=1, source_target_pairs={{0,8},{8,0},{16,24},{24,16},{1,9},{9,1},{17,25},{25,17},{2,10},{10... | collective-permute-start | bytes 36872 | tf_op jit(solution)/shard_map/ppermute | solution.py:87
  20.3 8.5 %collective-permute-start.9 = (f32[312,128]{1,0:T(8,128)S(1)}, f32[312,128]{1,0:T(8,128)S(1)}, u32[]{:S(2)}, u32[]{:S(2)}) collective-permute-start(f32[312,128]{1,0:T(8,128)S(1)} %shard_map.131.refs_1_.refs_15_), channel_id=1, source_target_pairs={{0,3},{1,2},{2,1},{3,0},{4,7},{5,6},{6,5},{7,4},{8,11},{9,10},{10,... | collective-permute-start | bytes 479240 | tf_op jit(solution)/shard_map/ppermute | solution.py:87
  23.9 6.4 %collective-permute-start.8 = (f32[312,128]{1,0:T(8,128)S(1)}, f32[312,128]{1,0:T(8,128)S(1)}, u32[]{:S(2)}, u32[]{:S(2)}) collective-permute-start(f32[312,128]{1,0:T(8,128)S(1)} %shard_map.131.refs_1_.refs_15_), channel_id=1, source_target_pairs={{0,1},{1,0},{2,3},{3,2},{4,5},{5,4},{6,7},{7,6},{8,9},{9,8},{10,11... | collective-permute-start | bytes 479240 | tf_op jit(solution)/shard_map/ppermute | solution.py:87
  23.9 26.7 %collective-permute-start.12 = (f32[512,128]{1,0:T(8,128)S(1)}, f32[512,128]{1,0:T(8,128)S(1)}, u32[]{:S(2)}, u32[]{:S(2)}) collective-permute-start(f32[512,128]{1,0:T(8,128)S(1)} %pad_maximum_fusion.refs_0_), channel_id=1, source_target_pairs={{0,4},{4,0},{1,5},{5,1},{2,6},{6,2},{3,7},{7,3},{8,12},{12,8},{9,1... | collective-permute-start | bytes 786440 | tf_op jit(solution)/shard_map/ppermute | solution.py:588
  23.9 26.7 %collective-permute-start.13 = (f32[512,128]{1,0:T(8,128)S(1)}, f32[512,128]{1,0:T(8,128)S(1)}, u32[]{:S(2)}, u32[]{:S(2)}) collective-permute-start(f32[512,128]{1,0:T(8,128)S(1)} %collective-permute-done.11.refs_1_), channel_id=1, source_target_pairs={{0,4},{4,0},{1,5},{5,1},{2,6},{6,2},{3,7},{7,3},{8,12},{12,8},{9,1... | collective-permute-start | bytes 786440 | tf_op jit(solution)/shard_map/ppermute | solution.py:588
  24.4 7.1 %collective-permute-start.7 = (f32[312,128]{1,0:T(8,128)S(1)}, f32[312,128]{1,0:T(8,128)S(1)}, u32[]{:S(2)}, u32[]{:S(2)}) collective-permute-start(f32[312,128]{1,0:T(8,128)S(1)} %shard_map.131.refs_1_.refs_15_), channel_id=1, source_target_pairs={{0,4},{4,0},{1,5},{5,1},{2,6},{6,2},{3,7},{7,3},{8,12},{12,8},{9,1... | collective-permute-start | bytes 479240 | tf_op jit(solution)/shard_map/ppermute | solution.py:87
  28.8 6.2 %collective-permute-start.6 = (f32[312,128]{1,0:T(8,128)S(1)}, f32[312,128]{1,0:T(8,128)S(1)}, u32[]{:S(2)}, u32[]{:S(2)}) collective-permute-start(f32[312,128]{1,0:T(8,128)S(1)} %shard_map.131.refs_1_.refs_15_), channel_id=1, source_target_pairs={{0,24},{8,16},{16,8},{24,0},{1,25},{9,17},{17,9},{25,1},{2,26},{10... | collective-permute-start | bytes 479240 | tf_op jit(solution)/shard_map/ppermute | solution.py:87
  30.3 6.2 %collective-permute-start.5 = (f32[312,128]{1,0:T(8,128)S(1)}, f32[312,128]{1,0:T(8,128)S(1)}, u32[]{:S(2)}, u32[]{:S(2)}) collective-permute-start(f32[312,128]{1,0:T(8,128)S(1)} %shard_map.131.refs_1_.refs_15_), channel_id=1, source_target_pairs={{0,8},{8,0},{16,24},{24,16},{1,9},{9,1},{17,25},{25,17},{2,10},{10... | collective-permute-start | bytes 479240 | tf_op jit(solution)/shard_map/ppermute | solution.py:87
  (1 other events, 9.9 us)
where the time goes:
time: 58.3 us; the launch traced here: 58.2 us
  starting transfers between devices  18.3 us (31%)
  waiting for transfers between devices  15.4 us (26%)
  blocking collectives  12.1 us (21%)
  Pallas kernels  10.1 us (17%)
  other arithmetic  1.37 us (2%)
  between operations  0.8 us (1%)
    ppermute x10, starting transfers between devices, neighbours(): found.append([lax.ppermute(array, axis, p) for p in pairs])  12.9 us
    all_to_all x1, blocking collectives, shards(): received = lax.all_to_all(sent.reshape(devices, 2, LANES), axes, 0, 0)  12.1 us
    ppermute x10, waiting for transfers between devices, neighbours(): found.append([lax.ppermute(array, axis, p) for p in pairs])  11.9 us
    pallas_call x1, Pallas kernels, shards(): pl.pallas_call(functools.partial(third_kernel, counts, axes, blocks, shap...  7.58 us
    ppermute x1, waiting for transfers between devices, shards(): lax.ppermute(line, 'ta', [(i, i ^ 1) for i in range(nt)])  3.5 us
    ppermute x1, starting transfers between devices, shards(): lax.ppermute(line, 'ta', [(i, i ^ 1) for i in range(nt)])  3.03 us
    pallas_call x1, Pallas kernels, shards(): pl.pallas_call(functools.partial(second_kernel, counts, axes, blocks, gat...  1.98 us
    ppermute x1, starting transfers between devices, shards(): other = lax.ppermute(pair, 'ta', [(i, i ^ 2) for i in range(nt)])  1.83 us
  transfers between devices with their start and end apart: 14, of which 8 were waited for; matrix products, arithmetic and copies ran while one was open for 0% of the time, Pallas kernels for 4%

commit v1 on v0

--- a/solution.py
+++ b/solution.py
@@ -1,5 +1,4 @@
 import functools
-import math
 
 import jax
 import jax.numpy as jnp
@@ -8,6 +7,7 @@
 from jax.experimental import pallas as pl
 from jax.experimental.pallas import tpu as pltpu
 from jax.sharding import PartitionSpec as P
+
 
 BY = 4
 NVEC = 24
@@ -86,6 +86,37 @@
         pairs = pairings(lax.axis_size(axis))
         found.append([lax.ppermute(array, axis, p) for p in pairs])
     return found
+
+
+def load_kernel(has_line, *refs):
+    sems = refs[-1]
+    count = sems.shape[0]
+    ins, outs = refs[:count], list(refs[count : 2 * count])
+    if has_line:
+        out, outs[-1] = outs[-1], refs[-2]
+    copies = [pltpu.make_async_copy(ins[i], outs[i], sems.at[i]) for i in range(count)]
+    for copy in reversed(copies):
+        copy.start()
+    if has_line:
+        copies[-1].wait()
+        source = outs[-1]
+        chunks = out.shape[0] // 12
+        even = lax.axis_index("ta") % 2 == 0
+        for p in range(2):
+            way = [
+                source[:, (p * 7 + d) * chunks * LANES : (p * 7 + d + 1) * chunks * LANES]
+                for d in range(7)
+            ]
+            ahead, behind = way[1], way[2]
+            ways = [way[0], jnp.where(even, ahead, behind), jnp.where(even, behind, ahead)]
+            ways += [way[3] + way[4], way[5], way[6]]
+            for d, value in enumerate(ways):
+                for c in range(chunks):
+                    row = (p * 6 + d) * chunks + c
+                    out[row : row + 1] = value[:, c * LANES : (c + 1) * LANES]
+        copies = copies[:-1]
+    for copy in copies:
+        copy.wait()
 
 
 def side_step(axis, which):
@@ -220,11 +251,15 @@
         sent[i * SUB : (i + 1) * SUB] = both
 
 
-def swap_pairs(x):
-    return jnp.where(iota(x.shape, 0) % 2 == 0, pltpu.roll(x, SUB - 1, 0), pltpu.roll(x, 1, 0))
-
-
-def bottom_apply(v, near, image, spread, gather, held, stride, nz, width):
+def exchanged(x, step):
+    rows = x.shape[0]
+    if rows == 2 * step:
+        return pltpu.roll(x, step, 0)
+    up, down = pltpu.roll(x, rows - step, 0), pltpu.roll(x, step, 0)
+    return jnp.where(iota(x.shape, 0) // step % 2 == 0, up, down)
+
+
+def bottom_apply(v, near, image, spread, gather, held, width):
     lane = iota(v.shape, 1)
     edge = width - NVEC2
     up = jnp.where(lane < edge, pltpu.roll(v, LANES - NVEC2, 1), pltpu.roll(v, edge, 1))
@@ -236,39 +271,30 @@
         total = term if total is None else total + term
     near[...] = total
     chunks = near.shape[1] // LANES
+    stride = 6 * chunks
     for c in range(chunks):
         here = pl.ds(c * LANES, LANES)
-        own = [near[q * SUB : (q + 1) * SUB, here] for q in range(2)]
-        side = [
-            [near[(2 * d + q) * SUB : (2 * d + q + 1) * SUB, here] for q in range(2)]
-            for d in (1, 2)
-        ]
-        stack = [
-            (0, own),
-            (1, [pltpu.roll(x, SUB - nz, 0) for x in own]),
-            (2, [pltpu.roll(x, nz, 0) for x in own]),
-            (3, [swap_pairs(x) for x in own]),
-            (5, side[0]),
-            (6, side[1]),
-        ]
-        acc_re = acc_im = None
-        for d, (re, im) in stack:
-            block = [held[pl.ds((p * 7 + d) * chunks + c, SUB, stride=stride), :] for p in range(2)]
-            if d == 3:
-                block = [
-                    block[p] + held[pl.ds((p * 7 + 4) * chunks + c, SUB, stride=stride), :]
-                    for p in range(2)
-                ]
-            got_re = block[0] * re - block[1] * im
-            got_im = block[0] * im + block[1] * re
-            acc_re = got_re if acc_re is None else acc_re + got_re
-            acc_im = got_im if acc_im is None else acc_im + got_im
-        image[:SUB, here] = acc_re
-        image[SUB:, here] = acc_im
-    total = bottom_shift * v
+        seen = [near[i * SUB : (i + 1) * SUB, here] for i in range(6)]
+        turned = [exchanged(x, 1) for x in seen]
+        for core in range(2):
+            acc = [None, None]
+            for n, rows in enumerate((seen, turned)):
+                beside = exchanged(rows[core], 2)
+                ways = [rows[core], beside, pltpu.roll(beside, 4, 0), rows[1 - core]]
+                ways += [rows[2 + core], rows[4 + core]]
+                for d, value in enumerate(ways):
+                    block = held[core][pl.ds(d * chunks + c, SUB, stride=stride), :]
+                    got = block * value
+                    acc[n] = got if acc[n] is None else acc[n] + got
+                image[(2 * n + core) * SUB : (2 * n + core + 1) * SUB, here] = acc[n]
+    total = None
     for part in parts(image[...]):
-        total = total + dot_nt(part, gather[...], None)
-    return total
+        term = dot_nt(part, gather[...], None)
+        total = term if total is None else total + term
+    first, second = total[: 2 * SUB], total[2 * SUB :]
+    re = first - exchanged(first, 1)
+    im = second + exchanged(second, 1)
+    return bottom_shift * v + jnp.where(iota(v.shape, 0) % 2 == 0, re, im)
 
 
 def whole_sum(x):
@@ -276,59 +302,44 @@
 
 
 def minimal_residual(r, f, s):
-    r_re, r_im, f_re, f_im, s_re, s_im = r[:SUB], r[SUB:], f[:SUB], f[SUB:], s[:SUB], s[SUB:]
-    ff = whole_sum(f_re * f_re + f_im * f_im)
-    ss = whole_sum(s_re * s_re + s_im * s_im)
-    cross_re = whole_sum(f_re * s_re + f_im * s_im)
-    cross_im = whole_sum(f_re * s_im - f_im * s_re)
-    one_re = whole_sum(f_re * r_re + f_im * r_im)
-    one_im = whole_sum(f_re * r_im - f_im * r_re)
-    two_re = whole_sum(s_re * r_re + s_im * r_im)
-    two_im = whole_sum(s_re * r_im - s_im * r_re)
+    sign = jnp.where(iota(r.shape, 0) % 2 == 0, 1.0, -1.0)
+    r_turn, s_turn, f_turn = exchanged(r, 1), exchanged(s, 1), exchanged(f, 1)
+    ff = whole_sum(f * f)
+    ss = whole_sum(s * s)
+    cross_re = whole_sum(f * s)
+    cross_im = whole_sum(sign * f * s_turn)
+    one_re = whole_sum(f * r)
+    one_im = whole_sum(sign * f * r_turn)
+    two_re = whole_sum(s * r)
+    two_im = whole_sum(sign * s * r_turn)
     determinant = ff * ss - cross_re * cross_re - cross_im * cross_im
     a_re = (ss * one_re - (cross_re * two_re - cross_im * two_im)) / determinant
     a_im = (ss * one_im - (cross_re * two_im + cross_im * two_re)) / determinant
     b_re = (ff * two_re - (cross_re * one_re + cross_im * one_im)) / determinant
     b_im = (ff * two_im - (cross_re * one_im - cross_im * one_re)) / determinant
-    return jnp.concatenate(
+    return a_re * r + b_re * f - sign * (a_im * r_turn + b_im * f_turn)
+
+
+def bottom_rows(nx, solution):
+    rows = jnp.concatenate(
         [
-            a_re * r_re - a_im * r_im + b_re * f_re - b_im * f_im,
-            a_re * r_im + a_im * r_re + b_re * f_im + b_im * f_re,
+            solution[0:4],
+            solution[6:10],
+            solution[0:2],
+            solution[0:2],
+            jnp.zeros((4, LANES), F32),
         ],
         axis=0,
     )
-
-
-def bottom_rows(sites, shape, solution):
-    nt, nz, nx = shape
-    here = [lax.axis_index(a) for a in ("ta", "gz", "xy")]
-    row, col = iota((2 * SUB, 2 * SUB), 0), iota((2 * SUB, 2 * SUB), 1)
-    site = row // 2
-    lines = jnp.full((2 * SUB, 2 * SUB), here[0] * nz + here[1], jnp.int32)
-    turns = {0: [], 1: [], -1: []}
-    at = 1
-    side_rows = []
-    for number, (axis, count) in enumerate(zip(("ta", "gz", "xy"), sites)):
-        for which in range(count):
-            step = side_step(axis, which)
-            if number == 0:
-                line = lax.rem(here[0] + step + nt, nt) * nz + here[1]
-                lines = jnp.where(site == at, line, lines)
-            elif number == 1:
-                line = here[0] * nz + lax.rem(here[1] + step + nz, nz)
-                lines = jnp.where(site == at, line, lines)
-            else:
-                side_rows.append((at, lax.rem(here[2] + step + nx, nx)))
-            at += 1
-    pick = one_hot((col % SUB == lines) & (col // SUB == row % 2))
-    rows = dot(pick, solution)
-
-    def turned(x):
-        return pltpu.roll(rows, lax.rem(LANES - NVEC2 * x, LANES), 1)
-
-    result = turned(here[2])
-    for n, x in side_rows:
-        result = jnp.where(iota(result.shape, 0) // 2 == n, turned(x), result)
+    x = lax.axis_index("xy")
+
+    def turned(step):
+        place = lax.rem(x + step + nx, nx)
+        return pltpu.roll(rows, lax.rem(LANES - NVEC2 * place, LANES), 1)
+
+    site = iota(rows.shape, 0) // 2
+    near, far = turned(side_step("xy", 0)), turned(side_step("xy", 1))
+    result = jnp.where(site == 4, near, jnp.where(site == 5, far, turned(0)))
     return jnp.where(iota(result.shape, 1) < NVEC2, result, 0.0)
 
 
@@ -420,35 +431,16 @@
 
 def third_kernel(counts, axes, blocks, shape, received, *refs):
     n_sites = 1 + sum(counts)
-    held_in, refs = refs[:4], refs[4:]
-    spread_in, gather_in, matrix_in, refs = refs[0], refs[1], refs[2], refs[3:]
+    held, spread, gather, matrix, refs = refs[:2], refs[2], refs[3], refs[4], refs[5:]
     vectors, refs = refs[:n_sites], refs[n_sites:]
-    middle, fine, spinor, out = refs[:4]
-    held, spread, gather, matrix, near, image, wide, sems = refs[4:]
+    middle, fine, spinor, out, near, image, wide = refs
     nt, nz, nx = shape
-    stride = held.shape[0] // SUB
-    depth = held_in[0].shape[0] // 2
     ta, gz = lax.axis_index("ta"), lax.axis_index("gz")
-    copies = []
-    for i, ref in enumerate(held_in):
-        for h in range(2):
-            line = (ta ^ (2 * (i % 2) + h)) * nz + (gz ^ (i // 2))
-            target = held.at[pl.ds(pl.multiple_of(line * stride, SUB), depth)]
-            copies.append(
-                pltpu.make_async_copy(ref.at[pl.ds(h * depth, depth)], target, sems.at[2 * i + h])
-            )
-    copies.append(pltpu.make_async_copy(spread_in, spread, sems.at[8]))
-    copies.append(pltpu.make_async_copy(gather_in, gather, sems.at[9]))
-    matrix_copy = pltpu.make_async_copy(matrix_in, matrix, sems.at[10])
-    for copy in copies:
-        copy.start()
-    matrix_copy.start()
     total = received.shape[0]
     row, col = iota((2 * SUB, total), 0), iota((2 * SUB, total), 1)
-    fold = one_hot((col // (2 * nx) == row % SUB) & (col % 2 == row // SUB))
+    line = (ta ^ (row // 2 % nt)) * nz + (gz ^ (row // SUB))
+    fold = one_hot((col // (2 * nx) == line) & (col % 2 == row % 2))
     r = dot(fold, received[...])
-    for copy in copies:
-        copy.wait()
     apply = functools.partial(
         bottom_apply,
         near=near,
@@ -456,14 +448,11 @@
         spread=spread,
         gather=gather,
         held=held,
-        stride=stride,
-        nz=nz,
         width=nx * NVEC2,
     )
     f = apply(r)
     s = apply(f)
-    rows = bottom_rows(counts, shape, minimal_residual(r, f, s))
-    matrix_copy.wait()
+    rows = bottom_rows(nx, minimal_residual(r, f, s))
     size = NVEC * NVEC * blocks // LANES
 
     def read_block(p, d, block):
@@ -493,10 +482,6 @@
     return pl.BlockSpec(memory_space=pltpu.VMEM)
 
 
-def anywhere():
-    return pl.BlockSpec(memory_space=pl.ANY)
-
-
 def top(rows):
     return pl.BlockSpec((rows, LANES), lambda i: (0, 0))
 
@@ -513,7 +498,7 @@
     split = bottom_blocks.reshape((2, 7, -1, NVEC2, NVEC2))
     line = lax.all_gather(right, "xy", axis=1, tiled=False)
 
-    def moved(v, axis, step):
+    def turned(v, axis, step):
         n = lax.axis_size(axis)
         return lax.ppermute(v, axis, [((i + step) % n, i) for i in range(n)])
 
@@ -521,7 +506,7 @@
         return jnp.einsum("dxjk,dxk->xj", blocks, v, precision=HIGHEST)
 
     def apply(v):
-        near = [v, moved(v, "ta", 1), moved(v, "ta", -1), moved(v, "gz", 1), moved(v, "gz", -1)]
+        near = [v, turned(v, "ta", 1), turned(v, "ta", -1), turned(v, "gz", 1), turned(v, "gz", -1)]
         near = jnp.stack(near + [jnp.roll(v, -1, 1), jnp.roll(v, 1, 1)], axis=1)
         re = product(split[0], near[0]) - product(split[1], near[1])
         im = product(split[0], near[1]) + product(split[1], near[0])
@@ -563,15 +548,31 @@
     size = vectors.shape[0]
     first, second, project, third = fine_tables()
     counts = [len(pairings(n)) for n in shape]
-    gathered = nt == 4 and nz == 2 and nx * NVEC2 <= LANES
+    gathered = nt == 4 and nz == 2 and 2 < nx and nx % 2 == 0 and nx * NVEC2 <= LANES
 
     halos = neighbours(source, axes)
     flat = [a for pair in halos for a in pair]
+    tables = (first, second, project, third)
+    loads = [jnp.asarray(a) for a in (source, gauge, vectors, fine) + tables]
+    shapes = [jax.ShapeDtypeStruct(a.shape, a.dtype) for a in loads]
+    scratch = []
     if gathered:
-        per_line = bottom_blocks.shape[-1] * 14 // LANES
-        depth = -(-per_line // SUB) * SUB
-        line = jnp.pad(bottom_blocks.reshape(per_line, LANES), ((0, depth - per_line), (0, 0)))
-        pair = jnp.concatenate([line, lax.ppermute(line, "ta", [(i, i ^ 1) for i in range(nt)])])
+        loads.append(bottom_blocks.reshape(1, -1))
+        shapes.append(shape_of(bottom_blocks.shape[-1] * 12 // LANES, LANES))
+        scratch.append(pltpu.VMEM(loads[-1].shape, F32))
+    loaded = pl.pallas_call(
+        functools.partial(load_kernel, gathered),
+        out_shape=tuple(shapes),
+        in_specs=[pl.BlockSpec(memory_space=pltpu.HBM)] * len(loads),
+        out_specs=(vmem(),) * len(loads),
+        scratch_shapes=scratch + [pltpu.SemaphoreType.DMA((len(loads),))],
+        compiler_params=params(4),
+    )(*[pltpu.with_memory_space_constraint(a, pltpu.HBM) for a in loads])
+    source, gauge, vectors, fine, first, second, project, third = loaded[:8]
+    if gathered:
+        line = loaded[8]
+        beside = lax.ppermute(line, "ta", [(i, i ^ 1) for i in range(nt)])
+        pair = jnp.concatenate([line, beside])
     payload = pl.pallas_call(
         functools.partial(first_kernel, counts, axes),
         out_shape=shape_of(SPINOR + size, LANES),
@@ -584,16 +585,12 @@
     flat_near = [a for pair in near for a in pair]
     if gathered:
         other = lax.ppermute(pair, "ta", [(i, i ^ 2) for i in range(nt)])
-        swap = [(i, i ^ 1) for i in range(nz)]
-        held = [pair, other, lax.ppermute(pair, "gz", swap), lax.ppermute(other, "gz", swap)]
+        held = jnp.concatenate([pair, other])
+        held = [held, lax.ppermute(held, "gz", [(i, i ^ 1) for i in range(nz)])]
     dests = devices if gathered else SUB
     residual, middle, sent = pl.pallas_call(
         functools.partial(second_kernel, counts, axes, blocks, gathered, dests),
-        out_shape=(
-            shape_of(SPINOR, LANES),
-            shape_of(2 * NVEC, LANES),
-            shape_of(2 * dests, LANES),
-        ),
+        out_shape=(shape_of(SPINOR, LANES), shape_of(2 * NVEC, LANES), shape_of(2 * dests, LANES)),
         grid=(1,),
         in_specs=[vmem()] + [top(SPINOR)] * (1 + len(flat_near)) + [vmem()] * 5,
         out_specs=(vmem(), vmem(), vmem()),
@@ -609,28 +606,18 @@
         spread = k_lane == (lane // (NVEC2 * NVEC2) * NVEC2 + lane % NVEC2)[None]
         gather = k_lane == (lane // NVEC2)[None]
         spread, gather = jnp.asarray(spread, BF16), jnp.asarray(gather, BF16)
-        wide = lane.size
-        stride = depth + SUB
         solution = pl.pallas_call(
             functools.partial(third_kernel, counts, axes, blocks, shape),
             out_shape=shape_of(SPINOR, LANES),
             grid=(1,),
-            in_specs=[vmem()]
-            + [anywhere()] * 7
-            + [vmem()] * (1 + len(flat_near))
-            + [vmem(), vmem(), top(SPINOR)],
+            in_specs=[vmem()] * (7 + len(flat_near)) + [vmem(), vmem(), top(SPINOR)],
             out_specs=vmem(),
             scratch_shapes=[
-                pltpu.VMEM((SUB * stride, LANES), F32),
-                pltpu.VMEM(spread.shape, BF16),
-                pltpu.VMEM(gather.shape, BF16),
-                pltpu.VMEM(matrix.shape, F32),
-                pltpu.VMEM((6 * SUB, wide), F32),
-                pltpu.VMEM((2 * SUB, wide), F32),
+                pltpu.VMEM((6 * SUB, lane.size), F32),
+                pltpu.VMEM((4 * SUB, lane.size), F32),
                 pltpu.VMEM(fine.shape, F32),
-                pltpu.SemaphoreType.DMA((11,)),
             ],
-            compiler_params=params(20),
+            compiler_params=params(8),
         )(received, *held, spread, gather, matrix, vectors, *flat_near, middle, fine, payload)
     else:
         solved = line_solve(sent[:2, :NVEC2], bottom_blocks)

time: 58.3 us -> 58.4 us (level)
  waiting for transfers between devices: 15.4 us -> 19.9 us
  other arithmetic: 1.37 us -> 0.02 us
  starting transfers between devices: 18.3 us -> 17 us
  blocking collectives: 12.1 us -> 11.1 us
  Pallas kernels: 10.1 us -> 9.34 us
    ppermute x1, waiting for transfers between devices: 0.01 us -> 4.76 us  [shards(): other = lax.ppermute(pair, 'ta', [(i, i ^ 2) for i in range(nt)])]
    pallas_call x1, Pallas kernels: 7.58 us -> 5.52 us  [shards(): pl.pallas_call(functools.partial(third_kernel, counts, axes, blocks, shap...]
    unnamed x1 -> x0, other arithmetic: 1.35 us -> none
    pallas_call x0 -> x1, Pallas kernels: none -> 1.32 us  [shards(): pl.pallas_call(functools.partial(load_kernel, gathered), out_shape=tuple(...]
    all_to_all x1, blocking collectives: 12.1 us -> 11.1 us  [shards(): received = lax.all_to_all(sent.reshape(devices, 2, LANES), axes, 0, 0)]
    ppermute x10, starting transfers between devices: 12.9 us -> 12 us  [neighbours(): found.append([lax.ppermute(array, axis, p) for p in pairs])]
    ppermute x3 -> x2, waiting for transfers between devices: 3.5 us -> 3.06 us  [the longest x1 3.06 us: shards(): beside = lax.ppermute(line, 'ta', [(i, i ^ 1) for i in range(nt)])]
    ppermute x3 -> x2, starting transfers between devices: 3.54 us -> 3.1 us  [the longest x1 3.03 us: shards(): beside = lax.ppermute(line, 'ta', [(i, i ^ 1) for i in range(nt)])]
  transfers between devices with their start and end apart: 14 -> 13, of which waited for: 8 -> 5; matrix products, arithmetic and copies ran while one was open for 0% -> 0% of each run, Pallas kernels for 4% -> 4%
where the time goes in v1:
time: 58.4 us; the launch traced here: 58.1 us
  waiting for transfers between devices  19.9 us (34%)
  starting transfers between devices  17 us (29%)
  blocking collectives  11.1 us (19%)
  Pallas kernels  9.34 us (16%)
  between operations  0.74 us (1%)
    ppermute x10, waiting for transfers between devices, neighbours(): found.append([lax.ppermute(array, axis, p) for p in pairs])  12.1 us
    ppermute x10, starting transfers between devices, neighbours(): found.append([lax.ppermute(array, axis, p) for p in pairs])  12 us
    all_to_all x1, blocking collectives, shards(): received = lax.all_to_all(sent.reshape(devices, 2, LANES), axes, 0, 0)  11.1 us
    pallas_call x1, Pallas kernels, shards(): pl.pallas_call(functools.partial(third_kernel, counts, axes, blocks, shap...  5.52 us
    ppermute x1, waiting for transfers between devices, shards(): other = lax.ppermute(pair, 'ta', [(i, i ^ 2) for i in range(nt)])  4.76 us
    ppermute x1, waiting for transfers between devices, shards(): beside = lax.ppermute(line, 'ta', [(i, i ^ 1) for i in range(nt)])  3.06 us
    ppermute x1, starting transfers between devices, shards(): beside = lax.ppermute(line, 'ta', [(i, i ^ 1) for i in range(nt)])  3.03 us
    pallas_call x1, Pallas kernels, shards(): pl.pallas_call(functools.partial(second_kernel, counts, axes, blocks, gat...  1.98 us
  transfers between devices with their start and end apart: 13, of which 5 were waited for; matrix products, arithmetic and copies ran while one was open for 0% of the time, Pallas kernels for 4%

profile of v1, /device:TPU:0, one launch (start us, length us, event | category | flops | bytes accessed | tf_op | source)
XLA Modules:
  0.0 58.1 jit_solution(7464991931214035455)
XLA Ops:
  0.6 1.3 %shard_map.131 = (f32[24,128]{1,0:T(8,128)S(1)}, f32[144,128]{1,0:T(8,128)S(1)}, f32[288,128]{1,0:T(8,128)S(1)}, bf16[576,128]{1,0:T(8,128)(2,1)S(1)}, f32[96,19...) custom-call(f32[24,128]{1,0:T(8,128)} %bitcast.19, ...), custom_call_target="tpu_custom_call" | custom-call | tf_op jit(solution)/shard_map/pallas_call | solution.py:563
  2.0 3.0 %collective-permute-start.10 = (f32[216,128]{1,0:T(8,128)S(1)}, f32[216,128]{1,0:T(8,128)S(1)}, u32[]{:S(2)}, u32[]{:S(2)}) collective-permute-start(f32[216,128]{1,0:T(8,128)S(1)} %get-tuple-element.23), channel_id=1, source_target_pairs={{0,8},{8,0},{16,24},{24,16},{1,9},{9,1},{17,25},{25,17},{2,10},{10... | collective-permute-start | bytes 331784 | tf_op jit(solution)/shard_map/ppermute | solution.py:574
  5.0 3.1 %collective-permute-done.10 = f32[216,128]{1,0:T(8,128)S(1)} collective-permute-done((f32[216,128]{1,0:T(8,128)S(1)}, f32[216,128]{1,0:T(8,128)S(1)}, u32[]{:S(2)}, u32[]{:S(2)}) %collective-permute-start.10) | collective-permute-done | bytes 110624 | tf_op jit(solution)/shard_map/ppermute | solution.py:574
  8.1 1.8 %collective-permute-start.11 = (f32[432,128]{1,0:T(8,128)S(1)}, f32[432,128]{1,0:T(8,128)S(1)}, u32[]{:S(2)}, u32[]{:S(2)}) collective-permute-start(f32[432,128]{1,0:T(8,128)S(1)} %pad_maximum_fusion), channel_id=1, source_target_pairs={{0,16},{8,24},{16,0},{24,8},{1,17},{9,25},{17,1},{25,9},{2,18},{10... | collective-permute-start | bytes 663560 | tf_op jit(solution)/shard_map/ppermute | solution.py:587
  9.9 0.0 copy-start
  10.0 0.0 copy-start.1
  10.0 0.0 copy-start.2
  10.0 4.8 %collective-permute-done.11 = f32[432,128]{1,0:T(8,128)S(1)} collective-permute-done((f32[432,128]{1,0:T(8,128)S(1)}, f32[432,128]{1,0:T(8,128)S(1)}, u32[]{:S(2)}, u32[]{:S(2)}) %collective-permute-start.11) | collective-permute-done | bytes 221216 | tf_op jit(solution)/shard_map/ppermute | solution.py:587
  14.8 0.1 collective-permute-start.12
  14.8 1.5 %collective-permute-start = (f32[24,128]{1,0:T(8,128)S(1)}, f32[24,128]{1,0:T(8,128)S(1)}, u32[]{:S(2)}, u32[]{:S(2)}) collective-permute-start(f32[24,128]{1,0:T(8,128)S(1)} %bitcast.20), channel_id=1, source_target_pairs={{0,8},{8,0},{16,24},{24,16},{1,9},{9,1},{17,25},{25,17},{2,10},{10... | collective-permute-start | bytes 36872 | tf_op jit(solution)/shard_map/ppermute | solution.py:87
  16.4 1.5 %collective-permute-start.1 = (f32[24,128]{1,0:T(8,128)S(1)}, f32[24,128]{1,0:T(8,128)S(1)}, u32[]{:S(2)}, u32[]{:S(2)}) collective-permute-start(f32[24,128]{1,0:T(8,128)S(1)} %bitcast.21), channel_id=1, source_target_pairs={{0,24},{8,16},{16,8},{24,0},{1,25},{9,17},{17,9},{25,1},{2,26},{10... | collective-permute-start | bytes 36872 | tf_op jit(solution)/shard_map/ppermute | solution.py:87
  17.9 1.6 %collective-permute-start.3 = (f32[24,128]{1,0:T(8,128)S(1)}, f32[24,128]{1,0:T(8,128)S(1)}, u32[]{:S(2)}, u32[]{:S(2)}) collective-permute-start(f32[24,128]{1,0:T(8,128)S(1)} %bitcast.23), channel_id=1, source_target_pairs={{0,1},{1,0},{2,3},{3,2},{4,5},{5,4},{6,7},{7,6},{8,9},{9,8},{10,11... | collective-permute-start | bytes 36872 | tf_op jit(solution)/shard_map/ppermute | solution.py:87
  19.4 2.7 %collective-permute-start.4 = (f32[24,128]{1,0:T(8,128)S(1)}, f32[24,128]{1,0:T(8,128)S(1)}, u32[]{:S(2)}, u32[]{:S(2)}) collective-permute-start(f32[24,128]{1,0:T(8,128)S(1)} %bitcast.24), channel_id=1, source_target_pairs={{0,3},{1,2},{2,1},{3,0},{4,7},{5,6},{6,5},{7,4},{8,11},{9,10},{10,... | collective-permute-start | bytes 36872 | tf_op jit(solution)/shard_map/ppermute | solution.py:87
  22.2 0.0 collective-permute-done.1.refs_2_
  22.2 2.7 %collective-permute-done.4.refs_5_ = f32[24,128]{1,0:T(8,128)S(1)} collective-permute-done((f32[24,128]{1,0:T(8,128)S(1)}, f32[24,128]{1,0:T(8,128)S(1)}, u32[]{:S(2)}, u32[]{:S(2)}) %collective-permute-start.4) | collective-permute-done | bytes 12320 | tf_op jit(solution)/shard_map/ppermute | solution.py:87
  24.9 0.5 shard_map.132.refs_1_.refs_13_
  25.5 1.5 %collective-permute-start.5 = (f32[312,128]{1,0:T(8,128)S(1)}, f32[312,128]{1,0:T(8,128)S(1)}, u32[]{:S(2)}, u32[]{:S(2)}) collective-permute-start(f32[312,128]{1,0:T(8,128)S(1)} %shard_map.132.refs_1_.refs_13_), channel_id=1, source_target_pairs={{0,8},{8,0},{16,24},{24,16},{1,9},{9,1},{17,25},{25,17},{2,10},{10... | collective-permute-start | bytes 479240 | tf_op jit(solution)/shard_map/ppermute | solution.py:87
  27.0 0.6 %collective-permute-start.6 = (f32[312,128]{1,0:T(8,128)S(1)}, f32[312,128]{1,0:T(8,128)S(1)}, u32[]{:S(2)}, u32[]{:S(2)}) collective-permute-start(f32[312,128]{1,0:T(8,128)S(1)} %shard_map.132.refs_1_.refs_13_), channel_id=1, source_target_pairs={{0,24},{8,16},{16,8},{24,0},{1,25},{9,17},{17,9},{25,1},{2,26},{10... | collective-permute-start | bytes 479240 | tf_op jit(solution)/shard_map/ppermute | solution.py:87
  27.6 4.7 %collective-permute-done.5.refs_2_.refs_6_ = f32[312,128]{1,0:T(8,128)S(1)} collective-permute-done((f32[312,128]{1,0:T(8,128)S(1)}, f32[312,128]{1,0:T(8,128)S(1)}, u32[]{:S(2)}, u32[]{:S(2)}) %collective-permute-start.5) | collective-permute-done | bytes 159776 | tf_op jit(solution)/shard_map/ppermute | solution.py:87
  32.3 2.6 %collective-permute-start.9 = (f32[312,128]{1,0:T(8,128)S(1)}, f32[312,128]{1,0:T(8,128)S(1)}, u32[]{:S(2)}, u32[]{:S(2)}) collective-permute-start(f32[312,128]{1,0:T(8,128)S(1)} %shard_map.132.refs_1_.refs_13_), channel_id=1, source_target_pairs={{0,3},{1,2},{2,1},{3,0},{4,7},{5,6},{6,5},{7,4},{8,11},{9,10},{10,... | collective-permute-start | bytes 479240 | tf_op jit(solution)/shard_map/ppermute | solution.py:87
  34.9 4.6 %collective-permute-done.9.refs_6_.refs_10_ = f32[312,128]{1,0:T(8,128)S(1)} collective-permute-done((f32[312,128]{1,0:T(8,128)S(1)}, f32[312,128]{1,0:T(8,128)S(1)}, u32[]{:S(2)}, u32[]{:S(2)}) %collective-permute-start.9) | collective-permute-done | bytes 159776 | tf_op jit(solution)/shard_map/ppermute | solution.py:87
  39.5 2.0 %shard_map.133 = (f32[24,128]{1,0:T(8,128)}, f32[48,128]{1,0:T(8,128)S(1)}, f32[64,128]{1,0:T(8,128)S(1)}) custom-call(f32[24,128]{1,0:T(8,128)S(1)} %get-tuple-element.14.refs_0_, f32[312,128]{1,0:T(8,128)S(1)} %shard_map.132.refs_1_.refs_13_, f32[312,128]{1,0:T(8,128)S(1)} %collective-permute-done.5.refs_2_.refs_6_, ...), custom_call_target="tpu_custom_call" | custom-call | tf_op jit(solution)/shard_map/pallas_call | solution.py:591
  41.5 11.1 %all_to_all.5 = f32[32,2,128]{2,1,0:T(2,128)S(1)} all-to-all(f32[32,2,128]{2,1,0:T(2,128)S(1)} %bitcast.14), channel_id=1, replica_groups=mesh['ta'=4,'gz'=2,'xy'=4] {'ta','gz','xy'}, dimensions={0} | all-to-all | bytes 65536 | tf_op jit(solution)/shard_map/all_to_all | solution.py:602
  52.6 5.5 %shard_map.134 = f32[24,128]{1,0:T(8,128)} custom-call(f32[64,128]{1,0:T(8,128)S(1)} %bitcast.13, f32[864,128]{1,0:T(8,128)S(1)} %constant_dynamic-update-slice_fusion.refs_0_, f32[864,128]{1,0:T(8,128)S(1)} %collective-permute-done.12.refs_1_, bf16[128,2304]{1,0:T(8,128)(2,1)S(1)} %copy-done.1, bf16[128,2304]{1,0:T(8,128)(2,1)S(1)} %copy-done.2, ...), custom_call_target="tpu_custom_call" | custom-call | tf_op jit(solution)/shard_map/pallas_call | solution.py:609
  (19 shorter events, 0.1 us)
Async XLA Ops:
  0.6 14.2 %copy-start.3 = (f32[2,4,3,1,1,1,128]{6,5,4,3,2,1,0:T(1,128)S(1)}, f32[2,4,3,1,1,1,128]{6,5,4,3,2,1,0:T(1,128)}, u32[]{:S(2)}) copy-start(f32[2,4,3,1,1,1,128]{6,5,4,3,2,1,0:T(1,128)} %param.12) | copy-start | bytes 36868
  2.0 6.1 %collective-permute-start.10 = (f32[216,128]{1,0:T(8,128)S(1)}, f32[216,128]{1,0:T(8,128)S(1)}, u32[]{:S(2)}, u32[]{:S(2)}) collective-permute-start(f32[216,128]{1,0:T(8,128)S(1)} %get-tuple-element.23), channel_id=1, source_target_pairs={{0,8},{8,0},{16,24},{24,16},{1,9},{9,1},{17,25},{25,17},{2,10},{10... | collective-permute-start | bytes 331784 | tf_op jit(solution)/shard_map/ppermute | solution.py:574
  8.1 6.7 %collective-permute-start.11 = (f32[432,128]{1,0:T(8,128)S(1)}, f32[432,128]{1,0:T(8,128)S(1)}, u32[]{:S(2)}, u32[]{:S(2)}) collective-permute-start(f32[432,128]{1,0:T(8,128)S(1)} %pad_maximum_fusion), channel_id=1, source_target_pairs={{0,16},{8,24},{16,0},{24,8},{1,17},{9,25},{17,1},{25,9},{2,18},{10... | collective-permute-start | bytes 663560 | tf_op jit(solution)/shard_map/ppermute | solution.py:587
  9.9 42.6 %copy-start = (f32[2,9,24,1,1,1,768]{6,5,4,3,2,1,0:T(1,128)S(1)}, f32[2,9,24,1,1,1,768]{6,5,4,3,2,1,0:T(1,128)}, u32[]{:S(2)}) copy-start(f32[2,9,24,1,1,1,768]{6,5,4,3,2,1,0:T(1,128)} %param.15) | copy-start | bytes 3981316
  10.0 42.6 %copy-start.1 = (bf16[128,2304]{1,0:T(8,128)(2,1)S(1)}, bf16[128,2304]{1,0:T(8,128)(2,1)}, u32[]{:S(2)}) copy-start(bf16[128,2304]{1,0:T(8,128)(2,1)} %constant.16.clone.refs_2_) | copy-start | bytes 1769476
  10.0 42.6 %copy-start.2 = (bf16[128,2304]{1,0:T(8,128)(2,1)S(1)}, bf16[128,2304]{1,0:T(8,128)(2,1)}, u32[]{:S(2)}) copy-start(bf16[128,2304]{1,0:T(8,128)(2,1)} %constant.17.clone.refs_3_) | copy-start | bytes 1769476
  14.8 37.8 %collective-permute-start.12 = (f32[864,128]{1,0:T(8,128)S(1)}, f32[864,128]{1,0:T(8,128)S(1)}, u32[]{:S(2)}, u32[]{:S(2)}) collective-permute-start(f32[864,128]{1,0:T(8,128)S(1)} %constant_dynamic-update-slice_fusion.refs_0_), channel_id=1, source_target_pairs={{0,4},{4,0},{1,5},{5,1},{2,6},{6,2},{3,7},{7,3},{8,12},{12,8},{9,1... | collective-permute-start | bytes 1327112 | tf_op jit(solution)/shard_map/ppermute | solution.py:589
  14.8 4.6 %collective-permute-start = (f32[24,128]{1,0:T(8,128)S(1)}, f32[24,128]{1,0:T(8,128)S(1)}, u32[]{:S(2)}, u32[]{:S(2)}) collective-permute-start(f32[24,128]{1,0:T(8,128)S(1)} %bitcast.20), channel_id=1, source_target_pairs={{0,8},{8,0},{16,24},{24,16},{1,9},{9,1},{17,25},{25,17},{2,10},{10... | collective-permute-start | bytes 36872 | tf_op jit(solution)/shard_map/ppermute | solution.py:87
  16.4 5.8 %collective-permute-start.1 = (f32[24,128]{1,0:T(8,128)S(1)}, f32[24,128]{1,0:T(8,128)S(1)}, u32[]{:S(2)}, u32[]{:S(2)}) collective-permute-start(f32[24,128]{1,0:T(8,128)S(1)} %bitcast.21), channel_id=1, source_target_pairs={{0,24},{8,16},{16,8},{24,0},{1,25},{9,17},{17,9},{25,1},{2,26},{10... | collective-permute-start | bytes 36872 | tf_op jit(solution)/shard_map/ppermute | solution.py:87
  17.9 4.3 %collective-permute-start.2 = (f32[24,128]{1,0:T(8,128)S(1)}, f32[24,128]{1,0:T(8,128)S(1)}, u32[]{:S(2)}, u32[]{:S(2)}) collective-permute-start(f32[24,128]{1,0:T(8,128)S(1)} %bitcast.22), channel_id=1, source_target_pairs={{0,4},{4,0},{1,5},{5,1},{2,6},{6,2},{3,7},{7,3},{8,12},{12,8},{9,1... | collective-permute-start | bytes 36872 | tf_op jit(solution)/shard_map/ppermute | solution.py:87
  17.9 4.3 %collective-permute-start.3 = (f32[24,128]{1,0:T(8,128)S(1)}, f32[24,128]{1,0:T(8,128)S(1)}, u32[]{:S(2)}, u32[]{:S(2)}) collective-permute-start(f32[24,128]{1,0:T(8,128)S(1)} %bitcast.23), channel_id=1, source_target_pairs={{0,1},{1,0},{2,3},{3,2},{4,5},{5,4},{6,7},{7,6},{8,9},{9,8},{10,11... | collective-permute-start | bytes 36872 | tf_op jit(solution)/shard_map/ppermute | solution.py:87
  19.4 5.5 %collective-permute-start.4 = (f32[24,128]{1,0:T(8,128)S(1)}, f32[24,128]{1,0:T(8,128)S(1)}, u32[]{:S(2)}, u32[]{:S(2)}) collective-permute-start(f32[24,128]{1,0:T(8,128)S(1)} %bitcast.24), channel_id=1, source_target_pairs={{0,3},{1,2},{2,1},{3,0},{4,7},{5,6},{6,5},{7,4},{8,11},{9,10},{10,... | collective-permute-start | bytes 36872 | tf_op jit(solution)/shard_map/ppermute | solution.py:87
  25.5 6.8 %collective-permute-start.5 = (f32[312,128]{1,0:T(8,128)S(1)}, f32[312,128]{1,0:T(8,128)S(1)}, u32[]{:S(2)}, u32[]{:S(2)}) collective-permute-start(f32[312,128]{1,0:T(8,128)S(1)} %shard_map.132.refs_1_.refs_13_), channel_id=1, source_target_pairs={{0,8},{8,0},{16,24},{24,16},{1,9},{9,1},{17,25},{25,17},{2,10},{10... | collective-permute-start | bytes 479240 | tf_op jit(solution)/shard_map/ppermute | solution.py:87
  27.0 7.9 %collective-permute-start.6 = (f32[312,128]{1,0:T(8,128)S(1)}, f32[312,128]{1,0:T(8,128)S(1)}, u32[]{:S(2)}, u32[]{:S(2)}) collective-permute-start(f32[312,128]{1,0:T(8,128)S(1)} %shard_map.132.refs_1_.refs_13_), channel_id=1, source_target_pairs={{0,24},{8,16},{16,8},{24,0},{1,25},{9,17},{17,9},{25,1},{2,26},{10... | collective-permute-start | bytes 479240 | tf_op jit(solution)/shard_map/ppermute | solution.py:87
  27.6 7.3 %collective-permute-start.7 = (f32[312,128]{1,0:T(8,128)S(1)}, f32[312,128]{1,0:T(8,128)S(1)}, u32[]{:S(2)}, u32[]{:S(2)}) collective-permute-start(f32[312,128]{1,0:T(8,128)S(1)} %shard_map.132.refs_1_.refs_13_), channel_id=1, source_target_pairs={{0,4},{4,0},{1,5},{5,1},{2,6},{6,2},{3,7},{7,3},{8,12},{12,8},{9,1... | collective-permute-start | bytes 479240 | tf_op jit(solution)/shard_map/ppermute | solution.py:87
  27.6 7.3 %collective-permute-start.8 = (f32[312,128]{1,0:T(8,128)S(1)}, f32[312,128]{1,0:T(8,128)S(1)}, u32[]{:S(2)}, u32[]{:S(2)}) collective-permute-start(f32[312,128]{1,0:T(8,128)S(1)} %shard_map.132.refs_1_.refs_13_), channel_id=1, source_target_pairs={{0,1},{1,0},{2,3},{3,2},{4,5},{5,4},{6,7},{7,6},{8,9},{9,8},{10,11... | collective-permute-start | bytes 479240 | tf_op jit(solution)/shard_map/ppermute | solution.py:87
  32.3 7.2 %collective-permute-start.9 = (f32[312,128]{1,0:T(8,128)S(1)}, f32[312,128]{1,0:T(8,128)S(1)}, u32[]{:S(2)}, u32[]{:S(2)}) collective-permute-start(f32[312,128]{1,0:T(8,128)S(1)} %shard_map.132.refs_1_.refs_13_), channel_id=1, source_target_pairs={{0,3},{1,2},{2,1},{3,0},{4,7},{5,6},{6,5},{7,4},{8,11},{9,10},{10,... | collective-permute-start | bytes 479240 | tf_op jit(solution)/shard_map/ppermute | solution.py:87

commit v2 on v1

--- a/solution.py
+++ b/solution.py
@@ -32,7 +32,6 @@
     ],
     np.complex64,
 )
-chirality = np.array([1.0, 1.0, -1.0, -1.0])
 HIGHEST = lax.Precision.HIGHEST
 F32 = jnp.float32
 BF16 = jnp.bfloat16
@@ -56,20 +55,24 @@
             rebuild[..., way] = real_form(np.kron(lower, color)).reshape(SPINOR, 2, 2, 3)
     project = project.reshape(HALF * 8, 8 * SPINOR)
     rebuild = rebuild.reshape(SPINOR, HALF * 8)
+    return [jnp.asarray(t, BF16) for t in (project, rebuild)]
+
+
+def twisted(x, straight, crossed):
+    count = x.shape[0] // SPINOR
+    pieces = []
+    for i in range(count):
+        pieces += [x[i * SPINOR + HALF : (i + 1) * SPINOR], x[i * SPINOR : i * SPINOR + HALF]]
+    other = jnp.concatenate(pieces, axis=0)
+    row = iota(x.shape, 0) % SPINOR
+    sign = jnp.where((row % HALF < HALF // 2) != (row < HALF), crossed, -crossed)
+    return straight * x + sign * other
+
+
+def inverse_of(x, scale):
     mass = 4.0 + quark_mass
-    twist = np.kron(np.diag(mass + 1j * twist_mass * chirality), color)
-    diagonal = real_form(twist)
-    inverse = real_form(np.linalg.inv(twist))
-    first = project @ np.kron(np.eye(8), fine_damping * inverse)
-    second = np.concatenate(
-        [
-            0.5 * fine_damping * inverse @ rebuild,
-            fine_damping * (2.0 - fine_damping) * inverse,
-        ],
-        axis=1,
-    )
-    third = np.concatenate([0.5 * rebuild, -diagonal, np.eye(SPINOR)], axis=1)
-    return [np.asarray(t, np.float32) for t in (first, second, project, third)]
+    norm = mass * mass + twist_mass * twist_mass
+    return twisted(x, scale * mass / norm, -scale * twist_mass / norm)
 
 
 def pairings(n):
@@ -84,7 +87,12 @@
     found = []
     for axis in axes:
         pairs = pairings(lax.axis_size(axis))
-        found.append([lax.ppermute(array, axis, p) for p in pairs])
+        found.append(
+            [
+                lax.ppermute(array(axis, i) if callable(array) else array, axis, p)
+                for i, p in enumerate(pairs)
+            ]
+        )
     return found
 
 
@@ -137,39 +145,50 @@
     return jnp.where(even, pair[0], pair[1]), jnp.where(even, pair[1], pair[0])
 
 
-def dot(a, b):
-    return jnp.dot(a, b, precision=HIGHEST, preferred_element_type=F32)
-
-
-def dot_nt(a, b, precision=HIGHEST):
-    return lax.dot_general(
-        a, b, (((1,), (1,)), ((), ())), precision=precision, preferred_element_type=F32
-    )
-
-
-def parts(x):
-    high = x.astype(BF16)
-    rest = x - high.astype(F32)
-    middle = rest.astype(BF16)
-    low = (rest - middle.astype(F32)).astype(BF16)
-    return high, middle, low
+def parts(x, count):
+    found = []
+    for _ in range(count):
+        found.append(x.astype(BF16))
+        x = x - found[-1].astype(F32)
+    return found
+
+
+def table_left(table, x, count=2):
+    n = x.shape[1]
+    out = jnp.dot(table, jnp.concatenate(parts(x, count), axis=1), preferred_element_type=F32)
+    return sum(out[:, i * n : (i + 1) * n] for i in range(count))
+
+
+def table_right(x, table, count=2):
+    m = x.shape[0]
+    out = jnp.dot(jnp.concatenate(parts(x, count), axis=0), table, preferred_element_type=F32)
+    return sum(out[i * m : (i + 1) * m] for i in range(count))
+
+
+def product(a, b):
+    m = a.shape[0]
+    a_high, a_low = parts(a, 2)
+    b_high, b_low = parts(b, 2)
+    out = jnp.dot(jnp.concatenate([a_high, a_low], axis=0), b_high, preferred_element_type=F32)
+    return out[:m] + out[m:] + jnp.dot(a_high, b_low, preferred_element_type=F32)
 
 
 def iota(shape, dim):
     return lax.broadcasted_iota(jnp.int32, shape, dim)
 
 
-def one_hot(condition, dtype=F32):
+def one_hot(condition, dtype=BF16):
     return jnp.where(condition, 1.0, 0.0).astype(dtype)
 
 
-def hopping(spinor, halos, gauge, project, axes):
+def hopping(spinor, halos, gauge, project, rebuild, axes, change=None):
     seen = []
     for pair, axis in zip(halos, axes):
         seen.extend(ahead_behind(pair, axis))
     seen.append(pltpu.roll(spinor, LANES - 1, 1))
     seen.append(pltpu.roll(spinor, 1, 1))
-    half = dot(project, jnp.concatenate(seen, axis=0))
+    seen = jnp.concatenate(seen, axis=0)
+    half = table_left(project, seen if change is None else change(seen))
     rows = [[[None] * 3 for _ in range(2)] for _ in range(2)]
     for a in range(3):
         for b in range(3):
@@ -182,7 +201,8 @@
                 for p, value in ((0, out_re), (1, out_im)):
                     old = rows[p][s][a]
                     rows[p][s][a] = value if old is None else old + value
-    return [rows[p][s][a] for p in range(2) for s in range(2) for a in range(3)]
+    rows = [rows[p][s][a] for p in range(2) for s in range(2) for a in range(3)]
+    return table_left(rebuild, jnp.concatenate(rows, axis=0))
 
 
 def first_kernel(counts, axes, *refs):
@@ -191,11 +211,17 @@
     for count in counts:
         halos.append([r[...] for r in refs[at : at + count]])
         at += count
-    gauge, vectors, project, table, out = refs[at:]
+    gauge, vectors, project, rebuild, alone, out = refs[at:]
     value = source[...]
-    rows = hopping(value, halos, gauge, project[...], axes)
-    out[:SPINOR] = dot(table[...], jnp.concatenate(rows + [value], axis=0))
-    out[SPINOR:] = vectors[...]
+    start = functools.partial(inverse_of, scale=fine_damping)
+    hop = hopping(value, halos, gauge, project[...], rebuild[...], axes, start)
+    result = inverse_of(
+        fine_damping * (2.0 - fine_damping) * value + 0.5 * fine_damping * hop, 1.0
+    )
+    alone[...] = result
+    out[:SPINOR] = result
+    size = out.shape[0] - SPINOR
+    out[SPINOR:] = vectors[pl.ds(vectors.shape[0] - size, size), :]
 
 
 def strided_vectors(fine, i):
@@ -209,10 +235,10 @@
     for count in counts:
         halos.append([r[...] for r in refs[at : at + count]])
         at += count
-    gauge, fine, vectors, project, table, out, middle, sent, wide = refs[at:]
+    gauge, fine, vectors, project, rebuild, out, middle, sent, wide = refs[at:]
     spinor = own[...]
-    rows = hopping(spinor, halos, gauge, project[...], axes)
-    residual = dot(table[...], jnp.concatenate(rows + [spinor, source[...]], axis=0))
+    hop = hopping(spinor, halos, gauge, project[...], rebuild[...], axes)
+    residual = source[...] - twisted(spinor, 4.0 + quark_mass, twist_mass) + 0.5 * hop
     out[...] = residual
     low = residual.astype(BF16).astype(F32)
     wide[...] = fine[...].astype(F32)
@@ -224,27 +250,30 @@
         sum_re = sum_re + re * low_re + im * low_im
         sum_im = sum_im + re * low_im - im * low_re
     group = iota((LANES, LANES), 1) % blocks == iota((LANES, LANES), 0) // BY
-    right = dot(jnp.concatenate([sum_re, sum_im], axis=0), one_hot(group))
+    right = table_right(jnp.concatenate([sum_re, sum_im], axis=0), one_hot(group))
     middle[...] = right
     per = LANES // blocks
     count = NVEC // per
     keep = iota((NVEC, LANES), 1) // blocks == iota((NVEC, LANES), 0) % per
     pick = one_hot(iota((NVEC, NVEC), 1) // per == iota((NVEC, NVEC), 0) % count)
     kept = [jnp.where(keep, right[p * NVEC : (p + 1) * NVEC], 0.0) for p in range(2)]
-    pattern = dot(pick, jnp.concatenate(kept, axis=1))
+    pattern = table_left(pick, jnp.concatenate(kept, axis=1))
     pat_re, pat_im = pattern[:, :LANES], pattern[:, LANES:]
     size = NVEC2 * count
+    skip = vectors.shape[0] - 2 * size
     made_re, made_im = [], []
     for block in range(size // NVEC):
-        re = vectors[pl.ds(block * NVEC, NVEC), :]
-        im = vectors[pl.ds(size + block * NVEC, NVEC), :]
+        re = vectors[pl.ds(skip + block * NVEC, NVEC), :]
+        im = vectors[pl.ds(skip + size + block * NVEC, NVEC), :]
         made_re.append(re * pat_re + im * pat_im)
         made_im.append(re * pat_im - im * pat_re)
-    ones = jnp.ones((SUB, LANES), F32)
+    made = jnp.concatenate(made_re + made_im, axis=0)
+    summed = table_right(made, jnp.ones((LANES, LANES), BF16))
     shift = lax.axis_index("xy") * NVEC2 if place else 0
-    scatter = one_hot(iota((size, LANES), 1) == iota((size, LANES), 0) // count + shift)
+    home = iota((size, LANES), 1) == iota((size, LANES), 0) // count + shift
     line = [
-        dot(dot_nt(ones, jnp.concatenate(made, axis=0)), scatter) for made in (made_re, made_im)
+        jnp.sum(jnp.where(home, summed[p * size : (p + 1) * size], 0.0), axis=0, keepdims=True)
+        for p in range(2)
     ]
     both = jnp.where(iota((SUB, LANES), 0) % 2 == 0, line[0], line[1])
     for i in range(2 * dests // SUB):
@@ -265,11 +294,7 @@
     up = jnp.where(lane < edge, pltpu.roll(v, LANES - NVEC2, 1), pltpu.roll(v, edge, 1))
     down = jnp.where(lane >= NVEC2, pltpu.roll(v, NVEC2, 1), pltpu.roll(v, LANES - edge, 1))
     rows = jnp.concatenate([v, jnp.where(lane < width, up, 0.0), down], axis=0)
-    total = None
-    for part in parts(rows):
-        term = jnp.dot(part, spread[...], preferred_element_type=F32)
-        total = term if total is None else total + term
-    near[...] = total
+    near[...] = table_right(rows, spread[...], 3)
     chunks = near.shape[1] // LANES
     stride = 6 * chunks
     for c in range(chunks):
@@ -287,10 +312,7 @@
                     got = block * value
                     acc[n] = got if acc[n] is None else acc[n] + got
                 image[(2 * n + core) * SUB : (2 * n + core + 1) * SUB, here] = acc[n]
-    total = None
-    for part in parts(image[...]):
-        term = dot_nt(part, gather[...], None)
-        total = term if total is None else total + term
+    total = table_right(image[...], gather[...], 3)
     first, second = total[: 2 * SUB], total[2 * SUB :]
     re = first - exchanged(first, 1)
     im = second + exchanged(second, 1)
@@ -349,13 +371,9 @@
     size = NVEC2 * count
     spread = one_hot(
         (iota((LANES, 2 * LANES), 0) == iota((LANES, 2 * LANES), 1) // count)
-        & (iota((LANES, 2 * LANES), 1) < size),
-        BF16,
-    )
-    coefs = None
-    for part in parts(rows):
-        term = jnp.dot(part, spread, preferred_element_type=F32)
-        coefs = term if coefs is None else coefs + term
+        & (iota((LANES, 2 * LANES), 1) < size)
+    )
+    coefs = table_right(rows, spread, 3)
     same = iota((NVEC, size), 1) % count == iota((NVEC, size), 0) % count
     guesses = []
     for n, ref in enumerate(vectors):
@@ -367,7 +385,7 @@
             [jnp.where(same, coefs[2 * n + q : 2 * n + q + 1, :size], 0.0) for q in range(2)],
             axis=0,
         )
-        made = dot(left, wide_vectors)
+        made = product(left, wide_vectors)
         guesses.append(
             jnp.concatenate(
                 [
@@ -392,16 +410,17 @@
     near.append(
         jnp.where(aggregate == 0, pltpu.roll(own, LANES - blocks + 1, 1), pltpu.roll(own, 1, 1))
     )
+    count_blocks = size // NVEC
+    sums = [[None, None] for _ in range(count_blocks)]
+    for d, value in enumerate(near):
+        re, im = value[:NVEC], value[NVEC:]
+        for block in range(count_blocks):
+            m_re, m_im = [read_block(p, d, block) for p in range(2)]
+            got = [m_re * re - m_im * im, m_re * im + m_im * re]
+            sums[block] = [g if a is None else a + g for a, g in zip(sums[block], got)]
     made_re, made_im = [], []
-    for block in range(size // NVEC):
-        acc_re = acc_im = None
-        for d, value in enumerate(near):
-            re, im = value[:NVEC], value[NVEC:]
-            m_re, m_im = [read_block(p, d, block) for p in range(2)]
-            got_re = m_re * re - m_im * im
-            got_im = m_re * im + m_im * re
-            acc_re = got_re if acc_re is None else acc_re + got_re
-            acc_im = got_im if acc_im is None else acc_im + got_im
+    for block in range(count_blocks):
+        acc_re, acc_im = sums[block]
         row = iota((NVEC, LANES), 0) + block * NVEC
         at_home = (row % count) * per + iota((NVEC, LANES), 1) // blocks == row // count
         keep = 1.0 - middle_damping * middle_shift
@@ -411,13 +430,13 @@
         [jnp.concatenate(made_re, axis=0), jnp.concatenate(made_im, axis=0)], axis=1
     )
     row_sum = one_hot(iota((NVEC, size), 1) // count == iota((NVEC, size), 0))
-    summed = dot(row_sum, made)
+    summed = table_left(row_sum, made)
     summed = jnp.concatenate([summed[:, :LANES], summed[:, LANES:]], axis=0)
     lane_sum = one_hot(
         iota((LANES, LANES), 0) % blocks == iota((LANES, LANES), 1) % blocks
     )
-    update = dot(summed, lane_sum) + middle_damping * middle[...]
-    lift = one_hot(iota((LANES, LANES), 0) == iota((LANES, LANES), 1) // BY, BF16)
+    update = table_right(summed, lane_sum) + middle_damping * middle[...]
+    lift = one_hot(iota((LANES, LANES), 0) == iota((LANES, LANES), 1) // BY)
     lifted = jnp.dot(update.astype(BF16), lift, preferred_element_type=F32)
     u_re, u_im = lifted[:NVEC], lifted[NVEC:]
     wide[...] = fine[...].astype(F32)
@@ -440,7 +459,7 @@
     row, col = iota((2 * SUB, total), 0), iota((2 * SUB, total), 1)
     line = (ta ^ (row // 2 % nt)) * nz + (gz ^ (row // SUB))
     fold = one_hot((col // (2 * nx) == line) & (col % 2 == row % 2))
-    r = dot(fold, received[...])
+    r = table_left(fold, received[...], 3)
     apply = functools.partial(
         bottom_apply,
         near=near,
@@ -546,47 +565,50 @@
     matrix = middle_blocks.reshape(-1, LANES)
     vectors = middle_vectors.reshape(-1, LANES)
     size = vectors.shape[0]
-    first, second, project, third = fine_tables()
+    project, rebuild = fine_tables()
     counts = [len(pairings(n)) for n in shape]
     gathered = nt == 4 and nz == 2 and 2 < nx and nx % 2 == 0 and nx * NVEC2 <= LANES
 
     halos = neighbours(source, axes)
     flat = [a for pair in halos for a in pair]
-    tables = (first, second, project, third)
-    loads = [jnp.asarray(a) for a in (source, gauge, vectors, fine) + tables]
+    loads = [source, gauge, fine, project, rebuild, vectors]
     shapes = [jax.ShapeDtypeStruct(a.shape, a.dtype) for a in loads]
     scratch = []
+    depth = 0
     if gathered:
+        depth = bottom_blocks.shape[-1] * 12 // LANES
         loads.append(bottom_blocks.reshape(1, -1))
-        shapes.append(shape_of(bottom_blocks.shape[-1] * 12 // LANES, LANES))
+        shapes.append(shape_of(depth, LANES))
         scratch.append(pltpu.VMEM(loads[-1].shape, F32))
     loaded = pl.pallas_call(
         functools.partial(load_kernel, gathered),
         out_shape=tuple(shapes),
         in_specs=[pl.BlockSpec(memory_space=pltpu.HBM)] * len(loads),
-        out_specs=(vmem(),) * len(loads),
+        out_specs=(vmem(),) * len(shapes),
         scratch_shapes=scratch + [pltpu.SemaphoreType.DMA((len(loads),))],
         compiler_params=params(4),
     )(*[pltpu.with_memory_space_constraint(a, pltpu.HBM) for a in loads])
-    source, gauge, vectors, fine, first, second, project, third = loaded[:8]
+    source, gauge, fine, project, rebuild, mine = loaded[:6]
     if gathered:
-        line = loaded[8]
+        line = loaded[6]
         beside = lax.ppermute(line, "ta", [(i, i ^ 1) for i in range(nt)])
         pair = jnp.concatenate([line, beside])
-    payload = pl.pallas_call(
+    spinor, payload = pl.pallas_call(
         functools.partial(first_kernel, counts, axes),
-        out_shape=shape_of(SPINOR + size, LANES),
+        out_shape=(shape_of(SPINOR, LANES), shape_of(SPINOR + size, LANES)),
         in_specs=[vmem()] * (len(flat) + 5),
-        out_specs=vmem(),
+        out_specs=(vmem(), vmem()),
         compiler_params=params(8),
-    )(source, *flat, gauge, vectors, first, second)
-
-    near = neighbours(payload, axes)
+    )(source, *flat, gauge, mine, project, rebuild)
+
+    alone = (("ta", 0), ("xy", 1)) if gathered else ()
+    near = neighbours(lambda axis, i: spinor if (axis, i) in alone else payload, axes)
     flat_near = [a for pair in near for a in pair]
+    near_vectors = list(flat_near)
     if gathered:
         other = lax.ppermute(pair, "ta", [(i, i ^ 2) for i in range(nt)])
-        held = jnp.concatenate([pair, other])
-        held = [held, lax.ppermute(held, "gz", [(i, i ^ 1) for i in range(nz)])]
+        near_vectors[0] = lax.ppermute(vectors, "ta", pairings(nt)[0])
+        near_vectors[-1] = lax.ppermute(vectors, "xy", pairings(nx)[1])
     dests = devices if gathered else SUB
     residual, middle, sent = pl.pallas_call(
         functools.partial(second_kernel, counts, axes, blocks, gathered, dests),
@@ -596,15 +618,18 @@
         out_specs=(vmem(), vmem(), vmem()),
         scratch_shapes=[pltpu.VMEM(fine.shape, F32)],
         compiler_params=params(8),
-    )(source, payload, *flat_near, gauge, fine, vectors, project, third)
+    )(source, spinor, *flat_near, gauge, fine, mine, project, rebuild)
 
     if gathered:
         received = lax.all_to_all(sent.reshape(devices, 2, LANES), axes, 0, 0)
         received = received.reshape(2 * devices, LANES)
+        received, pair, other = lax.optimization_barrier((received, pair, other))
+        held = jnp.concatenate([pair, other])
+        held = [held, lax.ppermute(held, "gz", pairings(nz)[0])]
         lane = np.arange(nx * NVEC2 * NVEC2)
         k_lane = np.arange(LANES)[:, None]
         spread = k_lane == (lane // (NVEC2 * NVEC2) * NVEC2 + lane % NVEC2)[None]
-        gather = k_lane == (lane // NVEC2)[None]
+        gather = k_lane.T == (lane // NVEC2)[:, None]
         spread, gather = jnp.asarray(spread, BF16), jnp.asarray(gather, BF16)
         solution = pl.pallas_call(
             functools.partial(third_kernel, counts, axes, blocks, shape),
@@ -618,7 +643,7 @@
                 pltpu.VMEM(fine.shape, F32),
             ],
             compiler_params=params(8),
-        )(received, *held, spread, gather, matrix, vectors, *flat_near, middle, fine, payload)
+        )(received, *held, spread, gather, matrix, mine, *near_vectors, middle, fine, spinor)
     else:
         solved = line_solve(sent[:2, :NVEC2], bottom_blocks)
         solved = jnp.pad(solved, ((0, 0), (0, LANES - NVEC2)))
@@ -633,7 +658,7 @@
             out_specs=vmem(),
             scratch_shapes=[pltpu.VMEM(fine.shape, F32)],
             compiler_params=params(16),
-        )(rows, matrix, vectors, *flat_near, middle, fine, payload)
+        )(rows, matrix, mine, *near_vectors, middle, fine, spinor)
     return solution.reshape(source_field.shape), residual.reshape(source_field.shape)
 
 

time: 58.4 us -> 49.5 us (0.85)
  waiting for transfers between devices: 19.9 us -> 14.7 us
  Pallas kernels: 9.34 us -> 6.15 us
    ppermute x1, waiting for transfers between devices: 4.76 us -> 0.01 us  [shards(): other = lax.ppermute(pair, 'ta', [(i, i ^ 2) for i in range(nt)])]
    ppermute x11 -> x13, starting transfers between devices: 12.1 us -> 15.3 us  [the longest x10 14 us: neighbours(): lax.ppermute(array(axis, i) if callable(array) else array, axis, p)]
    pallas_call x1, Pallas kernels: 5.52 us -> 3.28 us  [shards(): pl.pallas_call(functools.partial(third_kernel, counts, axes, blocks, shap...]
    ppermute x1, starting transfers between devices: 1.83 us -> 0.07 us  [shards(): other = lax.ppermute(pair, 'ta', [(i, i ^ 2) for i in range(nt)])]
    ppermute x1, starting transfers between devices: 3.03 us -> 1.56 us  [shards(): beside = lax.ppermute(line, 'ta', [(i, i ^ 1) for i in range(nt)])]
    ppermute x1, waiting for transfers between devices: 3.06 us -> 1.76 us  [shards(): beside = lax.ppermute(line, 'ta', [(i, i ^ 1) for i in range(nt)])]
    ppermute x11 -> x13, waiting for transfers between devices: 12.1 us -> 12.9 us  [the longest x10 5.68 us: neighbours(): lax.ppermute(array(axis, i) if callable(array) else array, axis, p)]
    pallas_call x1, Pallas kernels: 1.98 us -> 1.27 us  [shards(): pl.pallas_call(functools.partial(second_kernel, counts, axes, blocks, gat...]
  transfers between devices with their start and end apart: 13 -> 15, of which waited for: 5 -> 6; matrix products, arithmetic and copies ran while one was open for 0% -> 0% of each run, Pallas kernels for 4% -> 6%
where the time goes in v2:
time: 49.5 us; the launch traced here: 49.2 us
  starting transfers between devices  17 us (34%)
  waiting for transfers between devices  14.7 us (30%)
  blocking collectives  10.6 us (21%)
  Pallas kernels  6.15 us (12%)
  between operations  0.78 us (2%)
    ppermute x10, starting transfers between devices, neighbours(): lax.ppermute(array(axis, i) if callable(array) else array, axis, p)  14 us
    all_to_all x1, blocking collectives, shards(): received = lax.all_to_all(sent.reshape(devices, 2, LANES), axes, 0, 0)  10.6 us
    ppermute x10, waiting for transfers between devices, neighbours(): lax.ppermute(array(axis, i) if callable(array) else array, axis, p)  5.68 us
    ppermute x1, waiting for transfers between devices, shards(): near_vectors[0] = lax.ppermute(vectors, 'ta', pairings(nt)[0])  5.01 us
    pallas_call x1, Pallas kernels, shards(): pl.pallas_call(functools.partial(third_kernel, counts, axes, blocks, shap...  3.28 us
    ppermute x1, waiting for transfers between devices, shards(): near_vectors[-1] = lax.ppermute(vectors, 'xy', pairings(nx)[1])  2.23 us
    ppermute x1, waiting for transfers between devices, shards(): beside = lax.ppermute(line, 'ta', [(i, i ^ 1) for i in range(nt)])  1.76 us
    ppermute x1, starting transfers between devices, shards(): beside = lax.ppermute(line, 'ta', [(i, i ^ 1) for i in range(nt)])  1.56 us
  transfers between devices with their start and end apart: 15, of which 6 were waited for; matrix products, arithmetic and copies ran while one was open for 0% of the time, Pallas kernels for 6%

profile of v2, /device:TPU:0, one launch (start us, length us, event | category | flops | bytes accessed | tf_op | source)
XLA Modules:
  0.0 49.2 jit_solution(8626990851064480703)
XLA Ops:
  0.6 3.0 %collective-permute-start = (f32[24,128]{1,0:T(8,128)}, f32[24,128]{1,0:T(8,128)S(1)}, u32[]{:S(2)}, u32[]{:S(2)}) collective-permute-start(f32[24,128]{1,0:T(8,128)} %bitcast.21), channel_id=1, source_target_pairs={{0,8},{8,0},{16,24},{24,16},{1,9},{9,1},{17,25},{25,17},{2,10},{10... | collective-permute-start | bytes 36872 | tf_op jit(solution)/shard_map/ppermute | solution.py:92
  3.7 1.5 %collective-permute-start.1 = (f32[24,128]{1,0:T(8,128)}, f32[24,128]{1,0:T(8,128)S(1)}, u32[]{:S(2)}, u32[]{:S(2)}) collective-permute-start(f32[24,128]{1,0:T(8,128)} %bitcast.22), channel_id=1, source_target_pairs={{0,24},{8,16},{16,8},{24,0},{1,25},{9,17},{17,9},{25,1},{2,26},{10... | collective-permute-start | bytes 36872 | tf_op jit(solution)/shard_map/ppermute | solution.py:92
  5.2 1.6 %collective-permute-start.3 = (f32[24,128]{1,0:T(8,128)}, f32[24,128]{1,0:T(8,128)S(1)}, u32[]{:S(2)}, u32[]{:S(2)}) collective-permute-start(f32[24,128]{1,0:T(8,128)} %bitcast.24), channel_id=1, source_target_pairs={{0,1},{1,0},{2,3},{3,2},{4,5},{5,4},{6,7},{7,6},{8,9},{9,8},{10,11... | collective-permute-start | bytes 36872 | tf_op jit(solution)/shard_map/ppermute | solution.py:92
  6.7 2.5 %collective-permute-start.4 = (f32[24,128]{1,0:T(8,128)}, f32[24,128]{1,0:T(8,128)S(1)}, u32[]{:S(2)}, u32[]{:S(2)}) collective-permute-start(f32[24,128]{1,0:T(8,128)} %bitcast.25), channel_id=1, source_target_pairs={{0,3},{1,2},{2,1},{3,0},{4,7},{5,6},{6,5},{7,4},{8,11},{9,10},{10,... | collective-permute-start | bytes 36872 | tf_op jit(solution)/shard_map/ppermute | solution.py:92
  9.2 1.2 %shard_map.113 = (f32[24,128]{1,0:T(8,128)S(1)}, f32[144,128]{1,0:T(8,128)S(1)}, bf16[576,128]{1,0:T(8,128)(2,1)S(1)}, bf16[96,192]{1,0:T(8,128)(2,1)S(1)}, bf16...) custom-call(f32[24,128]{1,0:T(8,128)} %bitcast.26, f32[144,128]{1,0:T(8,128)} %bitcast.20, ...), custom_call_target="tpu_custom_call" | custom-call | tf_op jit(solution)/shard_map/pallas_call | solution.py:583
  10.5 0.0 copy-start.2
  10.5 1.6 %collective-permute-start.10 = (f32[216,128]{1,0:T(8,128)S(1)}, f32[216,128]{1,0:T(8,128)S(1)}, u32[]{:S(2)}, u32[]{:S(2)}) collective-permute-start(f32[216,128]{1,0:T(8,128)S(1)} %get-tuple-element.26), channel_id=1, source_target_pairs={{0,8},{8,0},{16,24},{24,16},{1,9},{9,1},{17,25},{25,17},{2,10},{10... | collective-permute-start | bytes 331784 | tf_op jit(solution)/shard_map/ppermute | solution.py:594
  12.1 0.4 collective-permute-done.4.refs_5_
  12.4 0.4 shard_map.114
  12.9 1.5 %collective-permute-start.6 = (f32[312,128]{1,0:T(8,128)S(1)}, f32[312,128]{1,0:T(8,128)S(1)}, u32[]{:S(2)}, u32[]{:S(2)}) collective-permute-start(f32[312,128]{1,0:T(8,128)S(1)} %get-tuple-element.23), channel_id=1, source_target_pairs={{0,24},{8,16},{16,8},{24,0},{1,25},{9,17},{17,9},{25,1},{2,26},{10... | collective-permute-start | bytes 479240 | tf_op jit(solution)/shard_map/ppermute | solution.py:92
  14.4 1.8 %collective-permute-done.10 = f32[216,128]{1,0:T(8,128)S(1)} collective-permute-done((f32[216,128]{1,0:T(8,128)S(1)}, f32[216,128]{1,0:T(8,128)S(1)}, u32[]{:S(2)}, u32[]{:S(2)}) %collective-permute-start.10) | collective-permute-done | bytes 110624 | tf_op jit(solution)/shard_map/ppermute | solution.py:594
  16.1 0.1 collective-permute-start.11
  16.2 1.8 %collective-permute-start.5 = (f32[24,128]{1,0:T(8,128)S(1)}, f32[24,128]{1,0:T(8,128)S(1)}, u32[]{:S(2)}, u32[]{:S(2)}) collective-permute-start(f32[24,128]{1,0:T(8,128)S(1)} %get-tuple-element.22.refs_1_.refs_13_), channel_id=1, source_target_pairs={{0,8},{8,0},{16,24},{24,16},{1,9},{9,1},{17,25},{25,17},{2,10},{10... | collective-permute-start | bytes 36872 | tf_op jit(solution)/shard_map/ppermute | solution.py:92
  18.0 2.0 %collective-permute-done.5.refs_2_ = f32[24,128]{1,0:T(8,128)S(1)} collective-permute-done((f32[24,128]{1,0:T(8,128)S(1)}, f32[24,128]{1,0:T(8,128)S(1)}, u32[]{:S(2)}, u32[]{:S(2)}) %collective-permute-start.5) | collective-permute-done | bytes 12320 | tf_op jit(solution)/shard_map/ppermute | solution.py:92
  20.0 2.2 %collective-permute-start.9 = (f32[24,128]{1,0:T(8,128)S(1)}, f32[24,128]{1,0:T(8,128)S(1)}, u32[]{:S(2)}, u32[]{:S(2)}) collective-permute-start(f32[24,128]{1,0:T(8,128)S(1)} %get-tuple-element.22.refs_1_.refs_13_), channel_id=1, source_target_pairs={{0,3},{1,2},{2,1},{3,0},{4,7},{5,6},{6,5},{7,4},{8,11},{9,10},{10,... | collective-permute-start | bytes 36872 | tf_op jit(solution)/shard_map/ppermute | solution.py:92
  22.1 3.3 %collective-permute-done.9.refs_6_ = f32[24,128]{1,0:T(8,128)S(1)} collective-permute-done((f32[24,128]{1,0:T(8,128)S(1)}, f32[24,128]{1,0:T(8,128)S(1)}, u32[]{:S(2)}, u32[]{:S(2)}) %collective-permute-start.9) | collective-permute-done | bytes 12320 | tf_op jit(solution)/shard_map/ppermute | solution.py:92
  25.5 1.3 %shard_map.115 = (f32[24,128]{1,0:T(8,128)}, f32[48,128]{1,0:T(8,128)S(1)}, f32[64,128]{1,0:T(8,128)S(1)}) custom-call(f32[24,128]{1,0:T(8,128)S(1)} %get-tuple-element.17.refs_0_, f32[24,128]{1,0:T(8,128)S(1)} %get-tuple-element.22.refs_1_.refs_13_, f32[24,128]{1,0:T(8,128)S(1)} %collective-permute-done.5.refs_2_, ...), custom_call_target="tpu_custom_call" | custom-call | tf_op jit(solution)/shard_map/pallas_call | solution.py:613
  26.8 10.6 %all_to_all.5 = f32[32,2,128]{2,1,0:T(2,128)S(1)} all-to-all(f32[32,2,128]{2,1,0:T(2,128)S(1)} %bitcast.14), channel_id=1, replica_groups=mesh['ta'=4,'gz'=2,'xy'=4] {'ta','gz','xy'}, dimensions={0} | all-to-all | bytes 65536 | tf_op jit(solution)/shard_map/all_to_all | solution.py:624
  37.4 0.1 collective-permute-start.12
  37.5 0.7 %collective-permute-start.13 = (f32[288,128]{1,0:T(8,128)S(1)}, f32[288,128]{1,0:T(8,128)S(1)}, u32[]{:S(2)}, u32[]{:S(2)}) collective-permute-start(f32[288,128]{1,0:T(8,128)S(1)} %bitcast.17), channel_id=1, source_target_pairs={{0,8},{8,0},{16,24},{24,16},{1,9},{9,1},{17,25},{25,17},{2,10},{10... | collective-permute-start | bytes 442376 | tf_op jit(solution)/shard_map/ppermute | solution.py:610
  38.1 0.6 %collective-permute-start.14 = (f32[288,128]{1,0:T(8,128)S(1)}, f32[288,128]{1,0:T(8,128)S(1)}, u32[]{:S(2)}, u32[]{:S(2)}) collective-permute-start(f32[288,128]{1,0:T(8,128)S(1)} %bitcast.18), channel_id=1, source_target_pairs={{0,3},{1,2},{2,1},{3,0},{4,7},{5,6},{6,5},{7,4},{8,11},{9,10},{10,... | collective-permute-start | bytes 442376 | tf_op jit(solution)/shard_map/ppermute | solution.py:611
  38.7 5.0 %collective-permute-done.13.refs_6_ = f32[288,128]{1,0:T(8,128)S(1)} collective-permute-done((f32[288,128]{1,0:T(8,128)S(1)}, f32[288,128]{1,0:T(8,128)S(1)}, u32[]{:S(2)}, u32[]{:S(2)}) %collective-permute-start.13) | collective-permute-done | bytes 147488 | tf_op jit(solution)/shard_map/ppermute | solution.py:610
  43.7 2.2 %collective-permute-done.14.refs_10_ = f32[288,128]{1,0:T(8,128)S(1)} collective-permute-done((f32[288,128]{1,0:T(8,128)S(1)}, f32[288,128]{1,0:T(8,128)S(1)}, u32[]{:S(2)}, u32[]{:S(2)}) %collective-permute-start.14) | collective-permute-done | bytes 147488 | tf_op jit(solution)/shard_map/ppermute | solution.py:611
  46.0 3.3 %shard_map.116 = f32[24,128]{1,0:T(8,128)} custom-call(f32[64,128]{1,0:T(8,128)S(1)} %bitcast.13, f32[864,128]{1,0:T(8,128)S(1)} %constant_dynamic-update-slice_fusion.2.refs_0_, f32[864,128]{1,0:T(8,128)S(1)} %collective-permute-done.12.refs_1_, bf16[128,2304]{1,0:T(8,128)(2,1)S(1)} %copy-done.1, bf16[2304,128]{1,0:T(8,128)(2,1)S(1)} %copy-done.2, ...), custom_call_target="tpu_custom_call" | custom-call | tf_op jit(solution)/shard_map/pallas_call | solution.py:634
  (23 shorter events, 0.1 us)
Async XLA Ops:
  0.6 9.8 %collective-permute-start = (f32[24,128]{1,0:T(8,128)}, f32[24,128]{1,0:T(8,128)S(1)}, u32[]{:S(2)}, u32[]{:S(2)}) collective-permute-start(f32[24,128]{1,0:T(8,128)} %bitcast.21), channel_id=1, source_target_pairs={{0,8},{8,0},{16,24},{24,16},{1,9},{9,1},{17,25},{25,17},{2,10},{10... | collective-permute-start | bytes 36872 | tf_op jit(solution)/shard_map/ppermute | solution.py:92
  3.7 8.4 %collective-permute-start.1 = (f32[24,128]{1,0:T(8,128)}, f32[24,128]{1,0:T(8,128)S(1)}, u32[]{:S(2)}, u32[]{:S(2)}) collective-permute-start(f32[24,128]{1,0:T(8,128)} %bitcast.22), channel_id=1, source_target_pairs={{0,24},{8,16},{16,8},{24,0},{1,25},{9,17},{17,9},{25,1},{2,26},{10... | collective-permute-start | bytes 36872 | tf_op jit(solution)/shard_map/ppermute | solution.py:92
  5.2 6.9 %collective-permute-start.2 = (f32[24,128]{1,0:T(8,128)}, f32[24,128]{1,0:T(8,128)S(1)}, u32[]{:S(2)}, u32[]{:S(2)}) collective-permute-start(f32[24,128]{1,0:T(8,128)} %bitcast.23), channel_id=1, source_target_pairs={{0,4},{4,0},{1,5},{5,1},{2,6},{6,2},{3,7},{7,3},{8,12},{12,8},{9,1... | collective-permute-start | bytes 36872 | tf_op jit(solution)/shard_map/ppermute | solution.py:92
  5.2 6.9 %collective-permute-start.3 = (f32[24,128]{1,0:T(8,128)}, f32[24,128]{1,0:T(8,128)S(1)}, u32[]{:S(2)}, u32[]{:S(2)}) collective-permute-start(f32[24,128]{1,0:T(8,128)} %bitcast.24), channel_id=1, source_target_pairs={{0,1},{1,0},{2,3},{3,2},{4,5},{5,4},{6,7},{7,6},{8,9},{9,8},{10,11... | collective-permute-start | bytes 36872 | tf_op jit(solution)/shard_map/ppermute | solution.py:92
  6.7 5.7 %collective-permute-start.4 = (f32[24,128]{1,0:T(8,128)}, f32[24,128]{1,0:T(8,128)S(1)}, u32[]{:S(2)}, u32[]{:S(2)}) collective-permute-start(f32[24,128]{1,0:T(8,128)} %bitcast.25), channel_id=1, source_target_pairs={{0,3},{1,2},{2,1},{3,0},{4,7},{5,6},{6,5},{7,4},{8,11},{9,10},{10,... | collective-permute-start | bytes 36872 | tf_op jit(solution)/shard_map/ppermute | solution.py:92
  10.4 27.0 %copy-start.3 = (f32[2,24,1,1,1,768]{5,4,3,2,1,0:T(1,128)S(1)}, f32[2,24,1,1,1,768]{5,4,3,2,1,0:T(1,128)}, u32[]{:S(2)}) copy-start(f32[2,24,1,1,1,768]{5,4,3,2,1,0:T(1,128)} %param.14) | copy-start | bytes 442372
  10.4 35.5 %copy-start = (f32[2,9,24,1,1,1,768]{6,5,4,3,2,1,0:T(1,128)S(1)}, f32[2,9,24,1,1,1,768]{6,5,4,3,2,1,0:T(1,128)}, u32[]{:S(2)}) copy-start(f32[2,9,24,1,1,1,768]{6,5,4,3,2,1,0:T(1,128)} %param.13) | copy-start | bytes 3981316
  10.4 35.5 %copy-start.1 = (bf16[128,2304]{1,0:T(8,128)(2,1)S(1)}, bf16[128,2304]{1,0:T(8,128)(2,1)}, u32[]{:S(2)}) copy-start(bf16[128,2304]{1,0:T(8,128)(2,1)} %constant.10.clone.refs_2_) | copy-start | bytes 1769476
  10.5 35.5 %copy-start.2 = (bf16[2304,128]{1,0:T(8,128)(2,1)S(1)}, bf16[2304,128]{1,0:T(8,128)(2,1)}, u32[]{:S(2)}) copy-start(bf16[2304,128]{1,0:T(8,128)(2,1)} %constant.11.clone.refs_3_) | copy-start | bytes 1769476
  10.5 5.7 %collective-permute-start.10 = (f32[216,128]{1,0:T(8,128)S(1)}, f32[216,128]{1,0:T(8,128)S(1)}, u32[]{:S(2)}, u32[]{:S(2)}) collective-permute-start(f32[216,128]{1,0:T(8,128)S(1)} %get-tuple-element.26), channel_id=1, source_target_pairs={{0,8},{8,0},{16,24},{24,16},{1,9},{9,1},{17,25},{25,17},{2,10},{10... | collective-permute-start | bytes 331784 | tf_op jit(solution)/shard_map/ppermute | solution.py:594
  12.9 12.6 %collective-permute-start.6 = (f32[312,128]{1,0:T(8,128)S(1)}, f32[312,128]{1,0:T(8,128)S(1)}, u32[]{:S(2)}, u32[]{:S(2)}) collective-permute-start(f32[312,128]{1,0:T(8,128)S(1)} %get-tuple-element.23), channel_id=1, source_target_pairs={{0,24},{8,16},{16,8},{24,0},{1,25},{9,17},{17,9},{25,1},{2,26},{10... | collective-permute-start | bytes 479240 | tf_op jit(solution)/shard_map/ppermute | solution.py:92
  14.4 11.1 %collective-permute-start.7 = (f32[312,128]{1,0:T(8,128)S(1)}, f32[312,128]{1,0:T(8,128)S(1)}, u32[]{:S(2)}, u32[]{:S(2)}) collective-permute-start(f32[312,128]{1,0:T(8,128)S(1)} %get-tuple-element.23), channel_id=1, source_target_pairs={{0,4},{4,0},{1,5},{5,1},{2,6},{6,2},{3,7},{7,3},{8,12},{12,8},{9,1... | collective-permute-start | bytes 479240 | tf_op jit(solution)/shard_map/ppermute | solution.py:92
  14.4 11.1 %collective-permute-start.8 = (f32[312,128]{1,0:T(8,128)S(1)}, f32[312,128]{1,0:T(8,128)S(1)}, u32[]{:S(2)}, u32[]{:S(2)}) collective-permute-start(f32[312,128]{1,0:T(8,128)S(1)} %get-tuple-element.23), channel_id=1, source_target_pairs={{0,1},{1,0},{2,3},{3,2},{4,5},{5,4},{6,7},{7,6},{8,9},{9,8},{10,11... | collective-permute-start | bytes 479240 | tf_op jit(solution)/shard_map/ppermute | solution.py:92
  16.1 21.2 %collective-permute-start.11 = (f32[432,128]{1,0:T(8,128)S(1)}, f32[432,128]{1,0:T(8,128)S(1)}, u32[]{:S(2)}, u32[]{:S(2)}) collective-permute-start(f32[432,128]{1,0:T(8,128)S(1)} %constant_dynamic-update-slice_fusion), channel_id=1, source_target_pairs={{0,16},{8,24},{16,0},{24,8},{1,17},{9,25},{17,1},{25,9},{2,18},{10... | collective-permute-start | bytes 663560 | tf_op jit(solution)/shard_map/ppermute | solution.py:609
  16.2 3.8 %collective-permute-start.5 = (f32[24,128]{1,0:T(8,128)S(1)}, f32[24,128]{1,0:T(8,128)S(1)}, u32[]{:S(2)}, u32[]{:S(2)}) collective-permute-start(f32[24,128]{1,0:T(8,128)S(1)} %get-tuple-element.22.refs_1_.refs_13_), channel_id=1, source_target_pairs={{0,8},{8,0},{16,24},{24,16},{1,9},{9,1},{17,25},{25,17},{2,10},{10... | collective-permute-start | bytes 36872 | tf_op jit(solution)/shard_map/ppermute | solution.py:92
  20.0 5.5 %collective-permute-start.9 = (f32[24,128]{1,0:T(8,128)S(1)}, f32[24,128]{1,0:T(8,128)S(1)}, u32[]{:S(2)}, u32[]{:S(2)}) collective-permute-start(f32[24,128]{1,0:T(8,128)S(1)} %get-tuple-element.22.refs_1_.refs_13_), channel_id=1, source_target_pairs={{0,3},{1,2},{2,1},{3,0},{4,7},{5,6},{6,5},{7,4},{8,11},{9,10},{10,... | collective-permute-start | bytes 36872 | tf_op jit(solution)/shard_map/ppermute | solution.py:92
  37.4 8.6 %collective-permute-start.12 = (f32[864,128]{1,0:T(8,128)S(1)}, f32[864,128]{1,0:T(8,128)S(1)}, u32[]{:S(2)}, u32[]{:S(2)}) collective-permute-start(f32[864,128]{1,0:T(8,128)S(1)} %constant_dynamic-update-slice_fusion.2.refs_0_), channel_id=1, source_target_pairs={{0,4},{4,0},{1,5},{5,1},{2,6},{6,2},{3,7},{7,3},{8,12},{12,8},{9,1... | collective-permute-start | bytes 1327112 | tf_op jit(solution)/shard_map/ppermute | solution.py:628
  37.5 6.2 %collective-permute-start.13 = (f32[288,128]{1,0:T(8,128)S(1)}, f32[288,128]{1,0:T(8,128)S(1)}, u32[]{:S(2)}, u32[]{:S(2)}) collective-permute-start(f32[288,128]{1,0:T(8,128)S(1)} %bitcast.17), channel_id=1, source_target_pairs={{0,8},{8,0},{16,24},{24,16},{1,9},{9,1},{17,25},{25,17},{2,10},{10... | collective-permute-start | bytes 442376 | tf_op jit(solution)/shard_map/ppermute | solution.py:610
  38.1 7.8 %collective-permute-start.14 = (f32[288,128]{1,0:T(8,128)S(1)}, f32[288,128]{1,0:T(8,128)S(1)}, u32[]{:S(2)}, u32[]{:S(2)}) collective-permute-start(f32[288,128]{1,0:T(8,128)S(1)} %bitcast.18), channel_id=1, source_target_pairs={{0,3},{1,2},{2,1},{3,0},{4,7},{5,6},{6,5},{7,4},{8,11},{9,10},{10,... | collective-permute-start | bytes 442376 | tf_op jit(solution)/shard_map/ppermute | solution.py:611

commit v3 on v2

--- a/solution.py
+++ b/solution.py
@@ -209,7 +209,7 @@
     source, refs = refs[0], refs[1:]
     halos, at = [], 0
     for count in counts:
-        halos.append([r[...] for r in refs[at : at + count]])
+        halos.append([r[:SPINOR] for r in refs[at : at + count]])
         at += count
     gauge, vectors, project, rebuild, alone, out = refs[at:]
     value = source[...]
@@ -233,7 +233,7 @@
     source, own, refs = refs[0], refs[1], refs[2:]
     halos, at = [], 0
     for count in counts:
-        halos.append([r[...] for r in refs[at : at + count]])
+        halos.append([r[:SPINOR] for r in refs[at : at + count]])
         at += count
     gauge, fine, vectors, project, rebuild, out, middle, sent, wide = refs[at:]
     spinor = own[...]
@@ -288,32 +288,40 @@
     return jnp.where(iota(x.shape, 0) // step % 2 == 0, up, down)
 
 
-def bottom_apply(v, near, image, spread, gather, held, width):
+def bottom_spread(v, spread, width):
     lane = iota(v.shape, 1)
     edge = width - NVEC2
     up = jnp.where(lane < edge, pltpu.roll(v, LANES - NVEC2, 1), pltpu.roll(v, edge, 1))
     down = jnp.where(lane >= NVEC2, pltpu.roll(v, NVEC2, 1), pltpu.roll(v, LANES - edge, 1))
     rows = jnp.concatenate([v, jnp.where(lane < width, up, 0.0), down], axis=0)
-    near[...] = table_right(rows, spread[...], 3)
+    return table_right(rows, spread[...], 3)
+
+
+def bottom_products(near, image, held, cores):
     chunks = near.shape[1] // LANES
     stride = 6 * chunks
     for c in range(chunks):
         here = pl.ds(c * LANES, LANES)
         seen = [near[i * SUB : (i + 1) * SUB, here] for i in range(6)]
         turned = [exchanged(x, 1) for x in seen]
-        for core in range(2):
+        for at, core in enumerate(cores):
             acc = [None, None]
             for n, rows in enumerate((seen, turned)):
                 beside = exchanged(rows[core], 2)
                 ways = [rows[core], beside, pltpu.roll(beside, 4, 0), rows[1 - core]]
                 ways += [rows[2 + core], rows[4 + core]]
                 for d, value in enumerate(ways):
-                    block = held[core][pl.ds(d * chunks + c, SUB, stride=stride), :]
+                    block = held[at][pl.ds(d * chunks + c, SUB, stride=stride), :]
                     got = block * value
                     acc[n] = got if acc[n] is None else acc[n] + got
-                image[(2 * n + core) * SUB : (2 * n + core + 1) * SUB, here] = acc[n]
-    total = table_right(image[...], gather[...], 3)
-    first, second = total[: 2 * SUB], total[2 * SUB :]
+                row = (n * len(cores) + at) * SUB
+                image[row : row + SUB, here] = acc[n]
+
+
+def bottom_gather(image, gather, v):
+    half = v.shape[0]
+    total = table_right(image[: 2 * half], gather[...], 3)
+    first, second = total[:half], total[half:]
     re = first - exchanged(first, 1)
     im = second + exchanged(second, 1)
     return bottom_shift * v + jnp.where(iota(v.shape, 0) % 2 == 0, re, im)
@@ -448,11 +456,7 @@
     out[...] = spinor[...] + jnp.concatenate(sum_re + sum_im, axis=0)
 
 
-def third_kernel(counts, axes, blocks, shape, received, *refs):
-    n_sites = 1 + sum(counts)
-    held, spread, gather, matrix, refs = refs[:2], refs[2], refs[3], refs[4], refs[5:]
-    vectors, refs = refs[:n_sites], refs[n_sites:]
-    middle, fine, spinor, out, near, image, wide = refs
+def start_kernel(shape, received, held, spread, gather, right, near, own, image):
     nt, nz, nx = shape
     ta, gz = lax.axis_index("ta"), lax.axis_index("gz")
     total = received.shape[0]
@@ -460,17 +464,28 @@
     line = (ta ^ (row // 2 % nt)) * nz + (gz ^ (row // SUB))
     fold = one_hot((col // (2 * nx) == line) & (col % 2 == row % 2))
     r = table_left(fold, received[...], 3)
-    apply = functools.partial(
-        bottom_apply,
-        near=near,
-        image=image,
-        spread=spread,
-        gather=gather,
-        held=held,
-        width=nx * NVEC2,
-    )
-    f = apply(r)
-    s = apply(f)
+    right[...] = r
+    near[...] = bottom_spread(r, spread, nx * NVEC2)
+    bottom_products(near, image, (held,), (0,))
+    own[...] = bottom_gather(image, gather, r[:SUB])
+
+
+def third_kernel(counts, axes, blocks, shape, right, *refs):
+    passing = pltpu.make_async_copy(refs[0], refs[-5], refs[-1])
+    passing.start()
+    refs = refs[1:-1]
+    n_sites = 1 + sum(counts)
+    first_near, own, refs = refs[0], refs[1], refs[2:]
+    held, spread, gather, matrix, refs = refs[:2], refs[2], refs[3], refs[4], refs[5:]
+    vectors, refs = refs[:n_sites], refs[n_sites:]
+    middle, fine, spinor, out, _, near, image, wide = refs
+    nx = shape[2]
+    r = right[...]
+    bottom_products(first_near, image, (held[1],), (1,))
+    f = jnp.concatenate([own[...], bottom_gather(image, gather, r[SUB:])], axis=0)
+    near[...] = bottom_spread(f, spread, nx * NVEC2)
+    bottom_products(near, image, held, (0, 1))
+    s = bottom_gather(image, gather, f)
     rows = bottom_rows(nx, minimal_residual(r, f, s))
     size = NVEC * NVEC * blocks // LANES
 
@@ -480,6 +495,7 @@
     middle_step(
         counts, axes, blocks, rows, vectors, middle, read_block, fine, spinor, out, wide
     )
+    passing.wait()
 
 
 def fourth_kernel(counts, axes, blocks, rows, *refs):
@@ -501,8 +517,8 @@
     return pl.BlockSpec(memory_space=pltpu.VMEM)
 
 
-def top(rows):
-    return pl.BlockSpec((rows, LANES), lambda i: (0, 0))
+def anywhere():
+    return pl.BlockSpec(memory_space=pl.ANY)
 
 
 def shape_of(*dims):
@@ -613,8 +629,7 @@
     residual, middle, sent = pl.pallas_call(
         functools.partial(second_kernel, counts, axes, blocks, gathered, dests),
         out_shape=(shape_of(SPINOR, LANES), shape_of(2 * NVEC, LANES), shape_of(2 * dests, LANES)),
-        grid=(1,),
-        in_specs=[vmem()] + [top(SPINOR)] * (1 + len(flat_near)) + [vmem()] * 5,
+        in_specs=[vmem()] * (7 + len(flat_near)),
         out_specs=(vmem(), vmem(), vmem()),
         scratch_shapes=[pltpu.VMEM(fine.shape, F32)],
         compiler_params=params(8),
@@ -631,19 +646,31 @@
         spread = k_lane == (lane // (NVEC2 * NVEC2) * NVEC2 + lane % NVEC2)[None]
         gather = k_lane.T == (lane // NVEC2)[:, None]
         spread, gather = jnp.asarray(spread, BF16), jnp.asarray(gather, BF16)
-        solution = pl.pallas_call(
+        right, first_near, own = pl.pallas_call(
+            functools.partial(start_kernel, shape),
+            out_shape=(
+                shape_of(2 * SUB, LANES),
+                shape_of(6 * SUB, lane.size),
+                shape_of(SUB, LANES),
+            ),
+            in_specs=[vmem()] * 4,
+            out_specs=(vmem(),) * 3,
+            scratch_shapes=[pltpu.VMEM((2 * SUB, lane.size), F32)],
+            compiler_params=params(8),
+        )(received, held[0], spread, gather)
+        solution, residual = pl.pallas_call(
             functools.partial(third_kernel, counts, axes, blocks, shape),
-            out_shape=shape_of(SPINOR, LANES),
-            grid=(1,),
-            in_specs=[vmem()] * (7 + len(flat_near)) + [vmem(), vmem(), top(SPINOR)],
-            out_specs=vmem(),
+            out_shape=(shape_of(SPINOR, LANES), shape_of(SPINOR, LANES)),
+            in_specs=[vmem()] * (13 + len(flat_near)),
+            out_specs=(vmem(), anywhere()),
             scratch_shapes=[
                 pltpu.VMEM((6 * SUB, lane.size), F32),
                 pltpu.VMEM((4 * SUB, lane.size), F32),
                 pltpu.VMEM(fine.shape, F32),
+                pltpu.SemaphoreType.DMA,
             ],
             compiler_params=params(8),
-        )(received, *held, spread, gather, matrix, mine, *near_vectors, middle, fine, spinor)
+        )(right, residual, first_near, own, *held, spread, gather, matrix, mine, *near_vectors, middle, fine, spinor)
     else:
         solved = line_solve(sent[:2, :NVEC2], bottom_blocks)
         solved = jnp.pad(solved, ((0, 0), (0, LANES - NVEC2)))
@@ -653,8 +680,7 @@
         solution = pl.pallas_call(
             functools.partial(fourth_kernel, counts, axes, blocks),
             out_shape=shape_of(SPINOR, LANES),
-            grid=(1,),
-            in_specs=[vmem()] * (3 + len(flat_near)) + [vmem(), vmem(), top(SPINOR)],
+            in_specs=[vmem()] * (6 + len(flat_near)),
             out_specs=vmem(),
             scratch_shapes=[pltpu.VMEM(fine.shape, F32)],
             compiler_params=params(16),

time: 49.5 us -> 47.6 us (0.962)
  waiting for transfers between devices: 14.7 us -> 13.3 us
  blocking collectives: 10.6 us -> 9.51 us
  starting transfers between devices: 17 us -> 17.7 us
    ppermute x1, waiting for transfers between devices: 5.01 us -> 0.01 us  [shards(): near_vectors[0] = lax.ppermute(vectors, 'ta', pairings(nt)[0])]
    ppermute x1, waiting for transfers between devices: 2.23 us -> 6.21 us  [shards(): near_vectors[-1] = lax.ppermute(vectors, 'xy', pairings(nx)[1])]
    ppermute x1, waiting for transfers between devices: 1.76 us -> 0.01 us  [shards(): beside = lax.ppermute(line, 'ta', [(i, i ^ 1) for i in range(nt)])]
    ppermute x10, waiting for transfers between devices: 5.68 us -> 7.12 us  [neighbours(): lax.ppermute(array(axis, i) if callable(array) else array, axis, p)]
    ppermute x1, starting transfers between devices: 0.07 us -> 1.16 us  [shards(): other = lax.ppermute(pair, 'ta', [(i, i ^ 2) for i in range(nt)])]
    all_to_all x1, blocking collectives: 10.6 us -> 9.51 us  [shards(): received = lax.all_to_all(sent.reshape(devices, 2, LANES), axes, 0, 0)]
    pallas_call x0 -> x1, Pallas kernels: none -> 0.68 us  [shards(): pl.pallas_call(functools.partial(start_kernel, shape), out_shape=(shape_o...]
    pallas_call x1, Pallas kernels: 3.28 us -> 2.74 us  [shards(): pl.pallas_call(functools.partial(third_kernel, counts, axes, blocks, shap...]
  transfers between devices with their start and end apart: 15 -> 15, of which waited for: 6 -> 4; matrix products, arithmetic and copies ran while one was open for 0% -> 0% of each run, Pallas kernels for 6% -> 7%
where the time goes in v3:
time: 47.6 us; the launch traced here: 47.4 us
  starting transfers between devices  17.7 us (37%)
  waiting for transfers between devices  13.3 us (28%)
  blocking collectives  9.51 us (20%)
  Pallas kernels  5.9 us (12%)
  between operations  0.78 us (2%)
    ppermute x10, starting transfers between devices, neighbours(): lax.ppermute(array(axis, i) if callable(array) else array, axis, p)  13.7 us
    all_to_all x1, blocking collectives, shards(): received = lax.all_to_all(sent.reshape(devices, 2, LANES), axes, 0, 0)  9.51 us
    ppermute x10, waiting for transfers between devices, neighbours(): lax.ppermute(array(axis, i) if callable(array) else array, axis, p)  7.12 us
    ppermute x1, waiting for transfers between devices, shards(): near_vectors[-1] = lax.ppermute(vectors, 'xy', pairings(nx)[1])  6.21 us
    pallas_call x1, Pallas kernels, shards(): pl.pallas_call(functools.partial(third_kernel, counts, axes, blocks, shap...  2.74 us
    ppermute x1, starting transfers between devices, shards(): beside = lax.ppermute(line, 'ta', [(i, i ^ 1) for i in range(nt)])  1.56 us
    pallas_call x1, Pallas kernels, shards(): pl.pallas_call(functools.partial(load_kernel, gathered), out_shape=tuple(...  1.2 us
    ppermute x1, starting transfers between devices, shards(): other = lax.ppermute(pair, 'ta', [(i, i ^ 2) for i in range(nt)])  1.16 us
  transfers between devices with their start and end apart: 15, of which 4 were waited for; matrix products, arithmetic and copies ran while one was open for 0% of the time, Pallas kernels for 7%

profile of v3, /device:TPU:0, one launch (start us, length us, event | category | flops | bytes accessed | tf_op | source)
XLA Modules:
  0.0 47.4 jit_solution(8541824580160228472)
XLA Ops:
  0.6 5.1 %collective-permute-start.4 = (f32[24,128]{1,0:T(8,128)}, f32[24,128]{1,0:T(8,128)S(1)}, u32[]{:S(2)}, u32[]{:S(2)}) collective-permute-start(f32[24,128]{1,0:T(8,128)} %bitcast.21), channel_id=1, source_target_pairs={{0,3},{1,2},{2,1},{3,0},{4,7},{5,6},{6,5},{7,4},{8,11},{9,10},{10,... | collective-permute-start | bytes 36872 | tf_op jit(solution)/shard_map/ppermute | solution.py:92
  5.8 2.4 %collective-permute-start.1 = (f32[24,128]{1,0:T(8,128)}, f32[24,128]{1,0:T(8,128)S(1)}, u32[]{:S(2)}, u32[]{:S(2)}) collective-permute-start(f32[24,128]{1,0:T(8,128)} %bitcast.24), channel_id=1, source_target_pairs={{0,24},{8,16},{16,8},{24,0},{1,25},{9,17},{17,9},{25,1},{2,26},{10... | collective-permute-start | bytes 36872 | tf_op jit(solution)/shard_map/ppermute | solution.py:92
  8.2 0.5 %collective-permute-start = (f32[24,128]{1,0:T(8,128)}, f32[24,128]{1,0:T(8,128)S(1)}, u32[]{:S(2)}, u32[]{:S(2)}) collective-permute-start(f32[24,128]{1,0:T(8,128)} %bitcast.25), channel_id=1, source_target_pairs={{0,8},{8,0},{16,24},{24,16},{1,9},{9,1},{17,25},{25,17},{2,10},{10... | collective-permute-start | bytes 36872 | tf_op jit(solution)/shard_map/ppermute | solution.py:92
  8.8 1.2 %shard_map.113 = (f32[24,128]{1,0:T(8,128)S(1)}, f32[144,128]{1,0:T(8,128)S(1)}, bf16[576,128]{1,0:T(8,128)(2,1)S(1)}, bf16[96,192]{1,0:T(8,128)(2,1)S(1)}, bf16...) custom-call(f32[24,128]{1,0:T(8,128)} %bitcast.26, f32[144,128]{1,0:T(8,128)} %bitcast.20, ...), custom_call_target="tpu_custom_call" | custom-call | tf_op jit(solution)/shard_map/pallas_call | solution.py:599
  10.0 0.0 copy-start
  10.0 0.0 copy-start.1
  10.0 1.6 %collective-permute-start.10 = (f32[216,128]{1,0:T(8,128)S(1)}, f32[216,128]{1,0:T(8,128)S(1)}, u32[]{:S(2)}, u32[]{:S(2)}) collective-permute-start(f32[216,128]{1,0:T(8,128)S(1)} %get-tuple-element.31), channel_id=1, source_target_pairs={{0,8},{8,0},{16,24},{24,16},{1,9},{9,1},{17,25},{25,17},{2,10},{10... | collective-permute-start | bytes 331784 | tf_op jit(solution)/shard_map/ppermute | solution.py:610
  11.6 0.5 %collective-permute-done.refs_1_ = f32[24,128]{1,0:T(8,128)S(1)} collective-permute-done((f32[24,128]{1,0:T(8,128)}, f32[24,128]{1,0:T(8,128)S(1)}, u32[]{:S(2)}, u32[]{:S(2)}) %collective-permute-start) | collective-permute-done | bytes 12320 | tf_op jit(solution)/shard_map/ppermute | solution.py:92
  12.1 0.4 shard_map.114
  12.6 2.1 %collective-permute-start.8 = (f32[312,128]{1,0:T(8,128)S(1)}, f32[312,128]{1,0:T(8,128)S(1)}, u32[]{:S(2)}, u32[]{:S(2)}) collective-permute-start(f32[312,128]{1,0:T(8,128)S(1)} %get-tuple-element.28), channel_id=1, source_target_pairs={{0,1},{1,0},{2,3},{3,2},{4,5},{5,4},{6,7},{7,6},{8,9},{9,8},{10,11... | collective-permute-start | bytes 479240 | tf_op jit(solution)/shard_map/ppermute | solution.py:92
  14.6 0.9 %collective-permute-start.6 = (f32[312,128]{1,0:T(8,128)S(1)}, f32[312,128]{1,0:T(8,128)S(1)}, u32[]{:S(2)}, u32[]{:S(2)}) collective-permute-start(f32[312,128]{1,0:T(8,128)S(1)} %get-tuple-element.28), channel_id=1, source_target_pairs={{0,24},{8,16},{16,8},{24,0},{1,25},{9,17},{17,9},{25,1},{2,26},{10... | collective-permute-start | bytes 479240 | tf_op jit(solution)/shard_map/ppermute | solution.py:92
  15.6 1.2 %collective-permute-start.11 = (f32[432,128]{1,0:T(8,128)S(1)}, f32[432,128]{1,0:T(8,128)S(1)}, u32[]{:S(2)}, u32[]{:S(2)}) collective-permute-start(f32[432,128]{1,0:T(8,128)S(1)} %constant_dynamic-update-slice_fusion), channel_id=1, source_target_pairs={{0,16},{8,24},{16,0},{24,8},{1,17},{9,25},{17,1},{25,9},{2,18},{10... | collective-permute-start | bytes 663560 | tf_op jit(solution)/shard_map/ppermute | solution.py:625
  16.7 1.1 %collective-permute-start.9 = (f32[24,128]{1,0:T(8,128)S(1)}, f32[24,128]{1,0:T(8,128)S(1)}, u32[]{:S(2)}, u32[]{:S(2)}) collective-permute-start(f32[24,128]{1,0:T(8,128)S(1)} %get-tuple-element.27.refs_1_.refs_16_), channel_id=1, source_target_pairs={{0,3},{1,2},{2,1},{3,0},{4,7},{5,6},{6,5},{7,4},{8,11},{9,10},{10,... | collective-permute-start | bytes 36872 | tf_op jit(solution)/shard_map/ppermute | solution.py:92
  17.8 4.4 %collective-permute-done.9.refs_6_ = f32[24,128]{1,0:T(8,128)S(1)} collective-permute-done((f32[24,128]{1,0:T(8,128)S(1)}, f32[24,128]{1,0:T(8,128)S(1)}, u32[]{:S(2)}, u32[]{:S(2)}) %collective-permute-start.9) | collective-permute-done | bytes 12320 | tf_op jit(solution)/shard_map/ppermute | solution.py:92
  22.2 1.5 %collective-permute-start.5 = (f32[24,128]{1,0:T(8,128)S(1)}, f32[24,128]{1,0:T(8,128)S(1)}, u32[]{:S(2)}, u32[]{:S(2)}) collective-permute-start(f32[24,128]{1,0:T(8,128)S(1)} %get-tuple-element.27.refs_1_.refs_16_), channel_id=1, source_target_pairs={{0,8},{8,0},{16,24},{24,16},{1,9},{9,1},{17,25},{25,17},{2,10},{10... | collective-permute-start | bytes 36872 | tf_op jit(solution)/shard_map/ppermute | solution.py:92
  23.7 2.2 %collective-permute-done.5.refs_2_ = f32[24,128]{1,0:T(8,128)S(1)} collective-permute-done((f32[24,128]{1,0:T(8,128)S(1)}, f32[24,128]{1,0:T(8,128)S(1)}, u32[]{:S(2)}, u32[]{:S(2)}) %collective-permute-start.5) | collective-permute-done | bytes 12320 | tf_op jit(solution)/shard_map/ppermute | solution.py:92
  25.9 0.9 %shard_map.115 = (f32[24,128]{1,0:T(8,128)S(1)}, f32[48,128]{1,0:T(8,128)S(1)}, f32[64,128]{1,0:T(8,128)S(1)}) custom-call(f32[24,128]{1,0:T(8,128)S(1)} %get-tuple-element.22.refs_0_, f32[24,128]{1,0:T(8,128)S(1)} %get-tuple-element.27.refs_1_.refs_16_, f32[24,128]{1,0:T(8,128)S(1)} %collective-permute-done.5.refs_2_, ...), custom_call_target="tpu_custom_call" | custom-call | tf_op jit(solution)/shard_map/pallas_call | solution.py:629
  26.8 9.5 %all_to_all.5 = f32[32,2,128]{2,1,0:T(2,128)S(1)} all-to-all(f32[32,2,128]{2,1,0:T(2,128)S(1)} %bitcast.14), channel_id=1, replica_groups=mesh['ta'=4,'gz'=2,'xy'=4] {'ta','gz','xy'}, dimensions={0} | all-to-all | bytes 65536 | tf_op jit(solution)/shard_map/all_to_all | solution.py:639
  36.4 0.1 collective-permute-start.12
  36.5 0.6 %collective-permute-start.14 = (f32[288,128]{1,0:T(8,128)S(1)}, f32[288,128]{1,0:T(8,128)S(1)}, u32[]{:S(2)}, u32[]{:S(2)}) collective-permute-start(f32[288,128]{1,0:T(8,128)S(1)} %bitcast.17), channel_id=1, source_target_pairs={{0,3},{1,2},{2,1},{3,0},{4,7},{5,6},{6,5},{7,4},{8,11},{9,10},{10,... | collective-permute-start | bytes 442376 | tf_op jit(solution)/shard_map/ppermute | solution.py:627
  37.1 0.6 %collective-permute-start.13 = (f32[288,128]{1,0:T(8,128)S(1)}, f32[288,128]{1,0:T(8,128)S(1)}, u32[]{:S(2)}, u32[]{:S(2)}) collective-permute-start(f32[288,128]{1,0:T(8,128)S(1)} %bitcast.18), channel_id=1, source_target_pairs={{0,8},{8,0},{16,24},{24,16},{1,9},{9,1},{17,25},{25,17},{2,10},{10... | collective-permute-start | bytes 442376 | tf_op jit(solution)/shard_map/ppermute | solution.py:626
  37.7 0.7 %shard_map.116 = (f32[16,128]{1,0:T(8,128)S(1)}, f32[48,2304]{1,0:T(8,128)S(1)}, f32[8,128]{1,0:T(8,128)S(1)}) custom-call(f32[64,128]{1,0:T(8,128)S(1)} %bitcast.13, f32[864,128]{1,0:T(8,128)S(1)} %constant_dynamic-update-slice_fusion.2.held.refs_3_, bf16[128,2304]{1,0:T(8,128)(2,1)S(1)} %copy-done.1, bf16[2304,128]{1,0:T(8,128)(2,1)S(1)} %copy-done), custom_call_target="tpu_custom_call" | custom-call | tf_op jit(solution)/shard_map/pallas_call | solution.py:649
  38.4 6.2 %collective-permute-done.14.refs_13_ = f32[288,128]{1,0:T(8,128)S(1)} collective-permute-done((f32[288,128]{1,0:T(8,128)S(1)}, f32[288,128]{1,0:T(8,128)S(1)}, u32[]{:S(2)}, u32[]{:S(2)}) %collective-permute-start.14) | collective-permute-done | bytes 147488 | tf_op jit(solution)/shard_map/ppermute | solution.py:627
  44.6 2.7 %shard_map.117 = (f32[24,128]{1,0:T(8,128)}, f32[24,128]{1,0:T(8,128)}) custom-call(f32[16,128]{1,0:T(8,128)S(1)} %get-tuple-element.35.right, f32[24,128]{1,0:T(8,128)S(1)} %get-tuple-element.36.refs_0_, f32[48,2304]{1,0:T(8,128)S(1)} %get-tuple-element.37.refs_1_, f32[8,128]{1,0:T(8,128)S(1)} %get-tuple-element.38.refs_2_, ...), custom_call_target="tpu_custom_call" | custom-call | tf_op jit(solution)/shard_map/pallas_call | solution.py:661
  (24 shorter events, 0.1 us)
Async XLA Ops:
  0.6 9.3 %collective-permute-start.4 = (f32[24,128]{1,0:T(8,128)}, f32[24,128]{1,0:T(8,128)S(1)}, u32[]{:S(2)}, u32[]{:S(2)}) collective-permute-start(f32[24,128]{1,0:T(8,128)} %bitcast.21), channel_id=1, source_target_pairs={{0,3},{1,2},{2,1},{3,0},{4,7},{5,6},{6,5},{7,4},{8,11},{9,10},{10,... | collective-permute-start | bytes 36872 | tf_op jit(solution)/shard_map/ppermute | solution.py:92
  5.8 5.8 %collective-permute-start.3 = (f32[24,128]{1,0:T(8,128)}, f32[24,128]{1,0:T(8,128)S(1)}, u32[]{:S(2)}, u32[]{:S(2)}) collective-permute-start(f32[24,128]{1,0:T(8,128)} %bitcast.22), channel_id=1, source_target_pairs={{0,1},{1,0},{2,3},{3,2},{4,5},{5,4},{6,7},{7,6},{8,9},{9,8},{10,11... | collective-permute-start | bytes 36872 | tf_op jit(solution)/shard_map/ppermute | solution.py:92
  5.8 5.8 %collective-permute-start.2 = (f32[24,128]{1,0:T(8,128)}, f32[24,128]{1,0:T(8,128)S(1)}, u32[]{:S(2)}, u32[]{:S(2)}) collective-permute-start(f32[24,128]{1,0:T(8,128)} %bitcast.23), channel_id=1, source_target_pairs={{0,4},{4,0},{1,5},{5,1},{2,6},{6,2},{3,7},{7,3},{8,12},{12,8},{9,1... | collective-permute-start | bytes 36872 | tf_op jit(solution)/shard_map/ppermute | solution.py:92
  5.8 5.8 %collective-permute-start.1 = (f32[24,128]{1,0:T(8,128)}, f32[24,128]{1,0:T(8,128)S(1)}, u32[]{:S(2)}, u32[]{:S(2)}) collective-permute-start(f32[24,128]{1,0:T(8,128)} %bitcast.24), channel_id=1, source_target_pairs={{0,24},{8,16},{16,8},{24,0},{1,25},{9,17},{17,9},{25,1},{2,26},{10... | collective-permute-start | bytes 36872 | tf_op jit(solution)/shard_map/ppermute | solution.py:92
  8.2 3.9 %collective-permute-start = (f32[24,128]{1,0:T(8,128)}, f32[24,128]{1,0:T(8,128)S(1)}, u32[]{:S(2)}, u32[]{:S(2)}) collective-permute-start(f32[24,128]{1,0:T(8,128)} %bitcast.25), channel_id=1, source_target_pairs={{0,8},{8,0},{16,24},{24,16},{1,9},{9,1},{17,25},{25,17},{2,10},{10... | collective-permute-start | bytes 36872 | tf_op jit(solution)/shard_map/ppermute | solution.py:92
  10.0 26.5 %copy-start.3 = (f32[2,24,1,1,1,768]{5,4,3,2,1,0:T(1,128)S(1)}, f32[2,24,1,1,1,768]{5,4,3,2,1,0:T(1,128)}, u32[]{:S(2)}) copy-start(f32[2,24,1,1,1,768]{5,4,3,2,1,0:T(1,128)} %param.14) | copy-start | bytes 442372
  10.0 27.7 %copy-start = (bf16[2304,128]{1,0:T(8,128)(2,1)S(1)}, bf16[2304,128]{1,0:T(8,128)(2,1)}, u32[]{:S(2)}) copy-start(bf16[2304,128]{1,0:T(8,128)(2,1)} %constant.11.clone.gather.refs_6_) | copy-start | bytes 1769476
  10.0 27.7 %copy-start.1 = (bf16[128,2304]{1,0:T(8,128)(2,1)S(1)}, bf16[128,2304]{1,0:T(8,128)(2,1)}, u32[]{:S(2)}) copy-start(bf16[128,2304]{1,0:T(8,128)(2,1)} %constant.10.clone.spread.refs_5_) | copy-start | bytes 1769476
  10.0 5.5 %collective-permute-start.10 = (f32[216,128]{1,0:T(8,128)S(1)}, f32[216,128]{1,0:T(8,128)S(1)}, u32[]{:S(2)}, u32[]{:S(2)}) collective-permute-start(f32[216,128]{1,0:T(8,128)S(1)} %get-tuple-element.31), channel_id=1, source_target_pairs={{0,8},{8,0},{16,24},{24,16},{1,9},{9,1},{17,25},{25,17},{2,10},{10... | collective-permute-start | bytes 331784 | tf_op jit(solution)/shard_map/ppermute | solution.py:610
  12.6 13.4 %collective-permute-start.8 = (f32[312,128]{1,0:T(8,128)S(1)}, f32[312,128]{1,0:T(8,128)S(1)}, u32[]{:S(2)}, u32[]{:S(2)}) collective-permute-start(f32[312,128]{1,0:T(8,128)S(1)} %get-tuple-element.28), channel_id=1, source_target_pairs={{0,1},{1,0},{2,3},{3,2},{4,5},{5,4},{6,7},{7,6},{8,9},{9,8},{10,11... | collective-permute-start | bytes 479240 | tf_op jit(solution)/shard_map/ppermute | solution.py:92
  14.6 11.3 %collective-permute-start.7 = (f32[312,128]{1,0:T(8,128)S(1)}, f32[312,128]{1,0:T(8,128)S(1)}, u32[]{:S(2)}, u32[]{:S(2)}) collective-permute-start(f32[312,128]{1,0:T(8,128)S(1)} %get-tuple-element.28), channel_id=1, source_target_pairs={{0,4},{4,0},{1,5},{5,1},{2,6},{6,2},{3,7},{7,3},{8,12},{12,8},{9,1... | collective-permute-start | bytes 479240 | tf_op jit(solution)/shard_map/ppermute | solution.py:92
  14.6 11.3 %collective-permute-start.6 = (f32[312,128]{1,0:T(8,128)S(1)}, f32[312,128]{1,0:T(8,128)S(1)}, u32[]{:S(2)}, u32[]{:S(2)}) collective-permute-start(f32[312,128]{1,0:T(8,128)S(1)} %get-tuple-element.28), channel_id=1, source_target_pairs={{0,24},{8,16},{16,8},{24,0},{1,25},{9,17},{17,9},{25,1},{2,26},{10... | collective-permute-start | bytes 479240 | tf_op jit(solution)/shard_map/ppermute | solution.py:92
  15.6 20.8 %collective-permute-start.11 = (f32[432,128]{1,0:T(8,128)S(1)}, f32[432,128]{1,0:T(8,128)S(1)}, u32[]{:S(2)}, u32[]{:S(2)}) collective-permute-start(f32[432,128]{1,0:T(8,128)S(1)} %constant_dynamic-update-slice_fusion), channel_id=1, source_target_pairs={{0,16},{8,24},{16,0},{24,8},{1,17},{9,25},{17,1},{25,9},{2,18},{10... | collective-permute-start | bytes 663560 | tf_op jit(solution)/shard_map/ppermute | solution.py:625
  16.7 5.5 %collective-permute-start.9 = (f32[24,128]{1,0:T(8,128)S(1)}, f32[24,128]{1,0:T(8,128)S(1)}, u32[]{:S(2)}, u32[]{:S(2)}) collective-permute-start(f32[24,128]{1,0:T(8,128)S(1)} %get-tuple-element.27.refs_1_.refs_16_), channel_id=1, source_target_pairs={{0,3},{1,2},{2,1},{3,0},{4,7},{5,6},{6,5},{7,4},{8,11},{9,10},{10,... | collective-permute-start | bytes 36872 | tf_op jit(solution)/shard_map/ppermute | solution.py:92
  22.2 3.7 %collective-permute-start.5 = (f32[24,128]{1,0:T(8,128)S(1)}, f32[24,128]{1,0:T(8,128)S(1)}, u32[]{:S(2)}, u32[]{:S(2)}) collective-permute-start(f32[24,128]{1,0:T(8,128)S(1)} %get-tuple-element.27.refs_1_.refs_16_), channel_id=1, source_target_pairs={{0,8},{8,0},{16,24},{24,16},{1,9},{9,1},{17,25},{25,17},{2,10},{10... | collective-permute-start | bytes 36872 | tf_op jit(solution)/shard_map/ppermute | solution.py:92
  26.8 17.8 %copy-start.2 = (f32[2,9,24,1,1,1,768]{6,5,4,3,2,1,0:T(1,128)S(1)}, f32[2,9,24,1,1,1,768]{6,5,4,3,2,1,0:T(1,128)}, u32[]{:S(2)}) copy-start(f32[2,9,24,1,1,1,768]{6,5,4,3,2,1,0:T(1,128)} %param.13) | copy-start | bytes 3981316
  36.4 8.2 %collective-permute-start.12 = (f32[864,128]{1,0:T(8,128)S(1)}, f32[864,128]{1,0:T(8,128)S(1)}, u32[]{:S(2)}, u32[]{:S(2)}) collective-permute-start(f32[864,128]{1,0:T(8,128)S(1)} %constant_dynamic-update-slice_fusion.2.held.refs_3_), channel_id=1, source_target_pairs={{0,4},{4,0},{1,5},{5,1},{2,6},{6,2},{3,7},{7,3},{8,12},{12,8},{9,1... | collective-permute-start | bytes 1327112 | tf_op jit(solution)/shard_map/ppermute | solution.py:643
  36.5 8.1 %collective-permute-start.14 = (f32[288,128]{1,0:T(8,128)S(1)}, f32[288,128]{1,0:T(8,128)S(1)}, u32[]{:S(2)}, u32[]{:S(2)}) collective-permute-start(f32[288,128]{1,0:T(8,128)S(1)} %bitcast.17), channel_id=1, source_target_pairs={{0,3},{1,2},{2,1},{3,0},{4,7},{5,6},{6,5},{7,4},{8,11},{9,10},{10,... | collective-permute-start | bytes 442376 | tf_op jit(solution)/shard_map/ppermute | solution.py:627
  37.1 7.5 %collective-permute-start.13 = (f32[288,128]{1,0:T(8,128)S(1)}, f32[288,128]{1,0:T(8,128)S(1)}, u32[]{:S(2)}, u32[]{:S(2)}) collective-permute-start(f32[288,128]{1,0:T(8,128)S(1)} %bitcast.18), channel_id=1, source_target_pairs={{0,8},{8,0},{16,24},{24,16},{1,9},{9,1},{17,25},{25,17},{2,10},{10... | collective-permute-start | bytes 442376 | tf_op jit(solution)/shard_map/ppermute | solution.py:626

commit v4 on v3

--- a/solution.py
+++ b/solution.py
@@ -165,10 +165,9 @@
     return sum(out[i * m : (i + 1) * m] for i in range(count))
 
 
-def product(a, b):
+def product(a, b_high, b_low):
     m = a.shape[0]
     a_high, a_low = parts(a, 2)
-    b_high, b_low = parts(b, 2)
     out = jnp.dot(jnp.concatenate([a_high, a_low], axis=0), b_high, preferred_element_type=F32)
     return out[:m] + out[m:] + jnp.dot(a_high, b_low, preferred_element_type=F32)
 
@@ -229,7 +228,7 @@
     return [fine[pl.ds(p * NVEC * HALF + row, NVEC, stride=HALF), :] for p in range(2)]
 
 
-def second_kernel(counts, axes, blocks, place, dests, *refs):
+def second_kernel(counts, axes, blocks, together, *refs):
     source, own, refs = refs[0], refs[1], refs[2:]
     halos, at = [], 0
     for count in counts:
@@ -269,14 +268,16 @@
         made_im.append(re * pat_im - im * pat_re)
     made = jnp.concatenate(made_re + made_im, axis=0)
     summed = table_right(made, jnp.ones((LANES, LANES), BF16))
-    shift = lax.axis_index("xy") * NVEC2 if place else 0
-    home = iota((size, LANES), 1) == iota((size, LANES), 0) // count + shift
-    line = [
-        jnp.sum(jnp.where(home, summed[p * size : (p + 1) * size], 0.0), axis=0, keepdims=True)
-        for p in range(2)
-    ]
-    both = jnp.where(iota((SUB, LANES), 0) % 2 == 0, line[0], line[1])
-    for i in range(2 * dests // SUB):
+    line = []
+    for p in range(2):
+        home = iota((size, LANES), 0) // count + (p * NVEC2 if together else 0)
+        kept = jnp.where(iota((size, LANES), 1) == home, summed[p * size : (p + 1) * size], 0.0)
+        line.append(jnp.sum(kept, axis=0, keepdims=True))
+    if together:
+        both = jnp.broadcast_to(line[0] + line[1], (SUB, LANES))
+    else:
+        both = jnp.where(iota((SUB, LANES), 0) % 2 == 0, line[0], line[1])
+    for i in range(sent.shape[0] // SUB):
         sent[i * SUB : (i + 1) * SUB] = both
 
 
@@ -284,6 +285,8 @@
     rows = x.shape[0]
     if rows == 2 * step:
         return pltpu.roll(x, step, 0)
+    if rows == SUB:
+        return jnp.take_along_axis(x, iota(x.shape, 0) ^ step, axis=0)
     up, down = pltpu.roll(x, rows - step, 0), pltpu.roll(x, step, 0)
     return jnp.where(iota(x.shape, 0) // step % 2 == 0, up, down)
 
@@ -373,7 +376,15 @@
     return jnp.where(iota(result.shape, 1) < NVEC2, result, 0.0)
 
 
-def middle_step(counts, axes, blocks, rows, vectors, middle, read_block, fine, spinor, out, wide):
+def vector_parts(ref, size):
+    skip = ref.shape[0] - 2 * size
+    both = jnp.concatenate(
+        [ref[skip : skip + size], ref[skip + size : skip + 2 * size]], axis=1
+    )
+    return parts(both, 2)
+
+
+def middle_step(counts, axes, blocks, rows, pairs, middle, read_block, wide, spinor, out):
     per = LANES // blocks
     count = NVEC // per
     size = NVEC2 * count
@@ -384,16 +395,12 @@
     coefs = table_right(rows, spread, 3)
     same = iota((NVEC, size), 1) % count == iota((NVEC, size), 0) % count
     guesses = []
-    for n, ref in enumerate(vectors):
-        skip = ref.shape[0] - 2 * size
-        wide_vectors = jnp.concatenate(
-            [ref[skip : skip + size], ref[skip + size : skip + 2 * size]], axis=1
-        )
+    for n, pair in enumerate(pairs):
         left = jnp.concatenate(
             [jnp.where(same, coefs[2 * n + q : 2 * n + q + 1, :size], 0.0) for q in range(2)],
             axis=0,
         )
-        made = product(left, wide_vectors)
+        made = product(left, *pair)
         guesses.append(
             jnp.concatenate(
                 [
@@ -447,7 +454,6 @@
     lift = one_hot(iota((LANES, LANES), 0) == iota((LANES, LANES), 1) // BY)
     lifted = jnp.dot(update.astype(BF16), lift, preferred_element_type=F32)
     u_re, u_im = lifted[:NVEC], lifted[NVEC:]
-    wide[...] = fine[...].astype(F32)
     sum_re, sum_im = [], []
     for i in range(HALF):
         re, im = strided_vectors(wide, i)
@@ -459,11 +465,17 @@
 def start_kernel(shape, received, held, spread, gather, right, near, own, image):
     nt, nz, nx = shape
     ta, gz = lax.axis_index("ta"), lax.axis_index("gz")
-    total = received.shape[0]
-    row, col = iota((2 * SUB, total), 0), iota((2 * SUB, total), 1)
-    line = (ta ^ (row // 2 % nt)) * nz + (gz ^ (row // SUB))
-    fold = one_hot((col // (2 * nx) == line) & (col % 2 == row % 2))
-    r = table_left(fold, received[...], 3)
+    total, rows = received.shape[0], 2 * SUB
+    row, col = iota((nx * rows, total), 0), iota((nx * rows, total), 1)
+    line = (ta ^ (row % rows // 2 % nt)) * nz + (gz ^ (row % rows // SUB))
+    fold = one_hot(col == line * nx + row // rows)
+    found = table_left(fold, received[...], 3)
+    lane, part = iota((rows, LANES), 1), iota((rows, LANES), 0) % 2
+    r = jnp.zeros((rows, LANES), F32)
+    for x in range(nx):
+        block = found[x * rows : (x + 1) * rows]
+        turned = [pltpu.roll(block, ((x - q) * NVEC2) % LANES, 1) for q in range(2)]
+        r = jnp.where(lane // NVEC2 == x, jnp.where(part == 0, turned[0], turned[1]), r)
     right[...] = r
     near[...] = bottom_spread(r, spread, nx * NVEC2)
     bottom_products(near, image, (held,), (0,))
@@ -479,6 +491,7 @@
     held, spread, gather, matrix, refs = refs[:2], refs[2], refs[3], refs[4], refs[5:]
     vectors, refs = refs[:n_sites], refs[n_sites:]
     middle, fine, spinor, out, _, near, image, wide = refs
+    wide[...] = fine[...].astype(F32)
     nx = shape[2]
     r = right[...]
     bottom_products(first_near, image, (held[1],), (1,))
@@ -492,9 +505,8 @@
     def read_block(p, d, block):
         return matrix[pl.ds((p * 9 + d) * size + block * NVEC, NVEC), :]
 
-    middle_step(
-        counts, axes, blocks, rows, vectors, middle, read_block, fine, spinor, out, wide
-    )
+    pairs = [vector_parts(ref, NVEC2 * NVEC * blocks // LANES) for ref in vectors]
+    middle_step(counts, axes, blocks, rows, pairs, middle, read_block, wide, spinor, out)
     passing.wait()
 
 
@@ -508,9 +520,9 @@
     def read_block(p, d, block):
         return matrix[pl.ds((p * 9 + d) * size + block * NVEC, NVEC), :]
 
-    middle_step(
-        counts, axes, blocks, rows[...], vectors, middle, read_block, fine, spinor, out, wide
-    )
+    wide[...] = fine[...].astype(F32)
+    pairs = [vector_parts(ref, NVEC2 * NVEC * blocks // LANES) for ref in vectors]
+    middle_step(counts, axes, blocks, rows[...], pairs, middle, read_block, wide, spinor, out)
 
 
 def vmem():
@@ -627,8 +639,12 @@
         near_vectors[-1] = lax.ppermute(vectors, "xy", pairings(nx)[1])
     dests = devices if gathered else SUB
     residual, middle, sent = pl.pallas_call(
-        functools.partial(second_kernel, counts, axes, blocks, gathered, dests),
-        out_shape=(shape_of(SPINOR, LANES), shape_of(2 * NVEC, LANES), shape_of(2 * dests, LANES)),
+        functools.partial(second_kernel, counts, axes, blocks, gathered),
+        out_shape=(
+            shape_of(SPINOR, LANES),
+            shape_of(2 * NVEC, LANES),
+            shape_of(dests, LANES),
+        ),
         in_specs=[vmem()] * (7 + len(flat_near)),
         out_specs=(vmem(), vmem(), vmem()),
         scratch_shapes=[pltpu.VMEM(fine.shape, F32)],
@@ -636,8 +652,8 @@
     )(source, spinor, *flat_near, gauge, fine, mine, project, rebuild)
 
     if gathered:
-        received = lax.all_to_all(sent.reshape(devices, 2, LANES), axes, 0, 0)
-        received = received.reshape(2 * devices, LANES)
+        received = lax.all_to_all(sent.reshape(devices, 1, LANES), axes, 0, 0)
+        received = received.reshape(devices, LANES)
         received, pair, other = lax.optimization_barrier((received, pair, other))
         held = jnp.concatenate([pair, other])
         held = [held, lax.ppermute(held, "gz", pairings(nz)[0])]

time: 47.6 us -> 54.7 us (1.15)
  waiting for transfers between devices: 13.3 us -> 17.7 us
  starting transfers between devices: 17.7 us -> 19.4 us
  blocking collectives: 9.51 us -> 10.7 us
    ppermute x1, waiting for transfers between devices: 0.01 us -> 3.05 us  [shards(): beside = lax.ppermute(line, 'ta', [(i, i ^ 1) for i in range(nt)])]
    ppermute x1, starting transfers between devices: 1.56 us -> 3.03 us  [shards(): beside = lax.ppermute(line, 'ta', [(i, i ^ 1) for i in range(nt)])]
    ppermute x10, waiting for transfers between devices: 7.12 us -> 8.45 us  [neighbours(): lax.ppermute(array(axis, i) if callable(array) else array, axis, p)]
    all_to_all x1, blocking collectives: 9.51 us -> 10.7 us  [shards(): received = lax.all_to_all(sent.reshape(devices, 1, LANES), axes, 0, 0)]
    ppermute x1, starting transfers between devices: 1.16 us -> 1.83 us  [shards(): other = lax.ppermute(pair, 'ta', [(i, i ^ 2) for i in range(nt)])]
  transfers between devices with their start and end apart: 15 -> 15, of which waited for: 4 -> 8; matrix products, arithmetic and copies ran while one was open for 0% -> 0% of each run, Pallas kernels for 7% -> 4%
where the time goes in v4:
time: 54.7 us; the launch traced here: 54.5 us
  starting transfers between devices  19.4 us (35%)
  waiting for transfers between devices  17.7 us (32%)
  blocking collectives  10.7 us (20%)
  Pallas kernels  5.91 us (11%)
  between operations  0.74 us (1%)
    ppermute x10, starting transfers between devices, neighbours(): lax.ppermute(array(axis, i) if callable(array) else array, axis, p)  13.3 us
    all_to_all x1, blocking collectives, shards(): received = lax.all_to_all(sent.reshape(devices, 1, LANES), axes, 0, 0)  10.7 us
    ppermute x10, waiting for transfers between devices, neighbours(): lax.ppermute(array(axis, i) if callable(array) else array, axis, p)  8.45 us
    ppermute x1, waiting for transfers between devices, shards(): near_vectors[-1] = lax.ppermute(vectors, 'xy', pairings(nx)[1])  6.15 us
    ppermute x1, waiting for transfers between devices, shards(): beside = lax.ppermute(line, 'ta', [(i, i ^ 1) for i in range(nt)])  3.05 us
    ppermute x1, starting transfers between devices, shards(): beside = lax.ppermute(line, 'ta', [(i, i ^ 1) for i in range(nt)])  3.03 us
    pallas_call x1, Pallas kernels, shards(): pl.pallas_call(functools.partial(third_kernel, counts, axes, blocks, shap...  2.66 us
    ppermute x1, starting transfers between devices, shards(): other = lax.ppermute(pair, 'ta', [(i, i ^ 2) for i in range(nt)])  1.83 us
  transfers between devices with their start and end apart: 15, of which 8 were waited for; matrix products, arithmetic and copies ran while one was open for 0% of the time, Pallas kernels for 4%

profile of v4, /device:TPU:0, one launch (start us, length us, event | category | flops | bytes accessed | tf_op | source)
XLA Modules:
  0.0 54.5 jit_solution(10800539638633377796)
XLA Ops:
  0.6 1.2 %shard_map.113 = (f32[24,128]{1,0:T(8,128)S(1)}, f32[144,128]{1,0:T(8,128)S(1)}, bf16[576,128]{1,0:T(8,128)(2,1)S(1)}, bf16[96,192]{1,0:T(8,128)(2,1)S(1)}, bf16...) custom-call(f32[24,128]{1,0:T(8,128)} %bitcast.23, f32[144,128]{1,0:T(8,128)} %bitcast.22, ...), custom_call_target="tpu_custom_call" | custom-call | tf_op jit(solution)/shard_map/pallas_call | solution.py:611
  1.9 3.0 %collective-permute-start.10 = (f32[216,128]{1,0:T(8,128)S(1)}, f32[216,128]{1,0:T(8,128)S(1)}, u32[]{:S(2)}, u32[]{:S(2)}) collective-permute-start(f32[216,128]{1,0:T(8,128)S(1)} %get-tuple-element.31), channel_id=1, source_target_pairs={{0,8},{8,0},{16,24},{24,16},{1,9},{9,1},{17,25},{25,17},{2,10},{10... | collective-permute-start | bytes 331784 | tf_op jit(solution)/shard_map/ppermute | solution.py:622
  4.9 3.0 %collective-permute-done.10 = f32[216,128]{1,0:T(8,128)S(1)} collective-permute-done((f32[216,128]{1,0:T(8,128)S(1)}, f32[216,128]{1,0:T(8,128)S(1)}, u32[]{:S(2)}, u32[]{:S(2)}) %collective-permute-start.10) | collective-permute-done | bytes 110624 | tf_op jit(solution)/shard_map/ppermute | solution.py:622
  8.0 1.8 %collective-permute-start.11 = (f32[432,128]{1,0:T(8,128)S(1)}, f32[432,128]{1,0:T(8,128)S(1)}, u32[]{:S(2)}, u32[]{:S(2)}) collective-permute-start(f32[432,128]{1,0:T(8,128)S(1)} %constant_dynamic-update-slice_fusion), channel_id=1, source_target_pairs={{0,16},{8,24},{16,0},{24,8},{1,17},{9,25},{17,1},{25,9},{2,18},{10... | collective-permute-start | bytes 663560 | tf_op jit(solution)/shard_map/ppermute | solution.py:637
  9.8 3.6 %collective-permute-start.4 = (f32[24,128]{1,0:T(8,128)}, f32[24,128]{1,0:T(8,128)S(1)}, u32[]{:S(2)}, u32[]{:S(2)}) collective-permute-start(f32[24,128]{1,0:T(8,128)} %bitcast.24), channel_id=1, source_target_pairs={{0,3},{1,2},{2,1},{3,0},{4,7},{5,6},{6,5},{7,4},{8,11},{9,10},{10,... | collective-permute-start | bytes 36872 | tf_op jit(solution)/shard_map/ppermute | solution.py:92
  13.4 1.4 %collective-permute-start.1 = (f32[24,128]{1,0:T(8,128)}, f32[24,128]{1,0:T(8,128)S(1)}, u32[]{:S(2)}, u32[]{:S(2)}) collective-permute-start(f32[24,128]{1,0:T(8,128)} %bitcast.27), channel_id=1, source_target_pairs={{0,24},{8,16},{16,8},{24,0},{1,25},{9,17},{17,9},{25,1},{2,26},{10... | collective-permute-start | bytes 36872 | tf_op jit(solution)/shard_map/ppermute | solution.py:92
  14.9 0.7 %collective-permute-done.4.refs_5_ = f32[24,128]{1,0:T(8,128)S(1)} collective-permute-done((f32[24,128]{1,0:T(8,128)}, f32[24,128]{1,0:T(8,128)S(1)}, u32[]{:S(2)}, u32[]{:S(2)}) %collective-permute-start.4) | collective-permute-done | bytes 12320 | tf_op jit(solution)/shard_map/ppermute | solution.py:92
  15.5 1.5 %collective-permute-start = (f32[24,128]{1,0:T(8,128)}, f32[24,128]{1,0:T(8,128)S(1)}, u32[]{:S(2)}, u32[]{:S(2)}) collective-permute-start(f32[24,128]{1,0:T(8,128)} %bitcast.28), channel_id=1, source_target_pairs={{0,8},{8,0},{16,24},{24,16},{1,9},{9,1},{17,25},{25,17},{2,10},{10... | collective-permute-start | bytes 36872 | tf_op jit(solution)/shard_map/ppermute | solution.py:92
  17.3 0.9 %collective-permute-done.1.refs_2_ = f32[24,128]{1,0:T(8,128)S(1)} collective-permute-done((f32[24,128]{1,0:T(8,128)}, f32[24,128]{1,0:T(8,128)S(1)}, u32[]{:S(2)}, u32[]{:S(2)}) %collective-permute-start.1) | collective-permute-done | bytes 12320 | tf_op jit(solution)/shard_map/ppermute | solution.py:92
  18.2 1.2 %collective-permute-done.refs_1_ = f32[24,128]{1,0:T(8,128)S(1)} collective-permute-done((f32[24,128]{1,0:T(8,128)}, f32[24,128]{1,0:T(8,128)S(1)}, u32[]{:S(2)}, u32[]{:S(2)}) %collective-permute-start) | collective-permute-done | bytes 12320 | tf_op jit(solution)/shard_map/ppermute | solution.py:92
  19.4 0.4 shard_map.114
  19.8 1.4 %collective-permute-start.8 = (f32[312,128]{1,0:T(8,128)S(1)}, f32[312,128]{1,0:T(8,128)S(1)}, u32[]{:S(2)}, u32[]{:S(2)}) collective-permute-start(f32[312,128]{1,0:T(8,128)S(1)} %get-tuple-element.28), channel_id=1, source_target_pairs={{0,1},{1,0},{2,3},{3,2},{4,5},{5,4},{6,7},{7,6},{8,9},{9,8},{10,11... | collective-permute-start | bytes 479240 | tf_op jit(solution)/shard_map/ppermute | solution.py:92
  21.3 1.5 %collective-permute-start.6 = (f32[312,128]{1,0:T(8,128)S(1)}, f32[312,128]{1,0:T(8,128)S(1)}, u32[]{:S(2)}, u32[]{:S(2)}) collective-permute-start(f32[312,128]{1,0:T(8,128)S(1)} %get-tuple-element.28), channel_id=1, source_target_pairs={{0,24},{8,16},{16,8},{24,0},{1,25},{9,17},{17,9},{25,1},{2,26},{10... | collective-permute-start | bytes 479240 | tf_op jit(solution)/shard_map/ppermute | solution.py:92
  22.8 2.3 %collective-permute-start.9 = (f32[24,128]{1,0:T(8,128)S(1)}, f32[24,128]{1,0:T(8,128)S(1)}, u32[]{:S(2)}, u32[]{:S(2)}) collective-permute-start(f32[24,128]{1,0:T(8,128)S(1)} %get-tuple-element.27.refs_1_.refs_16_), channel_id=1, source_target_pairs={{0,3},{1,2},{2,1},{3,0},{4,7},{5,6},{6,5},{7,4},{8,11},{9,10},{10,... | collective-permute-start | bytes 36872 | tf_op jit(solution)/shard_map/ppermute | solution.py:92
  25.1 3.2 %collective-permute-done.9.refs_6_ = f32[24,128]{1,0:T(8,128)S(1)} collective-permute-done((f32[24,128]{1,0:T(8,128)S(1)}, f32[24,128]{1,0:T(8,128)S(1)}, u32[]{:S(2)}, u32[]{:S(2)}) %collective-permute-start.9) | collective-permute-done | bytes 12320 | tf_op jit(solution)/shard_map/ppermute | solution.py:92
  28.3 1.5 %collective-permute-start.5 = (f32[24,128]{1,0:T(8,128)S(1)}, f32[24,128]{1,0:T(8,128)S(1)}, u32[]{:S(2)}, u32[]{:S(2)}) collective-permute-start(f32[24,128]{1,0:T(8,128)S(1)} %get-tuple-element.27.refs_1_.refs_16_), channel_id=1, source_target_pairs={{0,8},{8,0},{16,24},{24,16},{1,9},{9,1},{17,25},{25,17},{2,10},{10... | collective-permute-start | bytes 36872 | tf_op jit(solution)/shard_map/ppermute | solution.py:92
  29.7 2.2 %collective-permute-done.5.refs_2_ = f32[24,128]{1,0:T(8,128)S(1)} collective-permute-done((f32[24,128]{1,0:T(8,128)S(1)}, f32[24,128]{1,0:T(8,128)S(1)}, u32[]{:S(2)}, u32[]{:S(2)}) %collective-permute-start.5) | collective-permute-done | bytes 12320 | tf_op jit(solution)/shard_map/ppermute | solution.py:92
  32.0 0.9 %shard_map.115 = (f32[24,128]{1,0:T(8,128)S(1)}, f32[48,128]{1,0:T(8,128)S(1)}, f32[32,128]{1,0:T(8,128)S(1)}) custom-call(f32[24,128]{1,0:T(8,128)S(1)} %get-tuple-element.22.refs_0_, f32[24,128]{1,0:T(8,128)S(1)} %get-tuple-element.27.refs_1_.refs_16_, f32[24,128]{1,0:T(8,128)S(1)} %collective-permute-done.5.refs_2_, ...), custom_call_target="tpu_custom_call" | custom-call | tf_op jit(solution)/shard_map/pallas_call | solution.py:641
  32.8 10.7 %all_to_all.5 = f32[32,1,128]{2,1,0:T(1,128)S(1)} all-to-all(f32[32,1,128]{2,1,0:T(1,128)S(1)} %bitcast.16), channel_id=1, replica_groups=mesh['ta'=4,'gz'=2,'xy'=4] {'ta','gz','xy'}, dimensions={0} | all-to-all | bytes 32768 | tf_op jit(solution)/shard_map/all_to_all | solution.py:655
  43.6 0.6 %collective-permute-start.14 = (f32[288,128]{1,0:T(8,128)S(1)}, f32[288,128]{1,0:T(8,128)S(1)}, u32[]{:S(2)}, u32[]{:S(2)}) collective-permute-start(f32[288,128]{1,0:T(8,128)S(1)} %bitcast.19), channel_id=1, source_target_pairs={{0,3},{1,2},{2,1},{3,0},{4,7},{5,6},{6,5},{7,4},{8,11},{9,10},{10,... | collective-permute-start | bytes 442376 | tf_op jit(solution)/shard_map/ppermute | solution.py:639
  44.3 0.6 %collective-permute-start.13 = (f32[288,128]{1,0:T(8,128)S(1)}, f32[288,128]{1,0:T(8,128)S(1)}, u32[]{:S(2)}, u32[]{:S(2)}) collective-permute-start(f32[288,128]{1,0:T(8,128)S(1)} %bitcast.20), channel_id=1, source_target_pairs={{0,8},{8,0},{16,24},{24,16},{1,9},{9,1},{17,25},{25,17},{2,10},{10... | collective-permute-start | bytes 442376 | tf_op jit(solution)/shard_map/ppermute | solution.py:638
  44.9 0.8 %shard_map.116 = (f32[16,128]{1,0:T(8,128)S(1)}, f32[48,2304]{1,0:T(8,128)S(1)}, f32[8,128]{1,0:T(8,128)S(1)}) custom-call(f32[32,128]{1,0:T(8,128)S(1)} %bitcast.15, f32[864,128]{1,0:T(8,128)S(1)} %constant_dynamic-update-slice_fusion.2.held.refs_3_, bf16[128,2304]{1,0:T(8,128)(2,1)S(1)} %copy-done.1, bf16[2304,128]{1,0:T(8,128)(2,1)S(1)} %copy-done), custom_call_target="tpu_custom_call" | custom-call | tf_op jit(solution)/shard_map/pallas_call | solution.py:665
  45.6 6.2 %collective-permute-done.14.refs_13_ = f32[288,128]{1,0:T(8,128)S(1)} collective-permute-done((f32[288,128]{1,0:T(8,128)S(1)}, f32[288,128]{1,0:T(8,128)S(1)}, u32[]{:S(2)}, u32[]{:S(2)}) %collective-permute-start.14) | collective-permute-done | bytes 147488 | tf_op jit(solution)/shard_map/ppermute | solution.py:639
  51.8 2.7 %shard_map.117 = (f32[24,128]{1,0:T(8,128)}, f32[24,128]{1,0:T(8,128)}) custom-call(f32[16,128]{1,0:T(8,128)S(1)} %get-tuple-element.35.right, f32[24,128]{1,0:T(8,128)S(1)} %get-tuple-element.36.refs_0_, f32[48,2304]{1,0:T(8,128)S(1)} %get-tuple-element.37.refs_1_, f32[8,128]{1,0:T(8,128)S(1)} %get-tuple-element.38.refs_2_, ...), custom_call_target="tpu_custom_call" | custom-call | tf_op jit(solution)/shard_map/pallas_call | solution.py:677
  (24 shorter events, 0.5 us)
Async XLA Ops:
  1.8 41.8 %copy-start.3 = (f32[2,24,1,1,1,768]{5,4,3,2,1,0:T(1,128)S(1)}, f32[2,24,1,1,1,768]{5,4,3,2,1,0:T(1,128)}, u32[]{:S(2)}) copy-start(f32[2,24,1,1,1,768]{5,4,3,2,1,0:T(1,128)} %param.14) | copy-start | bytes 442372
  1.9 43.0 %copy-start = (bf16[2304,128]{1,0:T(8,128)(2,1)S(1)}, bf16[2304,128]{1,0:T(8,128)(2,1)}, u32[]{:S(2)}) copy-start(bf16[2304,128]{1,0:T(8,128)(2,1)} %constant.11.clone.gather.refs_6_) | copy-start | bytes 1769476
  1.9 43.0 %copy-start.1 = (bf16[128,2304]{1,0:T(8,128)(2,1)S(1)}, bf16[128,2304]{1,0:T(8,128)(2,1)}, u32[]{:S(2)}) copy-start(bf16[128,2304]{1,0:T(8,128)(2,1)} %constant.10.clone.spread.refs_5_) | copy-start | bytes 1769476
  1.9 6.1 %collective-permute-start.10 = (f32[216,128]{1,0:T(8,128)S(1)}, f32[216,128]{1,0:T(8,128)S(1)}, u32[]{:S(2)}, u32[]{:S(2)}) collective-permute-start(f32[216,128]{1,0:T(8,128)S(1)} %get-tuple-element.31), channel_id=1, source_target_pairs={{0,8},{8,0},{16,24},{24,16},{1,9},{9,1},{17,25},{25,17},{2,10},{10... | collective-permute-start | bytes 331784 | tf_op jit(solution)/shard_map/ppermute | solution.py:622
  8.0 35.5 %collective-permute-start.11 = (f32[432,128]{1,0:T(8,128)S(1)}, f32[432,128]{1,0:T(8,128)S(1)}, u32[]{:S(2)}, u32[]{:S(2)}) collective-permute-start(f32[432,128]{1,0:T(8,128)S(1)} %constant_dynamic-update-slice_fusion), channel_id=1, source_target_pairs={{0,16},{8,24},{16,0},{24,8},{1,17},{9,25},{17,1},{25,9},{2,18},{10... | collective-permute-start | bytes 663560 | tf_op jit(solution)/shard_map/ppermute | solution.py:637
  9.8 5.7 %collective-permute-start.4 = (f32[24,128]{1,0:T(8,128)}, f32[24,128]{1,0:T(8,128)S(1)}, u32[]{:S(2)}, u32[]{:S(2)}) collective-permute-start(f32[24,128]{1,0:T(8,128)} %bitcast.24), channel_id=1, source_target_pairs={{0,3},{1,2},{2,1},{3,0},{4,7},{5,6},{6,5},{7,4},{8,11},{9,10},{10,... | collective-permute-start | bytes 36872 | tf_op jit(solution)/shard_map/ppermute | solution.py:92
  13.4 3.9 %collective-permute-start.3 = (f32[24,128]{1,0:T(8,128)}, f32[24,128]{1,0:T(8,128)S(1)}, u32[]{:S(2)}, u32[]{:S(2)}) collective-permute-start(f32[24,128]{1,0:T(8,128)} %bitcast.25), channel_id=1, source_target_pairs={{0,1},{1,0},{2,3},{3,2},{4,5},{5,4},{6,7},{7,6},{8,9},{9,8},{10,11... | collective-permute-start | bytes 36872 | tf_op jit(solution)/shard_map/ppermute | solution.py:92
  13.4 3.9 %collective-permute-start.2 = (f32[24,128]{1,0:T(8,128)}, f32[24,128]{1,0:T(8,128)S(1)}, u32[]{:S(2)}, u32[]{:S(2)}) collective-permute-start(f32[24,128]{1,0:T(8,128)} %bitcast.26), channel_id=1, source_target_pairs={{0,4},{4,0},{1,5},{5,1},{2,6},{6,2},{3,7},{7,3},{8,12},{12,8},{9,1... | collective-permute-start | bytes 36872 | tf_op jit(solution)/shard_map/ppermute | solution.py:92
  13.4 4.8 %collective-permute-start.1 = (f32[24,128]{1,0:T(8,128)}, f32[24,128]{1,0:T(8,128)S(1)}, u32[]{:S(2)}, u32[]{:S(2)}) collective-permute-start(f32[24,128]{1,0:T(8,128)} %bitcast.27), channel_id=1, source_target_pairs={{0,24},{8,16},{16,8},{24,0},{1,25},{9,17},{17,9},{25,1},{2,26},{10... | collective-permute-start | bytes 36872 | tf_op jit(solution)/shard_map/ppermute | solution.py:92
  15.5 3.9 %collective-permute-start = (f32[24,128]{1,0:T(8,128)}, f32[24,128]{1,0:T(8,128)S(1)}, u32[]{:S(2)}, u32[]{:S(2)}) collective-permute-start(f32[24,128]{1,0:T(8,128)} %bitcast.28), channel_id=1, source_target_pairs={{0,8},{8,0},{16,24},{24,16},{1,9},{9,1},{17,25},{25,17},{2,10},{10... | collective-permute-start | bytes 36872 | tf_op jit(solution)/shard_map/ppermute | solution.py:92
  19.8 12.1 %collective-permute-start.8 = (f32[312,128]{1,0:T(8,128)S(1)}, f32[312,128]{1,0:T(8,128)S(1)}, u32[]{:S(2)}, u32[]{:S(2)}) collective-permute-start(f32[312,128]{1,0:T(8,128)S(1)} %get-tuple-element.28), channel_id=1, source_target_pairs={{0,1},{1,0},{2,3},{3,2},{4,5},{5,4},{6,7},{7,6},{8,9},{9,8},{10,11... | collective-permute-start | bytes 479240 | tf_op jit(solution)/shard_map/ppermute | solution.py:92
  21.3 10.7 %collective-permute-start.7 = (f32[312,128]{1,0:T(8,128)S(1)}, f32[312,128]{1,0:T(8,128)S(1)}, u32[]{:S(2)}, u32[]{:S(2)}) collective-permute-start(f32[312,128]{1,0:T(8,128)S(1)} %get-tuple-element.28), channel_id=1, source_target_pairs={{0,4},{4,0},{1,5},{5,1},{2,6},{6,2},{3,7},{7,3},{8,12},{12,8},{9,1... | collective-permute-start | bytes 479240 | tf_op jit(solution)/shard_map/ppermute | solution.py:92
  21.3 10.7 %collective-permute-start.6 = (f32[312,128]{1,0:T(8,128)S(1)}, f32[312,128]{1,0:T(8,128)S(1)}, u32[]{:S(2)}, u32[]{:S(2)}) collective-permute-start(f32[312,128]{1,0:T(8,128)S(1)} %get-tuple-element.28), channel_id=1, source_target_pairs={{0,24},{8,16},{16,8},{24,0},{1,25},{9,17},{17,9},{25,1},{2,26},{10... | collective-permute-start | bytes 479240 | tf_op jit(solution)/shard_map/ppermute | solution.py:92
  22.8 5.5 %collective-permute-start.9 = (f32[24,128]{1,0:T(8,128)S(1)}, f32[24,128]{1,0:T(8,128)S(1)}, u32[]{:S(2)}, u32[]{:S(2)}) collective-permute-start(f32[24,128]{1,0:T(8,128)S(1)} %get-tuple-element.27.refs_1_.refs_16_), channel_id=1, source_target_pairs={{0,3},{1,2},{2,1},{3,0},{4,7},{5,6},{6,5},{7,4},{8,11},{9,10},{10,... | collective-permute-start | bytes 36872 | tf_op jit(solution)/shard_map/ppermute | solution.py:92
  28.3 3.7 %collective-permute-start.5 = (f32[24,128]{1,0:T(8,128)S(1)}, f32[24,128]{1,0:T(8,128)S(1)}, u32[]{:S(2)}, u32[]{:S(2)}) collective-permute-start(f32[24,128]{1,0:T(8,128)S(1)} %get-tuple-element.27.refs_1_.refs_16_), channel_id=1, source_target_pairs={{0,8},{8,0},{16,24},{24,16},{1,9},{9,1},{17,25},{25,17},{2,10},{10... | collective-permute-start | bytes 36872 | tf_op jit(solution)/shard_map/ppermute | solution.py:92
  32.8 19.0 %copy-start.2 = (f32[2,9,24,1,1,1,768]{6,5,4,3,2,1,0:T(1,128)S(1)}, f32[2,9,24,1,1,1,768]{6,5,4,3,2,1,0:T(1,128)}, u32[]{:S(2)}) copy-start(f32[2,9,24,1,1,1,768]{6,5,4,3,2,1,0:T(1,128)} %param.13) | copy-start | bytes 3981316
  43.6 8.2 %collective-permute-start.12 = (f32[864,128]{1,0:T(8,128)S(1)}, f32[864,128]{1,0:T(8,128)S(1)}, u32[]{:S(2)}, u32[]{:S(2)}) collective-permute-start(f32[864,128]{1,0:T(8,128)S(1)} %constant_dynamic-update-slice_fusion.2.held.refs_3_), channel_id=1, source_target_pairs={{0,4},{4,0},{1,5},{5,1},{2,6},{6,2},{3,7},{7,3},{8,12},{12,8},{9,1... | collective-permute-start | bytes 1327112 | tf_op jit(solution)/shard_map/ppermute | solution.py:659
  43.6 8.1 %collective-permute-start.14 = (f32[288,128]{1,0:T(8,128)S(1)}, f32[288,128]{1,0:T(8,128)S(1)}, u32[]{:S(2)}, u32[]{:S(2)}) collective-permute-start(f32[288,128]{1,0:T(8,128)S(1)} %bitcast.19), channel_id=1, source_target_pairs={{0,3},{1,2},{2,1},{3,0},{4,7},{5,6},{6,5},{7,4},{8,11},{9,10},{10,... | collective-permute-start | bytes 442376 | tf_op jit(solution)/shard_map/ppermute | solution.py:639
  44.3 7.5 %collective-permute-start.13 = (f32[288,128]{1,0:T(8,128)S(1)}, f32[288,128]{1,0:T(8,128)S(1)}, u32[]{:S(2)}, u32[]{:S(2)}) collective-permute-start(f32[288,128]{1,0:T(8,128)S(1)} %bitcast.20), channel_id=1, source_target_pairs={{0,8},{8,0},{16,24},{24,16},{1,9},{9,1},{17,25},{25,17},{2,10},{10... | collective-permute-start | bytes 442376 | tf_op jit(solution)/shard_map/ppermute | solution.py:638
